TPU v7x, 32 devices: a whole 2x2x4 slice. The times are simulated.
32 devices in a mesh: dp: 4 (over z), ctx: 2 (over x), tp: 4 (over y, core).
Axes of the slice: x: 2, y: 2, z: 4, core: 2. Of those that a mesh axis runs over, the one named last changes fastest.
Arguments:
- tokens: bfloat16 [4096, 2048], P(('dp', 'ctx')), may hold values from -6 to 6
- segments: int32 [4, 1024], P('dp'), may hold values from 0 to 3, never falling along the last dimension, each value on 1 to 512 neighbouring positions
- attn_gain: float32 [2048], replicated, may hold values from 0.5 to 1.5
- query_weight: bfloat16 [2048, 2048], P(None, 'tp'), may hold values from -0.125 to 0.125
- key_weight: bfloat16 [2048, 256], P(None, 'tp'), may hold values from -0.125 to 0.125
- value_weight: bfloat16 [2048, 256], P(None, 'tp'), may hold values from -0.125 to 0.125
- output_weight: bfloat16 [2048, 2048], P('tp'), may hold values from -2 to 2
- mlp_gain: float32 [2048], replicated, may hold values from 0.5 to 1.5
- gate_weight: bfloat16 [2048, 5632], P(None, 'tp'), may hold values from -0.125 to 0.125
- up_weight: bfloat16 [2048, 5632], P(None, 'tp'), may hold values from -0.125 to 0.125
- down_weight: bfloat16 [5632, 2048], P('tp'), may hold values from -0.078125 to 0.078125
- cotangent: bfloat16 [4096, 2048], P(('dp', 'ctx')), may hold values from -6 to 6
Outputs:
- layer_out: float32 [4096, 2048], P(('dp', 'ctx'))
- tokens_grad: float32 [4096, 2048], P(('dp', 'ctx'))
- attn_gain_grad: float32 [2048], P(('dp', 'ctx'))
- query_grad: float32 [2048, 2048], P(('dp', 'ctx'), 'tp')
- key_grad: float32 [2048, 256], P(('dp', 'ctx'), 'tp')
- value_grad: float32 [2048, 256], P(('dp', 'ctx'), 'tp')
- output_grad: float32 [2048, 2048], P('tp', ('dp', 'ctx'))
- mlp_gain_grad: float32 [2048], P(('dp', 'ctx'))
- gate_grad: float32 [2048, 5632], P(('dp', 'ctx'), 'tp')
- up_grad: float32 [2048, 5632], P(('dp', 'ctx'), 'tp')
- down_grad: float32 [5632, 2048], P('tp', ('dp', 'ctx'))
Inputs may be any that keep to these rules, and one draw needn't show every extreme that they name: `segments`: along each packed sequence the document numbers never fall; a document has 1 to 512 tokens, and one document of each sequence has exactly 512.
All inputs are finite; a program needn't handle non-finite values.
Results may differ from a plain program's by a relative error of at most 0.013.
Values may be sent and summed in bfloat16 or wider, within the bound.
A program may use at most 192 MiB of HBM per device.

v0:
```python
import functools

import jax
import jax.numpy as jnp
from jax import lax
from jax.experimental import pallas as pl
from jax.experimental.pallas import tpu as pltpu
from jax.sharding import PartitionSpec as P

HEAD = 64
EPSILON = 1e-05
MASKED = -1000000000.0
BF = jnp.bfloat16
F32 = jnp.float32
QB = 128


def contract(left_side, right_side, left_dim, right_dim):
    return lax.dot_general(
        left_side,
        right_side,
        (((left_dim,), (right_dim,)), ((), ())),
        preferred_element_type=F32,
    )


def swap(value, axis, mask):
    size = lax.axis_size(axis)
    return lax.ppermute(value, axis, [(i, i ^ mask) for i in range(size)])


def bits_of(axis):
    return [(axis, 1 << k) for k in range((lax.axis_size(axis) - 1).bit_length())]


def rope_tables(positions, head_width):
    frequency = 10000.0 ** (-jnp.arange(0, head_width, 2, dtype=F32) / head_width)
    angles = positions.astype(F32)[:, None] * frequency[None, :]
    cos_half, sin_half = jnp.cos(angles), jnp.sin(angles)
    return (
        jnp.concatenate([cos_half] * 4, -1),
        jnp.concatenate([sin_half] * 4, -1),
    )


def lane_index(shape):
    return lax.broadcasted_iota(jnp.int32, shape, len(shape) - 1)


def turn(values):
    low = lane_index(values.shape) % HEAD < HEAD // 2
    width = values.shape[-1]
    return jnp.where(
        low, -pltpu.roll(values, width - HEAD // 2, 1), pltpu.roll(values, HEAD // 2, 1)
    )


def enter_kernel(x_ref, gain_ref, wq_ref, wkv_ref, cos_ref, sin_ref, a_ref, q_ref, kv_ref):
    x = x_ref[...].astype(F32)
    inverse = lax.rsqrt(jnp.mean(x * x, axis=-1, keepdims=True) + EPSILON)
    a = (x * inverse * gain_ref[...]).astype(BF)
    a_ref[...] = a
    cos, sin = cos_ref[...], sin_ref[...]
    pairs = q_ref.shape[1] // 128
    q = jnp.dot(a, wq_ref[...], preferred_element_type=F32)
    cos_all = jnp.concatenate([cos] * pairs, -1)
    sin_all = jnp.concatenate([sin] * pairs, -1)
    q_rot = (q * cos_all + turn(q) * sin_all).astype(BF)
    q_ref[...] = q_rot * (HEAD**-0.5)
    kv = jnp.dot(a, wkv_ref[...], preferred_element_type=F32)
    is_key = lane_index(kv.shape) < HEAD
    kv_ref[...] = jnp.where(is_key, kv * cos + turn(kv) * sin, kv).astype(BF)


def enter(tokens, gain, wq, wkv, cos, sin):
    rows, d = tokens.shape
    tile = 128
    row = lambda i: (i, 0)
    fixed = lambda i: (0, 0)
    return pl.pallas_call(
        enter_kernel,
        grid=(rows // tile,),
        in_specs=[
            pl.BlockSpec((tile, d), row),
            pl.BlockSpec((1, d), fixed),
            pl.BlockSpec(wq.shape, fixed),
            pl.BlockSpec(wkv.shape, fixed),
            pl.BlockSpec((tile, 128), row),
            pl.BlockSpec((tile, 128), row),
        ],
        out_specs=[
            pl.BlockSpec((tile, d), row),
            pl.BlockSpec((tile, wq.shape[1]), row),
            pl.BlockSpec((tile, 128), row),
        ],
        out_shape=[
            jax.ShapeDtypeStruct((rows, d), BF),
            jax.ShapeDtypeStruct((rows, wq.shape[1]), BF),
            jax.ShapeDtypeStruct((rows, 128), BF),
        ],
        name="enter",
    )(tokens, gain, wq, wkv, cos, sin)


def lay_keys(ctx, kv_ref, k_refs, v_refs):
    count, rows, _ = kv_ref.shape
    for j in range(count):
        kv = kv_ref[j].astype(F32)
        other = pltpu.roll(kv, HEAD, 1)
        low = lane_index(kv.shape) < HEAD
        at = pl.ds(pl.multiple_of((ctx ^ j) * rows, rows), rows)
        k_refs[0][at, :] = jnp.where(low, kv, 0.0).astype(BF)
        k_refs[1][at, :] = jnp.where(low, 0.0, other).astype(BF)
        v_refs[0][at, :] = jnp.where(low, other, 0.0).astype(BF)
        v_refs[1][at, :] = jnp.where(low, 0.0, kv).astype(BF)


def mask_of(ctx, block, rows, window, segc_ref, segr_ref, pairs):
    first_q = ctx * rows + block * QB
    start = pl.multiple_of(jnp.maximum(first_q + QB - window, 0), QB)
    key_seg = segc_ref[pl.ds(start, window), :]
    query_seg = segr_ref[:, pl.ds(pl.multiple_of(first_q, QB), QB)]
    key_pos = start + lax.broadcasted_iota(jnp.int32, (window, QB), 0)
    query_pos = first_q + lax.broadcasted_iota(jnp.int32, (window, QB), 1)
    bias = jnp.where((key_seg == query_seg) & (key_pos <= query_pos), 0.0, MASKED)
    return start, jnp.concatenate([bias] * pairs, -1)


def stack_pairs(ref, at, pairs):
    return jnp.concatenate([ref[at, 128 * g : 128 * (g + 1)] for g in range(pairs)], 0)


def forward_kernel(q_ref, kv_ref, segc_ref, segr_ref, o_ref, lse_ref, k0, k1, v0, v1, *, window):
    rows = q_ref.shape[0]
    pairs = q_ref.shape[1] // 128
    ctx = lax.axis_index("ctx")
    k_refs, v_refs = (k0, k1), (v0, v1)
    lay_keys(ctx, kv_ref, k_refs, v_refs)

    def body(block, carry):
        start, bias = mask_of(ctx, block, rows, window, segc_ref, segr_ref, pairs)
        at = pl.ds(pl.multiple_of(block * QB, QB), QB)
        keys_at = pl.ds(start, window)
        queries = stack_pairs(q_ref, at, pairs)
        mixed = None
        for parity in range(2):
            scores = contract(k_refs[parity][keys_at, :], queries, 1, 1) + bias
            top = jnp.max(scores, axis=0, keepdims=True)
            weights = jnp.exp(scores - top)
            total = jnp.sum(weights, axis=0, keepdims=True)
            lse_ref[pl.ds(block * 2 + parity, 1), :] = top + jnp.log(total)
            part = contract(v_refs[parity][keys_at, :], weights.astype(BF), 0, 0) / total
            mixed = part if mixed is None else mixed + part
        mixed = mixed.T.astype(BF)
        for g in range(pairs):
            o_ref[at, 128 * g : 128 * (g + 1)] = mixed[QB * g : QB * (g + 1), :]
        return carry

    lax.fori_loop(0, rows // QB, body, 0)


def attend(q, kv, seg_col, seg_row, window):
    rows, width = q.shape
    count = kv.shape[0]
    pairs = width // 128
    return pl.pallas_call(
        functools.partial(forward_kernel, window=window),
        out_shape=[
            jax.ShapeDtypeStruct((rows, width), BF),
            jax.ShapeDtypeStruct((rows // QB * 2, QB * pairs), F32),
        ],
        in_specs=[pl.BlockSpec(memory_space=pltpu.VMEM)] * 4,
        out_specs=[pl.BlockSpec(memory_space=pltpu.VMEM)] * 2,
        scratch_shapes=[pltpu.VMEM((count * rows, 128), BF)] * 4,
        name="attend",
    )(q, kv, seg_col, seg_row)


def backward_kernel(
    q_ref,
    hb_ref,
    kv_ref,
    lse_ref,
    segc_ref,
    segr_ref,
    cos_ref,
    sin_ref,
    qb_ref,
    own_ref,
    far_ref,
    k0,
    k1,
    v0,
    v1,
    dk,
    dv,
    *,
    window,
):
    rows = q_ref.shape[0]
    pairs = q_ref.shape[1] // 128
    count = kv_ref.shape[0]
    ctx = lax.axis_index("ctx")
    core = lax.rem(lax.axis_index("tp"), 2)
    k_refs, v_refs = (k0, k1), (v0, v1)
    lay_keys(ctx, kv_ref, k_refs, v_refs)
    dk[...] = jnp.zeros_like(dk)
    dv[...] = jnp.zeros_like(dv)
    half_blocks = rows // QB // 2

    def body(block, carry):
        start, bias = mask_of(ctx, block, rows, window, segc_ref, segr_ref, pairs)
        at = pl.ds(pl.multiple_of(block * QB, QB), QB)
        keys_at = pl.ds(start, window)
        queries = stack_pairs(q_ref, at, pairs)
        swapped = lax.rem(block + core * half_blocks, 2 * half_blocks)
        backs = stack_pairs(hb_ref, pl.ds(pl.multiple_of(swapped * QB, QB), QB), pairs)
        low = lane_index(queries.shape) < HEAD
        zero = jnp.zeros_like(queries)
        dq = None
        for parity in range(2):
            keep = low if parity == 0 else jnp.logical_not(low)
            keys = k_refs[parity][keys_at, :]
            scores = contract(keys, queries, 1, 1) + bias
            weights = jnp.exp(scores - lse_ref[pl.ds(block * 2 + parity, 1), :])
            back = contract(v_refs[parity][keys_at, :], backs, 1, 1)
            delta = jnp.sum(weights * back, axis=0, keepdims=True)
            score_back = (weights * (back - delta)).astype(BF)
            part = contract(keys, score_back, 0, 0)
            dq = part if dq is None else dq + part
            dk[keys_at, :] += contract(score_back, jnp.where(keep, queries, zero), 1, 0)
            dv[keys_at, :] += contract(weights.astype(BF), jnp.where(keep, backs, zero), 1, 0)
        dq = dq.T * (HEAD**-0.5)
        cos, sin = cos_ref[at, :], sin_ref[at, :]
        for g in range(pairs):
            piece = dq[QB * g : QB * (g + 1), :]
            qb_ref[at, 128 * g : 128 * (g + 1)] = (piece * cos - turn(piece * sin)).astype(BF)
        return carry

    lax.fori_loop(0, rows // QB, body, 0)
    for j in range(count):
        at = pl.ds(pl.multiple_of((ctx ^ j) * rows, rows), rows)
        a, b = dk[at, :], dv[at, :]
        low = lane_index(a.shape) < HEAD
        both = jnp.where(low, a + pltpu.roll(a, HEAD, 1), b + pltpu.roll(b, HEAD, 1))
        if j == 0:
            own_ref[...] = both
        else:
            far_ref[j - 1] = both.astype(BF)


def attend_back(q, hb, kv, lse, seg_col, seg_row, cos, sin, window):
    rows, width = q.shape
    count = kv.shape[0]
    return pl.pallas_call(
        functools.partial(backward_kernel, window=window),
        out_shape=[
            jax.ShapeDtypeStruct((rows, width), BF),
            jax.ShapeDtypeStruct((rows, 128), F32),
            jax.ShapeDtypeStruct((count - 1, rows, 128), BF),
        ],
        in_specs=[pl.BlockSpec(memory_space=pltpu.VMEM)] * 8,
        out_specs=[pl.BlockSpec(memory_space=pltpu.VMEM)] * 3,
        scratch_shapes=[pltpu.VMEM((count * rows, 128), BF)] * 4
        + [pltpu.VMEM((count * rows, 128), F32)] * 2,
        name="attend_back",
    )(q, hb, kv, lse, seg_col, seg_row, cos, sin)


def join_kernel(*refs):
    own_ref, cos_ref, sin_ref = refs[0], refs[-3], refs[-2]
    out_ref = refs[-1]
    total = own_ref[...]
    for ref in refs[1:-3]:
        total = total + ref[...].astype(F32)
    is_key = lane_index(total.shape) < HEAD
    turned = total * cos_ref[...] - turn(total * sin_ref[...])
    out_ref[...] = jnp.where(is_key, turned, total).astype(BF)


def join_keys(own, far, cos, sin):
    return pl.pallas_call(
        join_kernel,
        out_shape=jax.ShapeDtypeStruct(own.shape, BF),
        name="join_keys",
    )(own, *far, cos, sin)


STEP = 256


def gated(m, cot, wg, wu, wd):
    gate = contract(m, wg, 1, 0)
    up = contract(m, wu, 1, 0)
    back = contract(cot, wd, 1, 1)
    sig = 0.5 * jnp.tanh(0.5 * gate) + 0.5
    silu = gate * sig
    return (
        (silu * up).astype(BF),
        (back * up * (sig + silu * (1.0 - sig))).astype(BF),
        (back * silu).astype(BF),
    )


def own_kernel(
    m_ref,
    c_ref,
    wg_hbm,
    wu_hbm,
    wd_hbm,
    h_ref,
    gb_ref,
    ub_ref,
    send_ref,
    keep_ref,
    wg_ref,
    wu_ref,
    wd_ref,
    sems,
    *,
    tile,
):
    rows, d = m_ref.shape
    half = rows // 2
    width = wg_ref.shape[1]
    full, tail = divmod(width, STEP)

    def span(c, w):
        return pl.ds(c * STEP if isinstance(c, int) else pl.multiple_of(c * STEP, STEP), w)

    def copies(c, w):
        at = span(c, w)
        return [
            pltpu.make_async_copy(wg_hbm.at[:, at], wg_ref.at[:, at], sems.at[0, c]),
            pltpu.make_async_copy(wu_hbm.at[:, at], wu_ref.at[:, at], sems.at[1, c]),
            pltpu.make_async_copy(wd_hbm.at[at, :], wd_ref.at[at, :], sems.at[2, c]),
        ]

    for c in range(full + (1 if tail else 0)):
        for copy in copies(c, STEP if c < full else tail):
            copy.start()

    def chunk(c, w):
        for copy in copies(c, w):
            copy.wait()
        at = span(c, w)
        wg, wu, wd = wg_ref[:, at], wu_ref[:, at], wd_ref[at, :]
        for t in range(rows // tile):
            r = slice(t * tile, (t + 1) * tile)
            h, gb, ub = gated(m_ref[r, :], c_ref[r, :], wg, wu, wd)
            h_ref[r, at] = h
            gb_ref[r, at] = gb
            ub_ref[r, at] = ub

    def chunk_step(c, carry):
        chunk(c, STEP)
        return carry

    lax.fori_loop(0, full, chunk_step, 0)
    if tail:
        chunk(full, tail)

    def back_step(i, carry):
        at = span(i, STEP)
        wg, wu = wg_ref[at, :], wu_ref[at, :]
        for t in range(rows // tile):
            r = slice(t * tile, (t + 1) * tile)
            part = contract(gb_ref[r, :], wg, 1, 1) + contract(ub_ref[r, :], wu, 1, 1)
            if t * tile < half:
                keep_ref[r, at] = part
            else:
                send_ref[t * tile - half : (t + 1) * tile - half, at] = part.astype(BF)
        return carry

    lax.fori_loop(0, d // STEP, back_step, 0)


def own_rows(m, cot, wg, wu, wd):
    rows, d = m.shape
    width = wg.shape[1]
    out = jax.ShapeDtypeStruct((rows, width), BF)
    vmem = pl.BlockSpec(memory_space=pltpu.VMEM)
    hbm = pl.BlockSpec(memory_space=pl.ANY)
    return pl.pallas_call(
        functools.partial(own_kernel, tile=256),
        in_specs=[vmem, vmem, hbm, hbm, hbm],
        out_specs=[vmem] * 5,
        out_shape=[out] * 3
        + [jax.ShapeDtypeStruct((rows // 2, d), BF), jax.ShapeDtypeStruct((rows // 2, d), F32)],
        scratch_shapes=[pltpu.VMEM((d, width), BF)] * 2
        + [pltpu.VMEM((width, d), BF), pltpu.SemaphoreType.DMA((3, pl.cdiv(width, STEP)))],
        compiler_params=pltpu.CompilerParams(vmem_limit_bytes=58 << 20),
        cost_estimate=pl.CostEstimate(
            flops=10 * rows * d * width,
            bytes_accessed=6 * d * width + 10 * rows * d + 6 * rows * width,
            transcendentals=rows * width,
        ),
        name="own_rows",
    )(m, cot, wg, wu, wd)


def far_kernel(*refs, count, width, tile, block, offsets, sliced):
    m, cot = refs[:count], refs[count : 2 * count]
    refs = refs[2 * count :]
    m_src, c_src = m, cot
    if sliced:
        m_src, c_src = refs[:count], refs[count : 2 * count]
        refs = refs[2 * count :]
    wg_ref, wu_ref, wd_ref, h_own, gb_own, ub_own = refs[:6]
    gk, uk, dk, sends = refs[6:10]
    m_turned, c_turned, h_all, gb_all, ub_all = refs[10:]
    step = pl.program_id(0)
    rows = m[0].shape[0]
    first = gk.shape[0]

    @pl.when(step == 0)
    def _():
        if not sliced:
            dp, ctx = lax.axis_index("dp"), lax.axis_index("ctx")
            n_ctx = lax.axis_size("ctx")
            starts = [
                pl.multiple_of(((dp ^ a) * n_ctx + (ctx ^ b)) * block, 128) for a, b in offsets
            ]
        for src, dst in ((m_src, m_turned), (c_src, c_turned)):
            at = 0
            for ref in src:
                long = ref.shape[0]
                if sliced:
                    dst[:, at : at + long] = ref[...].T
                else:
                    for j, start in enumerate(starts):
                        piece = ref[:, pl.ds(start, block)]
                        dst[j * block : (j + 1) * block, at : at + long] = piece.T
                at += long

    def body(w):
        wg, wu, wd = wg_ref[:, :w], wu_ref[:, :w], wd_ref[:w, :]
        h_all[:rows, :w] = h_own[:, :w]
        gb_all[:rows, :w] = gb_own[:, :w]
        ub_all[:rows, :w] = ub_own[:, :w]
        at = rows
        for i in range(1, count):
            long = m[i].shape[0]
            size = min(tile, long)
            for t in range(long // size):
                src = slice(t * size, (t + 1) * size)
                dst = slice(at + t * size, at + (t + 1) * size)
                h, gb, ub = gated(m[i][src, :], cot[i][src, :], wg, wu, wd)
                h_all[dst, :w] = h
                gb_all[dst, :w] = gb
                ub_all[dst, :w] = ub
            at += long
        for i, (src, keep) in enumerate(((gb_all, gk), (ub_all, uk))):
            grad = contract(m_turned[...], src[:, :w], 1, 0)
            keep[:, :w] = grad[:first]
            sends[i, :, :w] = grad[first:].astype(BF)
        grad = contract(c_turned[...], h_all[:, :w], 1, 0)
        dk[:w, :] = grad[:first].T
        sends[2, :, :w] = grad[first:].astype(BF)

    full, tail = divmod(width, STEP)
    if tail:
        pl.when(step < full)(lambda: body(STEP))
        pl.when(step == full)(lambda: body(tail))
    else:
        body(STEP)


def far_rows(ms, cots, m_cols, cot_cols, wg, wu, wd, own, block, offsets):
    count = len(ms)
    rows, d = ms[0].shape
    width = wg.shape[1]
    total = sum(m.shape[0] for m in ms)
    wide = block * len(offsets)
    first = wide // 2
    fixed = lambda i: (0, 0)
    col = lambda i: (0, i)
    row = lambda i: (i, 0)
    whole = lambda a: pl.BlockSpec(a.shape, fixed, pipeline_mode=pl.Buffered(1))
    shape = jax.ShapeDtypeStruct
    extra = [] if m_cols is None else list(m_cols) + list(cot_cols)
    return pl.pallas_call(
        functools.partial(
            far_kernel,
            count=count,
            width=width,
            tile=512,
            block=block,
            offsets=offsets,
            sliced=m_cols is not None,
        ),
        grid=(pl.cdiv(width, STEP),),
        in_specs=[whole(a) for a in list(ms) + list(cots) + extra]
        + [pl.BlockSpec((d, STEP), col)] * 2
        + [pl.BlockSpec((STEP, d), row)]
        + [pl.BlockSpec((rows, STEP), col)] * 3,
        out_specs=[pl.BlockSpec((first, STEP), col)] * 2
        + [
            pl.BlockSpec((STEP, first), row),
            pl.BlockSpec((3, first, STEP), lambda i: (0, 0, i)),
        ],
        out_shape=[shape((first, width), F32)] * 2
        + [shape((width, first), F32), shape((3, first, width), BF)],
        scratch_shapes=[pltpu.VMEM((wide, total), BF)] * 2
        + [pltpu.VMEM((total, STEP), BF)] * 3,
        compiler_params=pltpu.CompilerParams(vmem_limit_bytes=60 << 20),
        cost_estimate=pl.CostEstimate(
            flops=6 * (total - rows) * d * width + 6 * total * wide * width,
            bytes_accessed=6 * d * width + 4 * total * d + 6 * rows * width,
            transcendentals=(total - rows) * width,
        ),
        name="far_rows",
    )(*ms, *cots, *extra, wg, wu, wd, *own)


def shards(
    tokens,
    segments,
    attn_gain,
    query_weight,
    key_weight,
    value_weight,
    output_weight,
    mlp_gain,
    gate_weight,
    up_weight,
    down_weight,
    cotangent,
):
    rows, d = tokens.shape
    half = rows // 2
    seq = segments.shape[1]
    window = min(seq, seq // 2 + QB)
    ctx, dp = lax.axis_index("ctx"), lax.axis_index("dp")
    n_ctx, n_dp = lax.axis_size("ctx"), lax.axis_size("dp")
    core = lax.rem(lax.axis_index("tp"), 2)
    tp_rest = bits_of("tp")[1:]
    block_width = d // (n_ctx * n_dp)
    every_bit = bits_of("ctx") + bits_of("dp")
    attn_share = [("ctx", 1)]
    mlp_reduce = bits_of("ctx")[1:] + bits_of("dp")[:-1]
    attn_reduce = [b for b in every_bit if b not in attn_share]

    def owner_offsets(reduce_bits):
        return [
            [bit for i, bit in enumerate(reduce_bits) if code >> (len(reduce_bits) - 1 - i) & 1]
            for code in range(1 << len(reduce_bits))
        ]

    def owner_start(chosen, flip=()):
        other_dp, other_ctx = dp, ctx
        for axis, mask in list(chosen) + list(flip):
            if axis == "dp":
                other_dp = other_dp ^ mask
            else:
                other_ctx = other_ctx ^ mask
        return (other_dp * n_ctx + other_ctx) * block_width

    def columns(value, chosen, flip=()):
        return lax.dynamic_slice_in_dim(value, owner_start(chosen, flip), block_width, 1)

    def all_columns(value, reduce_bits, flip=()):
        return jnp.concatenate(
            [columns(value, chosen, flip) for chosen in owner_offsets(reduce_bits)], 1
        )

    def own_half(value):
        return lax.dynamic_slice_in_dim(value, core * half, half, 0)

    def other_half(value):
        return lax.dynamic_slice_in_dim(value, (1 - core) * half, half, 0)

    def both_halves(value):
        return jnp.concatenate([own_half(value), other_half(value)], 0)

    def join_cores(value):
        return jnp.concatenate([value, swap(value, "tp", 1)], 0)

    def share(value, bits):
        pieces = [value]
        for axis, mask in bits:
            pieces = pieces + [swap(piece, axis, mask) for piece in pieces]
        return join_cores(jnp.concatenate(pieces[1:], 0))

    def share_group(by_ctx, by_dp, gate, gate_dp):
        both = swap(after(by_dp, gate_dp), "ctx", 1)
        return [
            by_ctx,
            swap(after(by_ctx, gate), "tp", 1),
            by_dp,
            swap(after(by_dp, gate_dp), "tp", 1),
            both,
            swap(both, "tp", 1),
        ]

    def mirror(value):
        return swap(value, "dp", n_dp - 1)

    def tp_start(send, keep):
        total = keep + swap(send.astype(BF), "tp", 1).astype(F32)
        for axis, mask in tp_rest[:-1]:
            low = total.astype(BF)
            total = low.astype(F32) + swap(low, axis, mask).astype(F32)
        low = total.astype(BF)
        return low, swap(low, *tp_rest[-1])

    def tp_end(low, other):
        return low.astype(F32) + other.astype(F32)

    def after(value, *others):
        return lax.optimization_barrier((value,) + others)[0]

    def reduce_blocks(value, reduce_bits, dim):
        for axis, mask in reduce_bits:
            middle = value.shape[dim] // 2
            keep = lax.slice_in_dim(value, 0, middle, axis=dim)
            send = lax.slice_in_dim(value, middle, 2 * middle, axis=dim).astype(BF)
            value = keep + swap(send, axis, mask).astype(F32)
        return value

    def sum_gains(value):
        value = value + swap(value, "tp", 1)
        for axis, mask in every_bit:
            value = value + swap(value, axis, mask)
        return lax.dynamic_slice_in_dim(value, owner_start(()), block_width, 1)

    def whole_rows(value):
        out = jnp.zeros((rows, value.shape[1]), F32)
        out = lax.dynamic_update_slice_in_dim(out, value, core * half, 0)
        return lax.dynamic_update_slice_in_dim(out, swap(value, "tp", 1), (1 - core) * half, 0)

    seg_row = segments
    seg_col = jnp.swapaxes(segments, 0, 1)
    query_pos = ctx * rows + jnp.arange(rows, dtype=jnp.int32)
    cos_table, sin_table = rope_tables(query_pos, HEAD)
    kv_weight = jnp.concatenate([key_weight, value_weight], 1)
    cot_half = own_half(cotangent)
    cot_own = jnp.concatenate([cot_half, other_half(cotangent)], 0)
    x_half = own_half(tokens).astype(F32)

    attn_in, q_rot, kv_own = enter(
        tokens, attn_gain[None], query_weight, kv_weight, cos_table, sin_table
    )
    kv_parts = [kv_own]
    for axis, mask in bits_of("ctx"):
        kv_parts = kv_parts + [swap(piece, axis, mask) for piece in kv_parts]
    kv_all = jnp.stack(kv_parts, 0)
    cot_start = after(cot_half, kv_all)
    cot_ctx, cot_dp = swap(cot_start, "ctx", 1), mirror(cot_start)
    heads_out, lse = attend(q_rot, kv_all, seg_col, seg_row, window)
    heads_mine, heads_other = own_half(heads_out), other_half(heads_out)
    low_one, far_one = tp_start(
        contract(heads_other, output_weight, 1, 0), contract(heads_mine, output_weight, 1, 0)
    )
    middle = x_half + tp_end(low_one, far_one)
    inverse_two = lax.rsqrt(jnp.mean(middle * middle, axis=-1, keepdims=True) + EPSILON)
    normed_two = middle * inverse_two
    mlp_half = (normed_two * mlp_gain).astype(BF)
    mlp_ctx, mlp_dp = swap(mlp_half, "ctx", 1), mirror(mlp_half)
    mlp_own = join_cores(mlp_half)
    cot_group = [cot_own] + share_group(cot_ctx, cot_dp, low_one, mlp_own)

    hidden_own, gate_own, up_own, back_send, back_keep = own_rows(
        mlp_own, cot_own, gate_weight, up_weight, down_weight
    )
    low_three, far_three = tp_start(back_send, back_keep)
    mlp_group = [mlp_own] + share_group(mlp_ctx, mlp_dp, back_send, low_three)
    hidden_own = after(hidden_own, low_three)

    offsets = tuple(
        (
            sum(mask for axis, mask in chosen if axis == "dp"),
            sum(mask for axis, mask in chosen if axis == "ctx"),
        )
        for chosen in owner_offsets(mlp_reduce)
    )
    aligned = block_width % 128 == 0
    m_cols = None if aligned else [all_columns(m, mlp_reduce) for m in mlp_group]
    c_cols = None if aligned else [all_columns(c, mlp_reduce) for c in cot_group]
    far = far_rows(
        mlp_group,
        cot_group,
        m_cols,
        c_cols,
        gate_weight,
        up_weight,
        down_weight,
        (hidden_own, gate_own, up_own),
        block_width,
        offsets,
    )

    crossed = swap(far[3], *mlp_reduce[0])
    mlp_in_back = tp_end(low_three, after(far_three, far[3]))
    scaled = mlp_in_back * mlp_gain
    middle_back = cot_half.astype(F32) + inverse_two * (
        scaled - normed_two * jnp.mean(scaled * normed_two, axis=-1, keepdims=True)
    )
    mlp_gain_part = jnp.sum(mlp_in_back * normed_two, axis=0)
    branch_half = middle_back.astype(BF)
    branch_own = join_cores(branch_half)
    heads_back = contract(branch_own, output_weight, 1, 1).astype(BF)

    hidden_two = after(hidden_own, branch_half)
    low_two, far_two = tp_start(
        contract(hidden_two[half:], down_weight, 1, 0),
        contract(hidden_two[:half], down_weight, 1, 0),
    )

    query_back, kv_part, kv_far = attend_back(
        q_rot, heads_back, kv_all, lse, seg_col, seg_row, cos_table, sin_table, window
    )
    kv_back = join_keys(
        kv_part,
        [swap(kv_far[j - 1], "ctx", j) for j in range(1, n_ctx)],
        cos_table,
        sin_table,
    )
    qkv_back = jnp.concatenate([query_back, kv_back], 1)
    back_mine, back_other = own_half(qkv_back), other_half(qkv_back)
    q_width = query_back.shape[1]

    def attn_back(part):
        return contract(part[:, :q_width], query_weight, 1, 1) + contract(
            part[:, q_width:], kv_weight, 1, 1
        )

    low_four, far_four = tp_start(attn_back(back_other), attn_back(back_mine))
    layer_out = whole_rows(middle + tp_end(low_two, after(far_two, low_four)))
    attn_in_back = tp_end(low_four, far_four)
    inverse_one = lax.rsqrt(jnp.mean(x_half * x_half, axis=-1, keepdims=True) + EPSILON)
    normed_one = x_half * inverse_one
    scaled_one = attn_in_back * attn_gain
    tokens_half = middle_back + inverse_one * (
        scaled_one - normed_one * jnp.mean(scaled_one * normed_one, axis=-1, keepdims=True)
    )
    tokens_grad = whole_rows(tokens_half)
    crossed = after(crossed, low_four).astype(F32)
    gate_grad = reduce_blocks(far[0] + crossed[0], mlp_reduce[1:], 0)
    up_grad = reduce_blocks(far[1] + crossed[1], mlp_reduce[1:], 0)
    down_grad = reduce_blocks(far[2] + crossed[2].T, mlp_reduce[1:], 1)
    gains = sum_gains(jnp.stack([jnp.sum(attn_in_back * normed_one, axis=0), mlp_gain_part]))

    flip = attn_share
    attn_cols = both_halves(all_columns(attn_in, attn_reduce))
    attn_cols_far = share(
        after(own_half(all_columns(attn_in, attn_reduce, flip)), mlp_group[1]), attn_share
    )
    heads_rel = jnp.concatenate([heads_mine, heads_other], 0)
    heads_far = swap(after(heads_rel, mlp_group[1]), *attn_share[0])
    branch_cols = all_columns(branch_own, attn_reduce)
    branch_cols_far = share(all_columns(branch_half, attn_reduce, flip), attn_share)
    back_rel = jnp.concatenate([back_mine, back_other], 0)
    back_far_rel = swap(back_rel, *attn_share[0])
    output_grad = reduce_blocks(
        contract(heads_rel, branch_cols, 0, 0) + contract(heads_far, branch_cols_far, 0, 0),
        attn_reduce,
        1,
    )
    qkv_grad = reduce_blocks(
        contract(attn_cols, back_rel, 0, 0) + contract(attn_cols_far, back_far_rel, 0, 0),
        attn_reduce,
        0,
    )
    return (
        layer_out,
        tokens_grad,
        gains[0],
        qkv_grad[:, :q_width],
        qkv_grad[:, q_width : q_width + HEAD],
        qkv_grad[:, q_width + HEAD :],
        output_grad,
        gains[1],
        gate_grad,
        up_grad,
        down_grad,
    )


def solution(mesh):
    return jax.shard_map(
        shards,
        mesh=mesh,
        in_specs=(
            P(("dp", "ctx"), None),
            P("dp", None),
            P(),
            P(None, "tp"),
            P(None, "tp"),
            P(None, "tp"),
            P("tp", None),
            P(),
            P(None, "tp"),
            P(None, "tp"),
            P("tp", None),
            P(("dp", "ctx"), None),
        ),
        out_specs=(
            P(("dp", "ctx"), None),
            P(("dp", "ctx"), None),
            P(("dp", "ctx")),
            P(("dp", "ctx"), "tp"),
            P(("dp", "ctx"), "tp"),
            P(("dp", "ctx"), "tp"),
            P("tp", ("dp", "ctx")),
            P(("dp", "ctx")),
            P(("dp", "ctx"), "tp"),
            P(("dp", "ctx"), "tp"),
            P("tp", ("dp", "ctx")),
        ),
        check_vma=False,
    )
```

profile of v0, /device:TPU:0, one launch (start us, length us, event | category | flops | bytes accessed | tf_op | source)
XLA Modules:
  0.0 417.1 jit_solution(17560796434810027202)
XLA Ops:
  0.7 1.4 copy.28
  4.3 1.3 pad_maximum_fusion.11
  6.7 6.2 %enter.1 = (bf16[512,2048]{1,0:T(8,128)(2,1)}, bf16[512,512]{1,0:T(8,128)(2,1)}, bf16[512,128]{1,0:T(8,128)(2,1)}) custom-call(bf16[512,2048]{1,0:T(8,128)(2,1)} %x_ref.1, f32[1,2048]{1,0:T(1,128)} %bitcast.46, bf16[2048,512]{1,0:T(8,128)(2,1)} %wq_ref.1, bf16[2048,128]{1,0:T(8,128)(2,1)} %pad_maximum_fusion.8.wkv_ref, ...), custom_call_target="tpu_custom_call" | custom-call | tf_op jit(solution)/shard_map/enter/pallas_call | solution.py:80
  12.8 3.0 collective-permute-start
  16.8 2.7 collective-permute-done
  19.5 1.6 pad_maximum_fusion.13.kv_ref
  21.1 8.1 %attend.1 = (bf16[512,512]{1,0:T(8,128)(2,1)}, f32[8,512]{1,0:T(8,128)}) custom-call(bf16[512,512]{1,0:T(8,128)(2,1)} %get-tuple-element.40.q_ref, bf16[2,512,128]{2,1,0:T(8,128)(2,1)} %pad_maximum_fusion.13.kv_ref, s32[1024,1]{1,0:T(8,128)} %copy.30.segc_ref, s32[1,1024]{1,0:T(1,128)} %segr_ref.3), custom_call_target="tpu_custom_call" | custom-call | tf_op jit(solution)/shard_map/attend/pallas_call | solution.py:166
  31.1 2.6 collective-permute-done.1
  34.6 1.8 collective-permute-start.2
  36.4 23.5 %collective-permute-done.2 = bf16[256,2048]{1,0:T(8,128)(2,1)S(1)} collective-permute-done((bf16[256,2048]{1,0:T(8,128)(2,1)S(1)}, bf16[256,2048]{1,0:T(8,128)(2,1)S(1)}, u32[]{:S(2)}, u32[]{:S(2)}) %collective-permute-start.2) | collective-permute-done | bytes 1048608 | tf_op jit(solution)/shard_map/ppermute | solution.py:29
  60.9 2.0 copy-done.19
  63.1 1.5 pad_maximum_fusion.3.c_ref.refs_7_
  64.6 3.8 collective-permute-start.14
  68.4 1.5 collective-permute-start.12
  69.9 1.6 pad_maximum_fusion.2.m_ref.refs_0_
  71.5 25.5 %own_rows.1 = (bf16[512,1408]{1,0:T(8,128)(2,1)}, bf16[512,1408]{1,0:T(8,128)(2,1)}, bf16[512,1408]{1,0:T(8,128)(2,1)}, bf16[256,2048]{1,0:T(8,128)(2,1)}, f32[256,2048]{1,0:T(8,128)}) custom-call(bf16[512,2048]{1,0:T(8,128)(2,1)} %pad_maximum_fusion.2.m_ref.refs_0_, bf16[512,2048]{1,0:T(8,128)(2,1)} %pad_maximum_fusion.3.c_ref.refs_7_, ...), custom_call_target="tpu_custom_call" | custom-call | flops 14763950080 | bytes 32112640 | tf_op jit(solution)/shard_map/own_rows/pallas_call | solution.py:384
  98.2 1.5 collective-permute-start.16
  100.0 2.8 add_convert_fusion.2
  102.8 21.9 %collective-permute-done.8.refs_3_ = bf16[256,2048]{1,0:T(8,128)(2,1)} collective-permute-done((bf16[256,2048]{1,0:T(8,128)(2,1)S(1)}, bf16[256,2048]{1,0:T(8,128)(2,1)}, u32[]{:S(2)}, u32[]{:S(2)}) %collective-permute-start.8) | collective-permute-done | bytes 1048608 | tf_op jit(solution)/shard_map/ppermute | solution.py:29
  125.8 20.5 %collective-permute-done.16.refs_12_ = bf16[256,2048]{1,0:T(8,128)(2,1)} collective-permute-done((bf16[256,2048]{1,0:T(8,128)(2,1)}, bf16[256,2048]{1,0:T(8,128)(2,1)}, u32[]{:S(2)}, u32[]{:S(2)}) %collective-permute-start.16) | collective-permute-done | bytes 1048608 | tf_op jit(solution)/shard_map/ppermute | solution.py:29
  146.3 21.8 %collective-permute-done.10.refs_5_ = bf16[256,2048]{1,0:T(8,128)(2,1)} collective-permute-done((bf16[256,2048]{1,0:T(8,128)(2,1)}, bf16[256,2048]{1,0:T(8,128)(2,1)}, u32[]{:S(2)}, u32[]{:S(2)}) %collective-permute-start.10) | collective-permute-done | bytes 1048608 | tf_op jit(solution)/shard_map/ppermute | solution.py:29
  168.0 2.5 constant_dynamic-slice_fusion.5
  171.8 1.7 collective-permute-start.5
  173.5 66.5 %far_rows.1 = (f32[256,1408]{1,0:T(8,128)}, f32[256,1408]{1,0:T(8,128)}, f32[1408,256]{1,0:T(8,128)}, bf16[3,256,1408]{2,1,0:T(8,128)(2,1)}) custom-call(bf16[512,2048]{1,0:T(8,128)(2,1)} %pad_maximum_fusion.2.m_ref.refs_0_, bf16[256,2048]{1,0:T(8,128)(2,1)} %collective-permute-done.6.refs_1_, bf16[256,2048]{1,0:T(8,128)(2,1)} %collective-permute-done.7.refs_2_, ...), custom_call_target="tpu_custom_call" | custom-call | flops 35433480192 | bytes 38404096 | tf_op jit(solution)/shard_map/far_rows/pallas_call | solution.py:482
  240.1 3.1 multiply_reduce_fusion
  243.2 3.4 fusion.68
  247.9 1.6 collective-permute-start.36
  252.7 15.7 %collective-permute-start.40 = (bf16[3,256,1408]{2,1,0:T(8,128)(2,1)}, bf16[3,256,1408]{2,1,0:T(8,128)(2,1)}, u32[]{:S(2)}, u32[]{:S(2)}) collective-permute-start(bf16[3,256,1408]{2,1,0:T(8,128)(2,1)} %get-tuple-element.54), channel_id=1, source_target_pairs={{0,8},{8,0},{16,24},{24,16},{1,9},{9,1},{17,25},{25,17},{2,10},{10... | collective-permute-start | bytes 6488072 | tf_op jit(solution)/shard_map/ppermute | solution.py:29
  268.7 5.5 %convolution_convert_fusion.1 = bf16[256,2048]{1,0:T(8,128)(2,1)} fusion(bf16[1408,2048]{1,0:T(8,128)(2,1)} %refs_16_.1, bf16[512,1408]{1,0:T(8,128)(2,1)S(1)} %copy-done.38), kind=kOutput, calls=%fused_computation.19 | convolution fusion | flops 1476919296 | bytes 7536640 | tf_op jit(solution)/shard_map/dot_general | solution.py:19
  274.1 2.9 copy.32
  277.3 3.6 fusion.16.hb_ref
  281.0 11.9 %attend_back.1 = (bf16[512,512]{1,0:T(8,128)(2,1)}, f32[512,128]{1,0:T(8,128)}, bf16[1,512,128]{2,1,0:T(8,128)(2,1)}) custom-call(bf16[512,512]{1,0:T(8,128)(2,1)} %get-tuple-element.40.q_ref, bf16[512,512]{1,0:T(8,128)(2,1)} %fusion.16.hb_ref, bf16[2,512,128]{2,1,0:T(8,128)(2,1)} %pad_maximum_fusion.13.kv_ref, f32[8,512]{1,0:T(8,128)} %get-tuple-element.57.lse_ref, ...), custom_call_target="tpu_custom_call" | custom-call | tf_op jit(solution)/shard_map/attend_back/pallas_call | solution.py:255
  292.8 1.4 fusion.49
  294.8 2.2 fusion.35
  297.8 1.3 copy-done.22
  300.0 10.2 %collective-permute-start.38 = (bf16[512,512]{1,0:T(8,128)(2,1)}, bf16[512,512]{1,0:T(8,128)(2,1)}, u32[]{:S(2)}, u32[]{:S(2)}) collective-permute-start(bf16[512,512]{1,0:T(8,128)(2,1)} %slice.146), channel_id=1, source_target_pairs={{0,8},{8,0},{16,24},{24,16},{1,9},{9,1},{17,25},{25,17},{2,10},{10... | collective-permute-start | bytes 1572872 | tf_op jit(solution)/shard_map/ppermute | solution.py:29
  310.3 4.0 add_convert_fusion.1
  315.0 2.0 join_keys.1
  318.3 1.5 fusion.57
  320.6 1.6 collective-permute-start.32
  323.6 4.0 collective-permute-done.38
  329.5 2.1 collective-permute-start.39
  331.5 5.2 %collective-permute-done.32 = bf16[512,640]{1,0:T(8,128)(2,1)S(1)} collective-permute-done((bf16[512,640]{1,0:T(8,128)(2,1)S(1)}, bf16[512,640]{1,0:T(8,128)(2,1)S(1)}, u32[]{:S(2)}, u32[]{:S(2)}) %collective-permute-start.32) | collective-permute-done | bytes 655392 | tf_op jit(solution)/shard_map/ppermute | solution.py:29
  336.7 2.1 convolution_add_fusion.2
  338.9 1.6 copy-done.9
  341.7 2.3 collective-permute-done.39
  344.9 1.8 add_convert_fusion
  346.7 1.5 collective-permute-start.24
  348.2 1.9 convert_element_type.127
  350.1 2.0 copy-done.5
  352.1 1.2 fusion.13
  353.4 2.9 copy.34
  357.9 3.8 constant_dynamic-update-slice_fusion.3
  361.7 1.9 fusion.14
  364.7 10.7 %collective-permute-done.24 = bf16[256,2048]{1,0:T(8,128)(2,1)} collective-permute-done((bf16[256,2048]{1,0:T(8,128)(2,1)}, bf16[256,2048]{1,0:T(8,128)(2,1)}, u32[]{:S(2)}, u32[]{:S(2)}) %collective-permute-start.24) | collective-permute-done | bytes 1048608 | tf_op jit(solution)/shard_map/ppermute | solution.py:29
  375.5 2.5 fusion.8
  378.8 5.3 %constant_dynamic-update-slice_fusion.1 = (f32[512,2048]{1,0:T(8,128)S(1)}, f32[256,2048]{1,0:T(8,128)}) fusion(f32[512,2048]{1,0:T(8,128)S(1)} %broadcast.63.clone.1, s32[]{:T(128)S(6)} %select_n.20, f32[256]{0:T(256)S(1)} %broadcast_multiply_fusion, bf16[512,2048]{1,0:T(8,128)(2,1)S(1)} %copy-done.7, f32[2048]{0:T(1024)S(1)} %copy-done.30, ...), kind=kLoop, calls=%fused_computation.133 | loop fusion | flops 10485760 | bytes 12603396 | tf_op jit(solution)/shard_map/dynamic_update_slice | solution.py:629
  385.2 1.6 slice_add_fusion
  386.9 1.8 collective-permute-start.34
  389.9 14.5 %collective-permute-done.34 = bf16[256,640]{0,1:T(8,128)(2,1)S(1)} collective-permute-done((bf16[256,640]{0,1:T(8,128)(2,1)S(1)}, bf16[256,640]{0,1:T(8,128)(2,1)S(1)}, u32[]{:S(2)}, u32[]{:S(2)}) %collective-permute-start.34) | collective-permute-done | bytes 327712 | tf_op jit(solution)/shard_map/ppermute | solution.py:29
  406.1 2.0 copy.33
  409.8 3.3 constant_dynamic-update-slice_fusion.2
  413.1 1.8 constant_dynamic-update-slice_fusion
  414.9 2.0 copy-done.14
  (188 shorter events, 36.5 us)
Async XLA Ops:
  0.6 29.7 %copy-start = (bf16[512,2048]{1,0:T(8,128)(2,1)S(1)}, bf16[512,2048]{1,0:T(8,128)(2,1)}, u32[]{:S(2)}) copy-start(bf16[512,2048]{1,0:T(8,128)(2,1)} %param.18) | copy-start | bytes 6291460
  6.7 9.1 %copy-start.31 = (s32[1,1024]{1,0:T(1,128)S(1)}, s32[1,1024]{1,0:T(1,128)}, u32[]{:S(2)}) copy-start(s32[1,1024]{1,0:T(1,128)} %segr_ref.3) | copy-start | bytes 12292
  12.8 6.7 %collective-permute-start = (bf16[512,128]{1,0:T(8,128)(2,1)}, bf16[512,128]{1,0:T(8,128)(2,1)S(1)}, u32[]{:S(2)}, u32[]{:S(2)}) collective-permute-start(bf16[512,128]{1,0:T(8,128)(2,1)} %get-tuple-element.41), channel_id=1, source_target_pairs={{0,4},{4,0},{1,5},{5,1},{2,6},{6,2},{3,7},{7,3},{8,12},{12,8},{9,1... | collective-permute-start | bytes 393224 | tf_op jit(solution)/shard_map/ppermute | solution.py:29
  30.3 3.5 copy-start.16
  31.1 2.7 collective-permute-start.1
  33.8 26.1 %copy-start.6 = (bf16[512,2048]{1,0:T(8,128)(2,1)S(1)}, bf16[512,2048]{1,0:T(8,128)(2,1)}, u32[]{:S(2)}) copy-start(bf16[512,2048]{1,0:T(8,128)(2,1)} %x_ref.1) | copy-start | bytes 6291460
  34.5 26.0 %copy-start.28 = (f32[2048]{0:T(1024)S(1)}, f32[2048]{0:T(1024)}, u32[]{:S(2)}) copy-start(f32[2048]{0:T(1024)} %param.19) | copy-start | bytes 24580
  34.6 25.3 %collective-permute-start.2 = (bf16[256,2048]{1,0:T(8,128)(2,1)S(1)}, bf16[256,2048]{1,0:T(8,128)(2,1)S(1)}, u32[]{:S(2)}, u32[]{:S(2)}) collective-permute-start(bf16[256,2048]{1,0:T(8,128)(2,1)S(1)} %add_convert_fusion.3), channel_id=1, source_target_pairs={{0,2},{1,3},{2,0},{3,1},{4,6},{5,7},{6,4},{7,5},{8,10},{9,11},{10,... | collective-permute-start | bytes 3145736 | tf_op jit(solution)/shard_map/ppermute | solution.py:29
  60.6 182.6 %copy-start.32 = (f32[256]{0:T(256)}, f32[256]{0:T(256)S(1)}, u32[]{:S(2)}) copy-start(f32[256]{0:T(256)S(1)} %add_rsqrt_fusion.1) | copy-start | bytes 3076
  60.9 9.1 %collective-permute-start.3 = (bf16[256,2048]{1,0:T(8,128)(2,1)S(1)}, bf16[256,2048]{1,0:T(8,128)(2,1)S(1)}, u32[]{:S(2)}, u32[]{:S(2)}) collective-permute-start(bf16[256,2048]{1,0:T(8,128)(2,1)S(1)} %multiply_convert_fusion), channel_id=1, source_target_pairs={{0,1},{1,0},{2,3},{3,2},{4,5},{5,4},{6,7},{7,6},{8,9},{9,8},{10,11... | collective-permute-start | bytes 3145736 | tf_op jit(solution)/shard_map/ppermute | solution.py:29
  64.6 33.6 %collective-permute-start.14 = (bf16[256,2048]{1,0:T(8,128)(2,1)S(1)}, bf16[256,2048]{1,0:T(8,128)(2,1)}, u32[]{:S(2)}, u32[]{:S(2)}) collective-permute-start(bf16[256,2048]{1,0:T(8,128)(2,1)S(1)} %get-tuple-element.49), channel_id=1, source_target_pairs={{0,24},{8,16},{16,8},{24,0},{1,25},{9,17},{17,9},{25,1},{2,26},{10... | collective-permute-start | bytes 3145736 | tf_op jit(solution)/shard_map/ppermute | solution.py:29
  68.4 29.0 %collective-permute-start.12 = (bf16[256,2048]{1,0:T(8,128)(2,1)S(1)}, bf16[256,2048]{1,0:T(8,128)(2,1)}, u32[]{:S(2)}, u32[]{:S(2)}) collective-permute-start(bf16[256,2048]{1,0:T(8,128)(2,1)S(1)} %get-tuple-element.49), channel_id=1, source_target_pairs={{0,4},{4,0},{1,5},{5,1},{2,6},{6,2},{3,7},{7,3},{8,12},{12,8},{9,1... | collective-permute-start | bytes 3145736 | tf_op jit(solution)/shard_map/ppermute | solution.py:29
  97.1 2.9 collective-permute-start.4
  97.1 27.6 %collective-permute-start.8 = (bf16[256,2048]{1,0:T(8,128)(2,1)S(1)}, bf16[256,2048]{1,0:T(8,128)(2,1)}, u32[]{:S(2)}, u32[]{:S(2)}) collective-permute-start(bf16[256,2048]{1,0:T(8,128)(2,1)S(1)} %multiply_convert_fusion), channel_id=1, source_target_pairs={{0,24},{8,16},{16,8},{24,0},{1,25},{9,17},{17,9},{25,1},{2,26},{10... | collective-permute-start | bytes 3145736 | tf_op jit(solution)/shard_map/ppermute | solution.py:29
  97.4 28.3 %collective-permute-start.13 = (bf16[256,2048]{1,0:T(8,128)(2,1)}, bf16[256,2048]{1,0:T(8,128)(2,1)}, u32[]{:S(2)}, u32[]{:S(2)}) collective-permute-start(bf16[256,2048]{1,0:T(8,128)(2,1)} %collective-permute-done.12.refs_8_), channel_id=1, source_target_pairs={{0,1},{1,0},{2,3},{3,2},{4,5},{5,4},{6,7},{7,6},{8,9},{9,8},{10,11... | collective-permute-start | bytes 3145736 | tf_op jit(solution)/shard_map/ppermute | solution.py:29
  97.6 27.6 %collective-permute-start.6 = (bf16[256,2048]{1,0:T(8,128)(2,1)S(1)}, bf16[256,2048]{1,0:T(8,128)(2,1)}, u32[]{:S(2)}, u32[]{:S(2)}) collective-permute-start(bf16[256,2048]{1,0:T(8,128)(2,1)S(1)} %multiply_convert_fusion), channel_id=1, source_target_pairs={{0,4},{4,0},{1,5},{5,1},{2,6},{6,2},{3,7},{7,3},{8,12},{12,8},{9,1... | collective-permute-start | bytes 3145736 | tf_op jit(solution)/shard_map/ppermute | solution.py:29
  98.2 48.1 %collective-permute-start.16 = (bf16[256,2048]{1,0:T(8,128)(2,1)}, bf16[256,2048]{1,0:T(8,128)(2,1)}, u32[]{:S(2)}, u32[]{:S(2)}) collective-permute-start(bf16[256,2048]{1,0:T(8,128)(2,1)} %collective-permute-done.14.refs_10_), channel_id=1, source_target_pairs={{0,4},{4,0},{1,5},{5,1},{2,6},{6,2},{3,7},{7,3},{8,12},{12,8},{9,1... | collective-permute-start | bytes 3145736 | tf_op jit(solution)/shard_map/ppermute | solution.py:29
  124.7 43.3 %collective-permute-start.10 = (bf16[256,2048]{1,0:T(8,128)(2,1)}, bf16[256,2048]{1,0:T(8,128)(2,1)}, u32[]{:S(2)}, u32[]{:S(2)}) collective-permute-start(bf16[256,2048]{1,0:T(8,128)(2,1)} %collective-permute-done.8.refs_3_), channel_id=1, source_target_pairs={{0,4},{4,0},{1,5},{5,1},{2,6},{6,2},{3,7},{7,3},{8,12},{12,8},{9,1... | collective-permute-start | bytes 3145736 | tf_op jit(solution)/shard_map/ppermute | solution.py:29
  125.2 46.2 %collective-permute-start.7 = (bf16[256,2048]{1,0:T(8,128)(2,1)}, bf16[256,2048]{1,0:T(8,128)(2,1)}, u32[]{:S(2)}, u32[]{:S(2)}) collective-permute-start(bf16[256,2048]{1,0:T(8,128)(2,1)} %collective-permute-done.6.refs_1_), channel_id=1, source_target_pairs={{0,1},{1,0},{2,3},{3,2},{4,5},{5,4},{6,7},{7,6},{8,9},{9,8},{10,11... | collective-permute-start | bytes 3145736 | tf_op jit(solution)/shard_map/ppermute | solution.py:29
  125.2 46.6 %collective-permute-start.15 = (bf16[256,2048]{1,0:T(8,128)(2,1)}, bf16[256,2048]{1,0:T(8,128)(2,1)}, u32[]{:S(2)}, u32[]{:S(2)}) collective-permute-start(bf16[256,2048]{1,0:T(8,128)(2,1)} %collective-permute-done.14.refs_10_), channel_id=1, source_target_pairs={{0,1},{1,0},{2,3},{3,2},{4,5},{5,4},{6,7},{7,6},{8,9},{9,8},{10,11... | collective-permute-start | bytes 3145736 | tf_op jit(solution)/shard_map/ppermute | solution.py:29
  125.8 47.7 %collective-permute-start.9 = (bf16[256,2048]{1,0:T(8,128)(2,1)}, bf16[256,2048]{1,0:T(8,128)(2,1)}, u32[]{:S(2)}, u32[]{:S(2)}) collective-permute-start(bf16[256,2048]{1,0:T(8,128)(2,1)} %collective-permute-done.8.refs_3_), channel_id=1, source_target_pairs={{0,1},{1,0},{2,3},{3,2},{4,5},{5,4},{6,7},{7,6},{8,9},{9,8},{10,11... | collective-permute-start | bytes 3145736 | tf_op jit(solution)/shard_map/ppermute | solution.py:29
  146.2 27.2 %collective-permute-start.17 = (bf16[256,2048]{1,0:T(8,128)(2,1)}, bf16[256,2048]{1,0:T(8,128)(2,1)}, u32[]{:S(2)}, u32[]{:S(2)}) collective-permute-start(bf16[256,2048]{1,0:T(8,128)(2,1)} %collective-permute-done.16.refs_12_), channel_id=1, source_target_pairs={{0,1},{1,0},{2,3},{3,2},{4,5},{5,4},{6,7},{7,6},{8,9},{9,8},{10,11... | collective-permute-start | bytes 3145736 | tf_op jit(solution)/shard_map/ppermute | solution.py:29
  168.0 5.5 %collective-permute-start.11 = (bf16[256,2048]{1,0:T(8,128)(2,1)}, bf16[256,2048]{1,0:T(8,128)(2,1)}, u32[]{:S(2)}, u32[]{:S(2)}) collective-permute-start(bf16[256,2048]{1,0:T(8,128)(2,1)} %collective-permute-done.10.refs_5_), channel_id=1, source_target_pairs={{0,1},{1,0},{2,3},{3,2},{4,5},{5,4},{6,7},{7,6},{8,9},{9,8},{10,11... | collective-permute-start | bytes 3145736 | tf_op jit(solution)/shard_map/ppermute | solution.py:29
  171.4 81.2 %collective-permute-start.30 = (bf16[256,1024]{1,0:T(8,128)(2,1)}, bf16[256,1024]{1,0:T(8,128)(2,1)}, u32[]{:S(2)}, u32[]{:S(2)}) collective-permute-start(bf16[256,1024]{1,0:T(8,128)(2,1)} %fusion.46), channel_id=1, source_target_pairs={{0,4},{4,0},{1,5},{5,1},{2,6},{6,2},{3,7},{7,3},{8,12},{12,8},{9,1... | collective-permute-start | bytes 1572872 | tf_op jit(solution)/shard_map/ppermute | solution.py:29
  171.8 68.2 %collective-permute-start.5 = (bf16[256,2048]{1,0:T(8,128)(2,1)}, bf16[256,2048]{1,0:T(8,128)(2,1)}, u32[]{:S(2)}, u32[]{:S(2)}) collective-permute-start(bf16[256,2048]{1,0:T(8,128)(2,1)} %add_convert_fusion.2), channel_id=1, source_target_pairs={{0,2},{1,3},{2,0},{3,1},{4,6},{5,7},{6,4},{7,5},{8,10},{9,11},{10,... | collective-permute-start | bytes 3145736 | tf_op jit(solution)/shard_map/ppermute | solution.py:29
  240.1 3.2 copy-start.2
  243.2 3.4 copy-start.34
  246.6 30.4 %collective-permute-start.20 = (bf16[256,2048]{1,0:T(8,128)(2,1)}, bf16[256,2048]{1,0:T(8,128)(2,1)}, u32[]{:S(2)}, u32[]{:S(2)}) collective-permute-start(bf16[256,2048]{1,0:T(8,128)(2,1)} %fusion.68), channel_id=1, source_target_pairs={{0,1},{1,0},{2,3},{3,2},{4,5},{5,4},{6,7},{7,6},{8,9},{9,8},{10,11... | collective-permute-start | bytes 3145736 | tf_op jit(solution)/shard_map/ppermute | solution.py:29
  247.9 20.5 %collective-permute-start.36 = (bf16[256,1024]{1,0:T(8,128)(2,1)S(1)}, bf16[256,1024]{1,0:T(8,128)(2,1)}, u32[]{:S(2)}, u32[]{:S(2)}) collective-permute-start(bf16[256,1024]{1,0:T(8,128)(2,1)S(1)} %pad_maximum_fusion.10), channel_id=1, source_target_pairs={{0,4},{4,0},{1,5},{5,1},{2,6},{6,2},{3,7},{7,3},{8,12},{12,8},{9,1... | collective-permute-start | bytes 1572872 | tf_op jit(solution)/shard_map/ppermute | solution.py:29
  249.7 19.0 %copy-start.38 = (bf16[512,1408]{1,0:T(8,128)(2,1)S(1)}, bf16[512,1408]{1,0:T(8,128)(2,1)}, u32[]{:S(2)}) copy-start(bf16[512,1408]{1,0:T(8,128)(2,1)} %get-tuple-element.56.refs_17_) | copy-start | bytes 4325380
  252.1 42.1 %collective-permute-start.35 = (bf16[512,512]{1,0:T(8,128)(2,1)}, bf16[512,512]{1,0:T(8,128)(2,1)}, u32[]{:S(2)}, u32[]{:S(2)}) collective-permute-start(bf16[512,512]{1,0:T(8,128)(2,1)} %pad_maximum_fusion.9), channel_id=1, source_target_pairs={{0,4},{4,0},{1,5},{5,1},{2,6},{6,2},{3,7},{7,3},{8,12},{12,8},{9,1... | collective-permute-start | bytes 1572872 | tf_op jit(solution)/shard_map/ppermute | solution.py:29
  252.7 76.8 %collective-permute-start.31 = (bf16[256,1024]{1,0:T(8,128)(2,1)}, bf16[256,1024]{1,0:T(8,128)(2,1)}, u32[]{:S(2)}, u32[]{:S(2)}) collective-permute-start(bf16[256,1024]{1,0:T(8,128)(2,1)} %collective-permute-done.30), channel_id=1, source_target_pairs={{0,1},{1,0},{2,3},{3,2},{4,5},{5,4},{6,7},{7,6},{8,9},{9,8},{10,11... | collective-permute-start | bytes 1572872 | tf_op jit(solution)/shard_map/ppermute | solution.py:29
  252.7 95.5 %collective-permute-start.40 = (bf16[3,256,1408]{2,1,0:T(8,128)(2,1)}, bf16[3,256,1408]{2,1,0:T(8,128)(2,1)}, u32[]{:S(2)}, u32[]{:S(2)}) collective-permute-start(bf16[3,256,1408]{2,1,0:T(8,128)(2,1)} %get-tuple-element.54), channel_id=1, source_target_pairs={{0,8},{8,0},{16,24},{24,16},{1,9},{9,1},{17,25},{25,17},{2,10},{10... | collective-permute-start | bytes 6488072 | tf_op jit(solution)/shard_map/ppermute | solution.py:29
  268.4 26.4 %collective-permute-start.37 = (bf16[256,1024]{1,0:T(8,128)(2,1)}, bf16[256,1024]{1,0:T(8,128)(2,1)}, u32[]{:S(2)}, u32[]{:S(2)}) collective-permute-start(bf16[256,1024]{1,0:T(8,128)(2,1)} %collective-permute-done.36), channel_id=1, source_target_pairs={{0,1},{1,0},{2,3},{3,2},{4,5},{5,4},{6,7},{7,6},{8,9},{9,8},{10,11... | collective-permute-start | bytes 1572872 | tf_op jit(solution)/shard_map/ppermute | solution.py:29
  277.0 33.2 %collective-permute-start.18 = (bf16[256,2048]{1,0:T(8,128)(2,1)}, bf16[256,2048]{1,0:T(8,128)(2,1)}, u32[]{:S(2)}, u32[]{:S(2)}) collective-permute-start(bf16[256,2048]{1,0:T(8,128)(2,1)} %convolution_convert_fusion.1), channel_id=1, source_target_pairs={{0,1},{1,0},{2,3},{3,2},{4,5},{5,4},{6,7},{7,6},{8,9},{9,8},{10,11... | collective-permute-start | bytes 3145736 | tf_op jit(solution)/shard_map/ppermute | solution.py:29
  294.2 20.1 %collective-permute-start.21 = (bf16[512,128]{1,0:T(8,128)(2,1)S(1)}, bf16[512,128]{1,0:T(8,128)(2,1)S(1)}, u32[]{:S(2)}, u32[]{:S(2)}) collective-permute-start(bf16[512,128]{1,0:T(8,128)(2,1)S(1)} %bitcast.52), channel_id=1, source_target_pairs={{0,4},{4,0},{1,5},{5,1},{2,6},{6,2},{3,7},{7,3},{8,12},{12,8},{9,1... | collective-permute-start | bytes 393224 | tf_op jit(solution)/shard_map/ppermute | solution.py:29
  294.8 15.4 %slice-start.2 = ((s8[5767168]{0:T(1024)(128)(4,1)}), s8[4194304]{0:T(1024)(128)(4,1)S(1)}, s32[]{:S(2)}) async-start(s8[5767168]{0:T(1024)(128)(4,1)} %bitcast.50), calls=%async_computation.2 | async-start | bytes 8388608
  297.1 13.2 %slice-start.3 = ((s8[5767168]{0:T(1024)(128)(4,1)}), s8[1572864]{0:T(1024)(128)(4,1)S(1)}, s32[]{:S(2)}) async-start(s8[5767168]{0:T(1024)(128)(4,1)} %bitcast.50), calls=%async_computation.3 | async-start | bytes 3145728
  297.1 13.2 %copy-start.39 = (bf16[512,1408]{1,0:T(8,128)(2,1)S(1)}, bf16[512,1408]{1,0:T(8,128)(2,1)}, u32[]{:S(2)}) copy-start(bf16[512,1408]{1,0:T(8,128)(2,1)} %get-tuple-element.56.refs_17_) | copy-start | bytes 4325380
  300.0 27.6 %collective-permute-start.38 = (bf16[512,512]{1,0:T(8,128)(2,1)}, bf16[512,512]{1,0:T(8,128)(2,1)}, u32[]{:S(2)}, u32[]{:S(2)}) collective-permute-start(bf16[512,512]{1,0:T(8,128)(2,1)} %slice.146), channel_id=1, source_target_pairs={{0,8},{8,0},{16,24},{24,16},{1,9},{9,1},{17,25},{25,17},{2,10},{10... | collective-permute-start | bytes 1572872 | tf_op jit(solution)/shard_map/ppermute | solution.py:29
  320.6 16.1 %collective-permute-start.32 = (bf16[512,640]{1,0:T(8,128)(2,1)S(1)}, bf16[512,640]{1,0:T(8,128)(2,1)S(1)}, u32[]{:S(2)}, u32[]{:S(2)}) collective-permute-start(bf16[512,640]{1,0:T(8,128)(2,1)S(1)} %pad_maximum_fusion.7), channel_id=1, source_target_pairs={{0,4},{4,0},{1,5},{5,1},{2,6},{6,2},{3,7},{7,3},{8,12},{12,8},{9,1... | collective-permute-start | bytes 1966088 | tf_op jit(solution)/shard_map/ppermute | solution.py:29
  322.6 22.3 %collective-permute-start.22 = (bf16[256,2048]{1,0:T(8,128)(2,1)S(1)}, bf16[256,2048]{1,0:T(8,128)(2,1)S(1)}, u32[]{:S(2)}, u32[]{:S(2)}) collective-permute-start(bf16[256,2048]{1,0:T(8,128)(2,1)S(1)} %fusion.3), channel_id=1, source_target_pairs={{0,1},{1,0},{2,3},{3,2},{4,5},{5,4},{6,7},{7,6},{8,9},{9,8},{10,11... | collective-permute-start | bytes 3145736 | tf_op jit(solution)/shard_map/ppermute | solution.py:29
  322.7 5.5 %copy-start.23 = (f32[512,1024]{1,0:T(8,128)S(1)}, f32[512,1024]{1,0:T(8,128)}, u32[]{:S(2)}) copy-start(f32[512,1024]{1,0:T(8,128)} %copy-done.22) | copy-start | bytes 6291460
  327.7 28.6 %collective-permute-start.19 = (bf16[256,2048]{1,0:T(8,128)(2,1)}, bf16[256,2048]{1,0:T(8,128)(2,1)}, u32[]{:S(2)}, u32[]{:S(2)}) collective-permute-start(bf16[256,2048]{1,0:T(8,128)(2,1)} %add_convert_fusion.1), channel_id=1, source_target_pairs={{0,2},{1,3},{2,0},{3,1},{4,6},{5,7},{6,4},{7,5},{8,10},{9,11},{10,... | collective-permute-start | bytes 3145736 | tf_op jit(solution)/shard_map/ppermute | solution.py:29
  329.5 14.5 %collective-permute-start.39 = (bf16[512,256]{1,0:T(8,128)(2,1)S(1)}, bf16[512,256]{1,0:T(8,128)(2,1)S(1)}, u32[]{:S(2)}, u32[]{:S(2)}) collective-permute-start(bf16[512,256]{1,0:T(8,128)(2,1)S(1)} %slice.148), channel_id=1, source_target_pairs={{0,16},{8,24},{16,0},{24,8},{1,17},{9,25},{17,1},{25,9},{2,18},{10... | collective-permute-start | bytes 786440 | tf_op jit(solution)/shard_map/ppermute | solution.py:29
  341.4 43.7 %collective-permute-start.33 = (bf16[512,640]{0,1:T(8,128)(2,1)}, bf16[512,640]{0,1:T(8,128)(2,1)}, u32[]{:S(2)}, u32[]{:S(2)}) collective-permute-start(bf16[512,640]{0,1:T(8,128)(2,1)} %slice.145), channel_id=1, source_target_pairs={{0,8},{8,0},{16,24},{24,16},{1,9},{9,1},{17,25},{25,17},{2,10},{10... | collective-permute-start | bytes 1966088 | tf_op jit(solution)/shard_map/ppermute | solution.py:29
  346.7 5.4 %copy-start.11 = (f32[1408,256]{0,1:T(8,128)S(1)}, f32[1408,256]{0,1:T(8,128)}, u32[]{:S(2)}) copy-start(f32[1408,256]{0,1:T(8,128)} %copy.32) | copy-start | bytes 4325380
  346.7 28.8 %collective-permute-start.24 = (bf16[256,2048]{1,0:T(8,128)(2,1)}, bf16[256,2048]{1,0:T(8,128)(2,1)}, u32[]{:S(2)}, u32[]{:S(2)}) collective-permute-start(bf16[256,2048]{1,0:T(8,128)(2,1)} %add_convert_fusion), channel_id=1, source_target_pairs={{0,2},{1,3},{2,0},{3,1},{4,6},{5,7},{6,4},{7,5},{8,10},{9,11},{10,... | collective-permute-start | bytes 3145736 | tf_op jit(solution)/shard_map/ppermute | solution.py:29
  356.3 5.4 %slice-start = ((s8[4325376]{0:T(1024)(128)(4,1)}), s8[4194304]{0:T(1024)(128)(4,1)S(1)}, s32[]{:S(2)}) async-start(s8[4325376]{0:T(1024)(128)(4,1)} %bitcast.36), calls=%async_computation | async-start | bytes 8388608
  357.8 3.8 slice-start.1
  357.9 3.8 copy-start.20
  357.9 3.8 copy-start.21
  361.6 48.2 %collective-permute-start.23 = (f32[256,2048]{1,0:T(8,128)}, f32[256,2048]{1,0:T(8,128)}, u32[]{:S(2)}, u32[]{:S(2)}) collective-permute-start(f32[256,2048]{1,0:T(8,128)} %get-tuple-element.98), channel_id=1, source_target_pairs={{0,1},{1,0},{2,3},{3,2},{4,5},{5,4},{6,7},{7,6},{8,9},{9,8},{10,11... | collective-permute-start | bytes 6291464 | tf_op jit(solution)/shard_map/ppermute | solution.py:29
  361.7 13.8 %copy-start.7 = (bf16[512,2048]{1,0:T(8,128)(2,1)S(1)}, bf16[512,2048]{1,0:T(8,128)(2,1)}, u32[]{:S(2)}) copy-start(bf16[512,2048]{1,0:T(8,128)(2,1)} %x_ref.1) | copy-start | bytes 6291460
  361.7 13.8 %copy-start.30 = (f32[2048]{0:T(1024)S(1)}, f32[2048]{0:T(1024)}, u32[]{:S(2)}) copy-start(f32[2048]{0:T(1024)} %param.14) | copy-start | bytes 24580
  361.7 13.8 %copy-start.36 = (f32[256]{0:T(256)S(1)}, f32[256]{0:T(256)}, u32[]{:S(2)}) copy-start(f32[256]{0:T(256)} %add_rsqrt_fusion) | copy-start | bytes 3076
  378.0 6.6 %collective-permute-start.26 = (f32[2,2048]{1,0:T(2,128)S(1)}, f32[2,2048]{1,0:T(2,128)S(1)}, u32[]{:S(2)}, u32[]{:S(2)}) collective-permute-start(f32[2,2048]{1,0:T(2,128)S(1)} %pad_maximum_fusion.14), channel_id=1, source_target_pairs={{0,1},{1,0},{2,3},{3,2},{4,5},{5,4},{6,7},{7,6},{8,9},{9,8},{10,11... | collective-permute-start | bytes 49160 | tf_op jit(solution)/shard_map/ppermute | solution.py:29
  378.8 6.4 %copy-start.10 = (f32[1024,640]{0,1:T(8,128)S(1)}, f32[1024,640]{0,1:T(8,128)}, u32[]{:S(2)}) copy-start(f32[1024,640]{0,1:T(8,128)} %copy-done.9) | copy-start | bytes 7864324
  384.1 29.1 %collective-permute-start.25 = (f32[256,2048]{1,0:T(8,128)}, f32[256,2048]{1,0:T(8,128)}, u32[]{:S(2)}, u32[]{:S(2)}) collective-permute-start(f32[256,2048]{1,0:T(8,128)} %get-tuple-element.96), channel_id=1, source_target_pairs={{0,1},{1,0},{2,3},{3,2},{4,5},{5,4},{6,7},{7,6},{8,9},{9,8},{10,11... | collective-permute-start | bytes 6291464 | tf_op jit(solution)/shard_map/ppermute | solution.py:29
  384.6 4.1 collective-permute-start.27
  386.9 17.5 %collective-permute-start.34 = (bf16[256,640]{0,1:T(8,128)(2,1)S(1)}, bf16[256,640]{0,1:T(8,128)(2,1)S(1)}, u32[]{:S(2)}, u32[]{:S(2)}) collective-permute-start(bf16[256,640]{0,1:T(8,128)(2,1)S(1)} %slice.147), channel_id=1, source_target_pairs={{0,16},{8,24},{16,0},{24,8},{1,17},{9,25},{17,1},{25,9},{2,18},{10... | collective-permute-start | bytes 983048 | tf_op jit(solution)/shard_map/ppermute | solution.py:29
  388.7 15.8 %collective-permute-start.28 = (f32[2,2048]{1,0:T(2,128)S(1)}, f32[2,2048]{1,0:T(2,128)S(1)}, u32[]{:S(2)}, u32[]{:S(2)}) collective-permute-start(f32[2,2048]{1,0:T(2,128)S(1)} %fusion.85), channel_id=1, source_target_pairs={{0,8},{8,0},{16,24},{24,16},{1,9},{9,1},{17,25},{25,17},{2,10},{10... | collective-permute-start | bytes 49160 | tf_op jit(solution)/shard_map/ppermute | solution.py:29
  404.5 4.7 %collective-permute-start.29 = (f32[2,2048]{1,0:T(2,128)S(1)}, f32[2,2048]{1,0:T(2,128)S(1)}, u32[]{:S(2)}, u32[]{:S(2)}) collective-permute-start(f32[2,2048]{1,0:T(2,128)S(1)} %add.213), channel_id=1, source_target_pairs={{0,16},{8,24},{16,0},{24,8},{1,17},{9,25},{17,1},{25,9},{2,18},{10... | collective-permute-start | bytes 49160 | tf_op jit(solution)/shard_map/ppermute | solution.py:29
  409.8 3.3 copy-start.13
  (21 other events, 42.0 us)
where the time goes:
time: 420 us; the launch traced here: 417 us
  waiting for transfers between devices  131 us (31%)
  Pallas kernels  120 us (29%)
  starting transfers between devices  55.5 us (13%)
  other arithmetic  44.1 us (10%)
  local copies, waits for them, and re-layouts  39.5 us (9%)
  matrix products  25 us (6%)
    ppermute x41, waiting for transfers between devices, swap(): return lax.ppermute(value, axis, [(i, i ^ mask) for i in range(size)])  131 us
    pallas_call x1, Pallas kernels, far_rows(): pl.pallas_call(functools.partial(far_kernel, count=count, width=width, ti...  66.5 us
    ppermute x41, starting transfers between devices, swap(): return lax.ppermute(value, axis, [(i, i ^ mask) for i in range(size)])  55.5 us
    pallas_call x1, Pallas kernels, own_rows(): pl.pallas_call(functools.partial(own_kernel, tile=256), in_specs=[vmem, v...  25.5 us
    dot_general x13, matrix products, contract(): lax.dot_general(left_side, right_side, (((left_dim,), (right_dim,)), ((),...  25 us
    unnamed x92, local copies, waits for them, and re-layouts  19.6 us
    pallas_call x1, Pallas kernels, attend_back(): pl.pallas_call(functools.partial(backward_kernel, window=window), out_sha...  11.9 us
    dynamic_update_slice x2, other arithmetic, whole_rows(): out = lax.dynamic_update_slice_in_dim(out, value, core * half, 0)  9.07 us
  transfers between devices with their start and end apart: 41, of which 13 were waited for; matrix products, arithmetic and copies ran while one was open for 20% of the time, Pallas kernels for 25%

commit v1 on v0

--- a/solution.py
+++ b/solution.py
@@ -13,6 +13,7 @@
 BF = jnp.bfloat16
 F32 = jnp.float32
 QB = 128
+BRIEF = pl.CostEstimate(flops=1, bytes_accessed=1, transcendentals=0)
 
 
 def contract(left_side, right_side, left_dim, right_dim):
@@ -53,6 +54,63 @@
     return jnp.where(
         low, -pltpu.roll(values, width - HEAD // 2, 1), pltpu.roll(values, HEAD // 2, 1)
     )
+
+
+def mate(axis, mask):
+    return {axis: lax.axis_index(axis) ^ mask}
+
+
+def greet(routes):
+    barrier = pltpu.get_barrier_semaphore()
+    distinct = sorted(set(routes))
+    for axis, mask in distinct:
+        pl.semaphore_signal(
+            barrier, inc=1, device_id=mate(axis, mask), device_id_type=pl.DeviceIdType.MESH
+        )
+    pl.semaphore_wait(barrier, len(distinct))
+
+
+def link(src, dst, sent, got, slot, route):
+    return pltpu.make_async_remote_copy(
+        src_ref=src,
+        dst_ref=dst,
+        send_sem=sent.at[slot],
+        recv_sem=got.at[slot],
+        device_id=mate(*route),
+        device_id_type=pl.DeviceIdType.MESH,
+    )
+
+
+def links(sources, landings, sent, got, routes, base=0):
+    return [
+        link(src, dst, sent, got, base + k, route)
+        for k, (src, dst, route) in enumerate(zip(sources, landings, routes))
+    ]
+
+
+def exchange_kernel(*refs, routes):
+    n = len(routes)
+    greet(routes)
+    copies = links(refs[:n], refs[n : 2 * n], *refs[2 * n :], routes)
+    for copy in copies:
+        copy.start()
+    for copy in copies:
+        copy.wait()
+
+
+def exchange(carried, collective_id, name):
+    arrays = [value for value, _ in carried]
+    anywhere = pl.BlockSpec(memory_space=pl.ANY)
+    return pl.pallas_call(
+        functools.partial(exchange_kernel, routes=tuple(route for _, route in carried)),
+        in_specs=[anywhere] * len(arrays),
+        out_specs=[anywhere] * len(arrays),
+        out_shape=[jax.ShapeDtypeStruct(a.shape, a.dtype) for a in arrays],
+        scratch_shapes=[pltpu.SemaphoreType.DMA((len(arrays),))] * 2,
+        compiler_params=pltpu.CompilerParams(collective_id=collective_id, has_side_effects=True),
+        cost_estimate=BRIEF,
+        name=name,
+    )(*arrays)
 
 
 def enter_kernel(x_ref, gain_ref, wq_ref, wkv_ref, cos_ref, sin_ref, a_ref, q_ref, kv_ref):
@@ -98,6 +156,7 @@
             jax.ShapeDtypeStruct((rows, wq.shape[1]), BF),
             jax.ShapeDtypeStruct((rows, 128), BF),
         ],
+        cost_estimate=BRIEF,
         name="enter",
     )(tokens, gain, wq, wkv, cos, sin)
 
@@ -172,6 +231,7 @@
         in_specs=[pl.BlockSpec(memory_space=pltpu.VMEM)] * 4,
         out_specs=[pl.BlockSpec(memory_space=pltpu.VMEM)] * 2,
         scratch_shapes=[pltpu.VMEM((count * rows, 128), BF)] * 4,
+        cost_estimate=BRIEF,
         name="attend",
     )(q, kv, seg_col, seg_row)
 
@@ -263,6 +323,7 @@
         out_specs=[pl.BlockSpec(memory_space=pltpu.VMEM)] * 3,
         scratch_shapes=[pltpu.VMEM((count * rows, 128), BF)] * 4
         + [pltpu.VMEM((count * rows, 128), F32)] * 2,
+        cost_estimate=BRIEF,
         name="attend_back",
     )(q, hb, kv, lse, seg_col, seg_row, cos, sin)
 
@@ -308,17 +369,22 @@
     wg_hbm,
     wu_hbm,
     wd_hbm,
+    sources,
     h_ref,
     gb_ref,
     ub_ref,
     send_ref,
     keep_ref,
+    landings,
     wg_ref,
     wu_ref,
     wd_ref,
     sems,
+    sent,
+    got,
     *,
     tile,
+    routes,
 ):
     rows, d = m_ref.shape
     half = rows // 2
@@ -339,6 +405,10 @@
     for c in range(full + (1 if tail else 0)):
         for copy in copies(c, STEP if c < full else tail):
             copy.start()
+    greet(routes)
+    carried = links(sources, landings, sent, got, routes)
+    for copy in carried:
+        copy.start()
 
     def chunk(c, w):
         for copy in copies(c, w):
@@ -373,48 +443,151 @@
         return carry
 
     lax.fori_loop(0, d // STEP, back_step, 0)
-
-
-def own_rows(m, cot, wg, wu, wd):
+    for copy in carried:
+        copy.wait()
+
+
+def own_rows(m, cot, wg, wu, wd, carried):
+    arrays = [value for value, _ in carried]
+    routes = tuple(route for _, route in carried)
     rows, d = m.shape
     width = wg.shape[1]
     out = jax.ShapeDtypeStruct((rows, width), BF)
     vmem = pl.BlockSpec(memory_space=pltpu.VMEM)
     hbm = pl.BlockSpec(memory_space=pl.ANY)
     return pl.pallas_call(
-        functools.partial(own_kernel, tile=256),
-        in_specs=[vmem, vmem, hbm, hbm, hbm],
-        out_specs=[vmem] * 5,
+        functools.partial(own_kernel, tile=256, routes=routes),
+        in_specs=[vmem, vmem, hbm, hbm, hbm, [hbm] * len(arrays)],
+        out_specs=[vmem] * 5 + [[hbm] * len(arrays)],
         out_shape=[out] * 3
-        + [jax.ShapeDtypeStruct((rows // 2, d), BF), jax.ShapeDtypeStruct((rows // 2, d), F32)],
+        + [jax.ShapeDtypeStruct((rows // 2, d), BF), jax.ShapeDtypeStruct((rows // 2, d), F32)]
+        + [[jax.ShapeDtypeStruct(a.shape, a.dtype) for a in arrays]],
         scratch_shapes=[pltpu.VMEM((d, width), BF)] * 2
-        + [pltpu.VMEM((width, d), BF), pltpu.SemaphoreType.DMA((3, pl.cdiv(width, STEP)))],
-        compiler_params=pltpu.CompilerParams(vmem_limit_bytes=58 << 20),
-        cost_estimate=pl.CostEstimate(
-            flops=10 * rows * d * width,
-            bytes_accessed=6 * d * width + 10 * rows * d + 6 * rows * width,
-            transcendentals=rows * width,
+        + [pltpu.VMEM((width, d), BF), pltpu.SemaphoreType.DMA((3, pl.cdiv(width, STEP)))]
+        + [pltpu.SemaphoreType.DMA((len(arrays),))] * 2,
+        compiler_params=pltpu.CompilerParams(
+            vmem_limit_bytes=58 << 20, collective_id=1, has_side_effects=True
         ),
+        cost_estimate=BRIEF,
         name="own_rows",
-    )(m, cot, wg, wu, wd)
-
-
-def far_kernel(*refs, count, width, tile, block, offsets, sliced):
+    )(m, cot, wg, wu, wd, arrays)
+
+
+def more_kernel(*refs, count, width, routes):
+    m, cot, refs = refs[:count], refs[count : 2 * count], refs[2 * count :]
+    wg_ref, wu_ref, wd_ref, hidden_ref = refs[:4]
+    n = len(routes)
+    sources, refs = refs[4 : 4 + n], refs[4 + n :]
+    h_ref, gb_ref, ub_ref, send_ref, keep_ref = refs[:5]
+    landings, (total, sent, got) = refs[5 : 5 + n], refs[5 + n :]
+    step = pl.program_id(0)
+    full, tail = divmod(width, STEP)
+    steps = full + (1 if tail else 0)
+    half = total.shape[0] // 2
+    lanes = 512
+
+    @pl.when(step == 0)
+    def _():
+        greet(routes)
+        for copy in links(sources, landings, sent, got, routes):
+            copy.start()
+        total[...] = jnp.zeros_like(total)
+
+    def body(w):
+        wg, wu, wd = wg_ref[:, :w], wu_ref[:, :w], wd_ref[:w, :]
+        at = 0
+        for i in range(count):
+            long = m[i].shape[0]
+            dst = slice(at, at + long)
+            h, gb, ub = gated(m[i][...], cot[i][...], wg, wu, wd)
+            h_ref[dst, :w] = h
+            gb_ref[dst, :w] = gb
+            ub_ref[dst, :w] = ub
+            at += long
+        for c in range(total.shape[1] // lanes):
+            cols = slice(c * lanes, (c + 1) * lanes)
+            total[:, cols] += contract(hidden_ref[:, :w], wd[:, cols], 1, 0)
+
+    if tail:
+        pl.when(step < full)(lambda: body(STEP))
+        pl.when(step == full)(lambda: body(tail))
+    else:
+        body(STEP)
+
+    @pl.when(step == steps - 1)
+    def _():
+        keep_ref[...] = total[:half]
+        send_ref[...] = total[half:].astype(BF)
+        for copy in links(sources, landings, sent, got, routes):
+            copy.wait()
+
+
+def more_rows(ms, cots, wg, wu, wd, hidden, carried):
+    count = len(ms)
+    d = ms[0].shape[1]
+    width = wg.shape[1]
+    rows = sum(m.shape[0] for m in ms)
+    own = hidden.shape[0]
+    fixed = lambda i: (0, 0)
+    col = lambda i: (0, i)
+    row = lambda i: (i, 0)
+    whole = lambda a: pl.BlockSpec(a.shape, fixed, pipeline_mode=pl.Buffered(1))
+    anywhere = pl.BlockSpec(memory_space=pl.ANY)
+    shape = jax.ShapeDtypeStruct
+    arrays = [value for value, _ in carried]
+    return pl.pallas_call(
+        functools.partial(
+            more_kernel, count=count, width=width, routes=tuple(route for _, route in carried)
+        ),
+        grid=(pl.cdiv(width, STEP),),
+        in_specs=[whole(a) for a in list(ms) + list(cots)]
+        + [pl.BlockSpec((d, STEP), col)] * 2
+        + [pl.BlockSpec((STEP, d), row), pl.BlockSpec((own, STEP), col)]
+        + [anywhere] * len(arrays),
+        out_specs=[pl.BlockSpec((rows, STEP), col)] * 3
+        + [pl.BlockSpec((own // 2, d), fixed)] * 2
+        + [anywhere] * len(arrays),
+        out_shape=[shape((rows, width), BF)] * 3
+        + [shape((own // 2, d), BF), shape((own // 2, d), F32)]
+        + [shape(a.shape, a.dtype) for a in arrays],
+        scratch_shapes=[pltpu.VMEM((own, d), F32)]
+        + [pltpu.SemaphoreType.DMA((len(arrays),))] * 2,
+        compiler_params=pltpu.CompilerParams(
+            vmem_limit_bytes=58 << 20, collective_id=3, has_side_effects=True
+        ),
+        cost_estimate=BRIEF,
+        name="more_rows",
+    )(*ms, *cots, wg, wu, wd, hidden, *arrays)
+
+
+def far_kernel(*refs, count, ready, width, tile, block, offsets, sliced, routes, cross):
     m, cot = refs[:count], refs[count : 2 * count]
     refs = refs[2 * count :]
     m_src, c_src = m, cot
     if sliced:
         m_src, c_src = refs[:count], refs[count : 2 * count]
         refs = refs[2 * count :]
-    wg_ref, wu_ref, wd_ref, h_own, gb_own, ub_own = refs[:6]
-    gk, uk, dk, sends = refs[6:10]
-    m_turned, c_turned, h_all, gb_all, ub_all = refs[10:]
+    wg_ref, wu_ref, wd_ref = refs[:3]
+    known = [refs[3:6], refs[6:9]]
+    refs = refs[9:]
+    n = len(routes)
+    sources, refs = refs[:n], refs[n:]
+    gk, uk, dk = refs[:3]
+    landings, refs = refs[3 : 3 + n], refs[3 + n :]
+    m_turned, c_turned, h_all, gb_all, ub_all, sends, gets, sent, got = refs
     step = pl.program_id(0)
-    rows = m[0].shape[0]
     first = gk.shape[0]
+    full, tail = divmod(width, STEP)
+    steps = full + (1 if tail else 0)
+
+    def carried():
+        return links(sources, landings, sent, got, routes, steps)
 
     @pl.when(step == 0)
     def _():
+        greet(list(routes) + [cross])
+        for copy in carried():
+            copy.start()
         if not sliced:
             dp, ctx = lax.axis_index("dp"), lax.axis_index("ctx")
             n_ctx = lax.axis_size("ctx")
@@ -433,13 +606,18 @@
                         dst[j * block : (j + 1) * block, at : at + long] = piece.T
                 at += long
 
+    def crossing(c, w):
+        return link(sends.at[c, :, :, :w], gets.at[c, :, :, :w], sent, got, c, cross)
+
     def body(w):
         wg, wu, wd = wg_ref[:, :w], wu_ref[:, :w], wd_ref[:w, :]
-        h_all[:rows, :w] = h_own[:, :w]
-        gb_all[:rows, :w] = gb_own[:, :w]
-        ub_all[:rows, :w] = ub_own[:, :w]
-        at = rows
-        for i in range(1, count):
+        at = 0
+        for some in known:
+            long = some[0].shape[0]
+            for src, dst in zip(some, (h_all, gb_all, ub_all)):
+                dst[at : at + long, :w] = src[:, :w]
+            at += long
+        for i in range(ready, count):
             long = m[i].shape[0]
             size = min(tile, long)
             for t in range(long // size):
@@ -450,67 +628,88 @@
                 gb_all[dst, :w] = gb
                 ub_all[dst, :w] = ub
             at += long
+        lanes = pl.ds(pl.multiple_of(step * STEP, STEP), w)
         for i, (src, keep) in enumerate(((gb_all, gk), (ub_all, uk))):
             grad = contract(m_turned[...], src[:, :w], 1, 0)
-            keep[:, :w] = grad[:first]
-            sends[i, :, :w] = grad[first:].astype(BF)
+            keep[:, lanes] = grad[:first]
+            sends[step, i, :, :w] = grad[first:].astype(BF)
         grad = contract(c_turned[...], h_all[:, :w], 1, 0)
-        dk[:w, :] = grad[:first].T
-        sends[2, :, :w] = grad[first:].astype(BF)
-
-    full, tail = divmod(width, STEP)
+        dk[lanes, :] = grad[:first].T
+        sends[step, 2, :, :w] = grad[first:].astype(BF)
+        crossing(step, w).start()
+
     if tail:
         pl.when(step < full)(lambda: body(STEP))
         pl.when(step == full)(lambda: body(tail))
     else:
         body(STEP)
 
-
-def far_rows(ms, cots, m_cols, cot_cols, wg, wu, wd, own, block, offsets):
+    @pl.when(step == steps - 1)
+    def _():
+        for c in range(steps):
+            w = STEP if c < full else tail
+            crossing(c, w).wait()
+            at = slice(c * STEP, c * STEP + w)
+            gk[:, at] += gets[c, 0, :, :w].astype(F32)
+            uk[:, at] += gets[c, 1, :, :w].astype(F32)
+            dk[at, :] += gets[c, 2, :, :w].astype(F32).T
+        for copy in carried():
+            copy.wait()
+
+
+def far_rows(ms, cots, m_cols, cot_cols, wg, wu, wd, known, ready, block, offsets, cross, carried):
     count = len(ms)
-    rows, d = ms[0].shape
+    d = ms[0].shape[1]
     width = wg.shape[1]
     total = sum(m.shape[0] for m in ms)
     wide = block * len(offsets)
     first = wide // 2
+    steps = pl.cdiv(width, STEP)
     fixed = lambda i: (0, 0)
     col = lambda i: (0, i)
     row = lambda i: (i, 0)
     whole = lambda a: pl.BlockSpec(a.shape, fixed, pipeline_mode=pl.Buffered(1))
+    anywhere = pl.BlockSpec(memory_space=pl.ANY)
     shape = jax.ShapeDtypeStruct
     extra = [] if m_cols is None else list(m_cols) + list(cot_cols)
+    arrays = [value for value, _ in carried]
+    routes = tuple(route for _, route in carried)
+    sems = pltpu.SemaphoreType.DMA((steps + len(carried),))
     return pl.pallas_call(
         functools.partial(
             far_kernel,
             count=count,
+            ready=ready,
             width=width,
             tile=512,
             block=block,
             offsets=offsets,
             sliced=m_cols is not None,
+            routes=routes,
+            cross=cross,
         ),
-        grid=(pl.cdiv(width, STEP),),
+        grid=(steps,),
         in_specs=[whole(a) for a in list(ms) + list(cots) + extra]
         + [pl.BlockSpec((d, STEP), col)] * 2
         + [pl.BlockSpec((STEP, d), row)]
-        + [pl.BlockSpec((rows, STEP), col)] * 3,
-        out_specs=[pl.BlockSpec((first, STEP), col)] * 2
-        + [
-            pl.BlockSpec((STEP, first), row),
-            pl.BlockSpec((3, first, STEP), lambda i: (0, 0, i)),
-        ],
+        + [pl.BlockSpec((a.shape[0], STEP), col) for a in known]
+        + [anywhere] * len(carried),
+        out_specs=[pl.BlockSpec((first, width), fixed)] * 2
+        + [pl.BlockSpec((width, first), fixed)]
+        + [anywhere] * len(carried),
         out_shape=[shape((first, width), F32)] * 2
-        + [shape((width, first), F32), shape((3, first, width), BF)],
+        + [shape((width, first), F32)]
+        + [shape(a.shape, a.dtype) for a in arrays],
         scratch_shapes=[pltpu.VMEM((wide, total), BF)] * 2
-        + [pltpu.VMEM((total, STEP), BF)] * 3,
-        compiler_params=pltpu.CompilerParams(vmem_limit_bytes=60 << 20),
-        cost_estimate=pl.CostEstimate(
-            flops=6 * (total - rows) * d * width + 6 * total * wide * width,
-            bytes_accessed=6 * d * width + 4 * total * d + 6 * rows * width,
-            transcendentals=(total - rows) * width,
+        + [pltpu.VMEM((total, STEP), BF)] * 3
+        + [pltpu.VMEM((steps, 3, first, STEP), BF)] * 2
+        + [sems] * 2,
+        compiler_params=pltpu.CompilerParams(
+            vmem_limit_bytes=60 << 20, collective_id=0, has_side_effects=True
         ),
+        cost_estimate=BRIEF,
         name="far_rows",
-    )(*ms, *cots, *extra, wg, wu, wd, *own)
+    )(*ms, *cots, *extra, wg, wu, wd, *known, *arrays)
 
 
 def shards(
@@ -576,33 +775,18 @@
     def join_cores(value):
         return jnp.concatenate([value, swap(value, "tp", 1)], 0)
 
-    def share(value, bits):
-        pieces = [value]
-        for axis, mask in bits:
-            pieces = pieces + [swap(piece, axis, mask) for piece in pieces]
-        return join_cores(jnp.concatenate(pieces[1:], 0))
-
-    def share_group(by_ctx, by_dp, gate, gate_dp):
-        both = swap(after(by_dp, gate_dp), "ctx", 1)
-        return [
-            by_ctx,
-            swap(after(by_ctx, gate), "tp", 1),
-            by_dp,
-            swap(after(by_dp, gate_dp), "tp", 1),
-            both,
-            swap(both, "tp", 1),
-        ]
+    def with_core(pieces):
+        return [piece for value in pieces for piece in (value, swap(value, "tp", 1))]
 
     def mirror(value):
         return swap(value, "dp", n_dp - 1)
 
-    def tp_start(send, keep):
+    def tp_low(send, keep):
         total = keep + swap(send.astype(BF), "tp", 1).astype(F32)
         for axis, mask in tp_rest[:-1]:
             low = total.astype(BF)
             total = low.astype(F32) + swap(low, axis, mask).astype(F32)
-        low = total.astype(BF)
-        return low, swap(low, *tp_rest[-1])
+        return total.astype(BF)
 
     def tp_end(low, other):
         return low.astype(F32) + other.astype(F32)
@@ -645,28 +829,92 @@
     for axis, mask in bits_of("ctx"):
         kv_parts = kv_parts + [swap(piece, axis, mask) for piece in kv_parts]
     kv_all = jnp.stack(kv_parts, 0)
-    cot_start = after(cot_half, kv_all)
-    cot_ctx, cot_dp = swap(cot_start, "ctx", 1), mirror(cot_start)
+    quarter = half // 2
+    cot_dp_a = mirror(cot_half[:quarter])
+    kv_all = after(kv_all, cot_dp_a)
     heads_out, lse = attend(q_rot, kv_all, seg_col, seg_row, window)
     heads_mine, heads_other = own_half(heads_out), other_half(heads_out)
-    low_one, far_one = tp_start(
+    low_one = tp_low(
         contract(heads_other, output_weight, 1, 0), contract(heads_mine, output_weight, 1, 0)
+    )
+    last, side, across = tp_rest[-1], ("ctx", 1), ("dp", n_dp - 1)
+    far_one, cot_ctx, cot_dp_b = exchange(
+        [(low_one, last), (cot_half, side), (cot_half[quarter:], across)], 2, "exchange_one"
     )
     middle = x_half + tp_end(low_one, far_one)
     inverse_two = lax.rsqrt(jnp.mean(middle * middle, axis=-1, keepdims=True) + EPSILON)
     normed_two = middle * inverse_two
     mlp_half = (normed_two * mlp_gain).astype(BF)
-    mlp_ctx, mlp_dp = swap(mlp_half, "ctx", 1), mirror(mlp_half)
     mlp_own = join_cores(mlp_half)
-    cot_group = [cot_own] + share_group(cot_ctx, cot_dp, low_one, mlp_own)
-
-    hidden_own, gate_own, up_own, back_send, back_keep = own_rows(
-        mlp_own, cot_own, gate_weight, up_weight, down_weight
-    )
-    low_three, far_three = tp_start(back_send, back_keep)
-    mlp_group = [mlp_own] + share_group(mlp_ctx, mlp_dp, back_send, low_three)
-    hidden_own = after(hidden_own, low_three)
-
+    hidden_own, gate_own, up_own, back_send, back_keep, (mlp_ctx, mlp_dp_a) = own_rows(
+        mlp_own,
+        cot_own,
+        gate_weight,
+        up_weight,
+        down_weight,
+        [(mlp_half, side), (mlp_half[:quarter], across)],
+    )
+    low_three = tp_low(back_send, back_keep)
+    mlp_near, cot_near = with_core([mlp_ctx]), with_core([cot_ctx])
+    more = more_rows(
+        mlp_near,
+        cot_near,
+        gate_weight,
+        up_weight,
+        down_weight,
+        hidden_own,
+        [
+            (low_three, last),
+            (cot_dp_a, side),
+            (cot_dp_b, side),
+            (mlp_half[quarter:], across),
+        ],
+    )
+    down_send, down_keep, far_three, cot_both_a, cot_both_b, mlp_dp_b = more[3:]
+    mlp_both = [swap(after(piece, far_three), "ctx", 1) for piece in (mlp_dp_a, mlp_dp_b)]
+    low_two = tp_low(down_send, down_keep)
+    mlp_in_back = tp_end(low_three, far_three)
+    scaled = mlp_in_back * mlp_gain
+    middle_back = cot_half.astype(F32) + inverse_two * (
+        scaled - normed_two * jnp.mean(scaled * normed_two, axis=-1, keepdims=True)
+    )
+    mlp_gain_part = jnp.sum(mlp_in_back * normed_two, axis=0)
+    branch_half = middle_back.astype(BF)
+    branch_own = join_cores(branch_half)
+    heads_back = contract(branch_own, output_weight, 1, 1).astype(BF)
+
+    query_back, kv_part, kv_far = attend_back(
+        q_rot, heads_back, kv_all, lse, seg_col, seg_row, cos_table, sin_table, window
+    )
+    kv_back = join_keys(
+        kv_part,
+        [swap(kv_far[j - 1], "ctx", j) for j in range(1, n_ctx)],
+        cos_table,
+        sin_table,
+    )
+    qkv_back = jnp.concatenate([query_back, kv_back], 1)
+    back_mine, back_other = own_half(qkv_back), other_half(qkv_back)
+    q_width = query_back.shape[1]
+
+    def attn_back(part):
+        return contract(part[:, :q_width], query_weight, 1, 1) + contract(
+            part[:, q_width:], kv_weight, 1, 1
+        )
+
+    low_four = tp_low(
+        attn_back(after(back_other, *mlp_both)), attn_back(after(back_mine, *mlp_both))
+    )
+
+    flip = attn_share
+    attn_cols = both_halves(all_columns(attn_in, attn_reduce))
+    attn_cols_half = own_half(all_columns(attn_in, attn_reduce, flip))
+    heads_rel = jnp.concatenate([heads_mine, heads_other], 0)
+    branch_cols = all_columns(branch_own, attn_reduce)
+    branch_cols_half = all_columns(branch_half, attn_reduce, flip)
+    back_rel = jnp.concatenate([back_mine, back_other], 0)
+
+    mlp_group = [mlp_own] + mlp_near + with_core([mlp_dp_a, mlp_dp_b] + mlp_both)
+    cot_group = [cot_own] + cot_near + with_core([cot_dp_a, cot_dp_b, cot_both_a, cot_both_b])
     offsets = tuple(
         (
             sum(mask for axis, mask in chosen if axis == "dp"),
@@ -685,48 +933,26 @@
         gate_weight,
         up_weight,
         down_weight,
-        (hidden_own, gate_own, up_own),
+        [hidden_own, gate_own, up_own, *more[:3]],
+        3,
         block_width,
         offsets,
-    )
-
-    crossed = swap(far[3], *mlp_reduce[0])
-    mlp_in_back = tp_end(low_three, after(far_three, far[3]))
-    scaled = mlp_in_back * mlp_gain
-    middle_back = cot_half.astype(F32) + inverse_two * (
-        scaled - normed_two * jnp.mean(scaled * normed_two, axis=-1, keepdims=True)
-    )
-    mlp_gain_part = jnp.sum(mlp_in_back * normed_two, axis=0)
-    branch_half = middle_back.astype(BF)
-    branch_own = join_cores(branch_half)
-    heads_back = contract(branch_own, output_weight, 1, 1).astype(BF)
-
-    hidden_two = after(hidden_own, branch_half)
-    low_two, far_two = tp_start(
-        contract(hidden_two[half:], down_weight, 1, 0),
-        contract(hidden_two[:half], down_weight, 1, 0),
-    )
-
-    query_back, kv_part, kv_far = attend_back(
-        q_rot, heads_back, kv_all, lse, seg_col, seg_row, cos_table, sin_table, window
-    )
-    kv_back = join_keys(
-        kv_part,
-        [swap(kv_far[j - 1], "ctx", j) for j in range(1, n_ctx)],
-        cos_table,
-        sin_table,
-    )
-    qkv_back = jnp.concatenate([query_back, kv_back], 1)
-    back_mine, back_other = own_half(qkv_back), other_half(qkv_back)
-    q_width = query_back.shape[1]
-
-    def attn_back(part):
-        return contract(part[:, :q_width], query_weight, 1, 1) + contract(
-            part[:, q_width:], kv_weight, 1, 1
-        )
-
-    low_four, far_four = tp_start(attn_back(back_other), attn_back(back_mine))
-    layer_out = whole_rows(middle + tp_end(low_two, after(far_two, low_four)))
+        mlp_reduce[0],
+        [
+            (low_four, last),
+            (low_two, last),
+            (branch_cols_half, side),
+            (heads_rel, side),
+            (attn_cols_half, side),
+            (back_rel, side),
+        ],
+    )
+    gate_part, up_part, down_part, far_four, far_two = far[:5]
+    branch_cols_far, heads_far, attn_cols_far, back_far_rel = far[5:]
+    branch_cols_far, attn_cols_far = join_cores(branch_cols_far), join_cores(attn_cols_far)
+
+
+    layer_out = whole_rows(middle + tp_end(low_two, far_two))
     attn_in_back = tp_end(low_four, far_four)
     inverse_one = lax.rsqrt(jnp.mean(x_half * x_half, axis=-1, keepdims=True) + EPSILON)
     normed_one = x_half * inverse_one
@@ -735,23 +961,11 @@
         scaled_one - normed_one * jnp.mean(scaled_one * normed_one, axis=-1, keepdims=True)
     )
     tokens_grad = whole_rows(tokens_half)
-    crossed = after(crossed, low_four).astype(F32)
-    gate_grad = reduce_blocks(far[0] + crossed[0], mlp_reduce[1:], 0)
-    up_grad = reduce_blocks(far[1] + crossed[1], mlp_reduce[1:], 0)
-    down_grad = reduce_blocks(far[2] + crossed[2].T, mlp_reduce[1:], 1)
+    gate_grad = reduce_blocks(gate_part, mlp_reduce[1:], 0)
+    up_grad = reduce_blocks(up_part, mlp_reduce[1:], 0)
+    down_grad = reduce_blocks(down_part, mlp_reduce[1:], 1)
     gains = sum_gains(jnp.stack([jnp.sum(attn_in_back * normed_one, axis=0), mlp_gain_part]))
 
-    flip = attn_share
-    attn_cols = both_halves(all_columns(attn_in, attn_reduce))
-    attn_cols_far = share(
-        after(own_half(all_columns(attn_in, attn_reduce, flip)), mlp_group[1]), attn_share
-    )
-    heads_rel = jnp.concatenate([heads_mine, heads_other], 0)
-    heads_far = swap(after(heads_rel, mlp_group[1]), *attn_share[0])
-    branch_cols = all_columns(branch_own, attn_reduce)
-    branch_cols_far = share(all_columns(branch_half, attn_reduce, flip), attn_share)
-    back_rel = jnp.concatenate([back_mine, back_other], 0)
-    back_far_rel = swap(back_rel, *attn_share[0])
     output_grad = reduce_blocks(
         contract(heads_rel, branch_cols, 0, 0) + contract(heads_far, branch_cols_far, 0, 0),
         attn_reduce,

time: 420 us -> 369 us (0.88)
  Pallas kernels: 120 us -> 189 us
  waiting for transfers between devices: 131 us -> 64.1 us
  starting transfers between devices: 55.5 us -> 22.5 us
  matrix products: 25 us -> 16.7 us
  other arithmetic: 44.1 us -> 36.7 us
    pallas_call x2 -> x4, Pallas kernels: 92.1 us -> 160 us  [the longest x1 70.6 us: far_rows(): pl.pallas_call(functools.partial(far_kernel, count=count, ready=ready, wi...]
    ppermute x41 -> x33, waiting for transfers between devices: 131 us -> 64.1 us  [swap(): return lax.ppermute(value, axis, [(i, i ^ mask) for i in range(size)])]
    ppermute x41 -> x33, starting transfers between devices: 55.5 us -> 22.5 us  [swap(): return lax.ppermute(value, axis, [(i, i ^ mask) for i in range(size)])]
    dot_general x13 -> x11, matrix products: 25 us -> 16.7 us  [contract(): lax.dot_general(left_side, right_side, (((left_dim,), (right_dim,)), ((),...]
    unnamed x92 -> x112, local copies, waits for them, and re-layouts: 19.6 us -> 16.6 us
  transfers between devices with their start and end apart: 41 -> 33, of which waited for: 13 -> 9; matrix products, arithmetic and copies ran while one was open for 20% -> 16% of each run, Pallas kernels for 25% -> 6%
where the time goes in v1:
time: 369 us; the launch traced here: 366 us
  Pallas kernels  189 us (51%)
  waiting for transfers between devices  64.1 us (17%)
  other arithmetic  36.7 us (10%)
  local copies, waits for them, and re-layouts  35.4 us (10%)
  starting transfers between devices  22.5 us (6%)
  matrix products  16.7 us (5%)
    pallas_call x1, Pallas kernels, far_rows(): pl.pallas_call(functools.partial(far_kernel, count=count, ready=ready, wi...  70.6 us
    ppermute x33, waiting for transfers between devices, swap(): return lax.ppermute(value, axis, [(i, i ^ mask) for i in range(size)])  64.1 us
    pallas_call x1, Pallas kernels, own_rows(): pl.pallas_call(functools.partial(own_kernel, tile=256, routes=routes), in...  31.9 us
    pallas_call x1, Pallas kernels, more_rows(): pl.pallas_call(functools.partial(more_kernel, count=count, width=width, r...  31.2 us
    pallas_call x1, Pallas kernels, exchange(): pl.pallas_call(functools.partial(exchange_kernel, routes=tuple((route for...  26.6 us
    ppermute x33, starting transfers between devices, swap(): return lax.ppermute(value, axis, [(i, i ^ mask) for i in range(size)])  22.5 us
    dot_general x11, matrix products, contract(): lax.dot_general(left_side, right_side, (((left_dim,), (right_dim,)), ((),...  16.7 us
    unnamed x112, local copies, waits for them, and re-layouts  16.6 us
  transfers between devices with their start and end apart: 33, of which 9 were waited for; matrix products, arithmetic and copies ran while one was open for 16% of the time, Pallas kernels for 6%

profile of v1, /device:TPU:0, one launch (start us, length us, event | category | flops | bytes accessed | tf_op | source)
XLA Modules:
  0.0 365.6 jit_solution(13421343554860522836)
XLA Ops:
  0.7 2.4 constant_dynamic-slice_fusion
  3.1 5.1 %collective-permute-start.1 = (bf16[128,2048]{1,0:T(8,128)(2,1)}, bf16[128,2048]{1,0:T(8,128)(2,1)}, u32[]{:S(2)}, u32[]{:S(2)}) collective-permute-start(bf16[128,2048]{1,0:T(8,128)(2,1)} %get-tuple-element.141), channel_id=1, source_target_pairs={{0,24},{8,16},{16,8},{24,0},{1,25},{9,17},{17,9},{25,1},{2,26},{10... | collective-permute-start | bytes 1572872 | tf_op jit(solution)/shard_map/ppermute | solution.py:30
  9.2 1.3 pad_maximum_fusion.11
  11.1 1.1 pad_maximum_fusion.8.wkv_ref
  12.2 6.4 %enter.1 = (bf16[512,2048]{1,0:T(8,128)(2,1)}, bf16[512,512]{1,0:T(8,128)(2,1)}, bf16[512,128]{1,0:T(8,128)(2,1)}) custom-call(bf16[512,2048]{1,0:T(8,128)(2,1)} %x_ref.1, f32[1,2048]{1,0:T(1,128)} %bitcast.28, bf16[2048,512]{1,0:T(8,128)(2,1)} %wq_ref.1, bf16[2048,128]{1,0:T(8,128)(2,1)} %pad_maximum_fusion.8.wkv_ref, ...), custom_call_target="tpu_custom_call" | custom-call | flops 1 | bytes 1 | tf_op jit(solution)/shard_map/enter/pallas_call | solution.py:138
  18.6 1.5 collective-permute-start
  20.1 1.0 copy.28.segc_ref
  21.1 2.6 collective-permute-done
  23.7 1.6 pad_maximum_fusion.13.kv_ref
  25.4 8.1 %attend.1 = (bf16[512,512]{1,0:T(8,128)(2,1)}, f32[8,512]{1,0:T(8,128)}) custom-call(bf16[512,512]{1,0:T(8,128)(2,1)} %get-tuple-element.52.q_ref, bf16[2,512,128]{2,1,0:T(8,128)(2,1)} %pad_maximum_fusion.13.kv_ref, s32[1024,1]{1,0:T(8,128)} %copy.28.segc_ref, s32[1,1024]{1,0:T(1,128)} %segr_ref.3), custom_call_target="tpu_custom_call" | custom-call | flops 1 | bytes 1 | tf_op jit(solution)/shard_map/attend/pallas_call | solution.py:225
  33.5 1.2 constant_dynamic-slice_fusion.19
  35.5 1.5 constant_dynamic-slice_fusion.18
  37.0 1.2 collective-permute-done.2
  38.2 1.7 add_convert_fusion.2.refs_0_
  39.9 26.6 %exchange_one.1 = (bf16[256,2048]{1,0:T(8,128)(2,1)}, bf16[256,2048]{1,0:T(8,128)(2,1)}, bf16[128,2048]{1,0:T(8,128)(2,1)}) custom-call(bf16[256,2048]{1,0:T(8,128)(2,1)} %add_convert_fusion.2.refs_0_, bf16[256,2048]{1,0:T(8,128)(2,1)} %get-tuple-element.139.refs_1_, bf16[128,2048]{1,0:T(8,128)(2,1)} %get-tuple-element.140.refs_2_), custom_call_target="tpu_custom_call" | custom-call | flops 1 | bytes 1 | tf_op jit(solution)/shard_map/exchange_one/pallas_call | solution.py:104
  66.5 2.2 multiply_reduce_fusion.2
  69.1 1.6 copy-done.4
  71.4 1.6 pad_maximum_fusion.3.c_ref.refs_11_
  73.0 1.1 fusion.58
  74.1 1.6 pad_maximum_fusion.2.m_ref.refs_0_
  75.6 31.9 %own_rows.1 = (bf16[512,1408]{1,0:T(8,128)(2,1)}, bf16[512,1408]{1,0:T(8,128)(2,1)}, bf16[512,1408]{1,0:T(8,128)(2,1)}, bf16[256,2048]{1,0:T(8,128)(2,1)}, f32[2...) custom-call(bf16[512,2048]{1,0:T(8,128)(2,1)} %pad_maximum_fusion.2.m_ref.refs_0_, ...), custom_call_target="tpu_custom_call" | custom-call | flops 1 | bytes 1 | tf_op jit(solution)/shard_map/own_rows/pallas_call | solution.py:458
  108.1 2.3 collective-permute-done.6
  110.4 2.9 add_convert_fusion.1.refs_8_
  113.6 31.2 %more_rows.1 = (bf16[512,1408]{1,0:T(8,128)(2,1)}, bf16[512,1408]{1,0:T(8,128)(2,1)}, bf16[512,1408]{1,0:T(8,128)(2,1)}, bf16[256,2048]{1,0:T(8,128)(2,1)}, f32[...) custom-call(bf16[256,2048]{1,0:T(8,128)(2,1)} %get-tuple-element.57., ...), custom_call_target="tpu_custom_call" | custom-call | flops 1 | bytes 1 | tf_op jit(solution)/shard_map/more_rows/pallas_call | solution.py:538
  144.8 2.5 multiply_reduce_fusion
  147.3 1.8 fusion.56
  149.1 1.7 constant_dynamic-slice_fusion.8
  151.8 1.1 constant_dynamic-slice_fusion.4
  154.8 1.5 collective-permute-start.10
  156.3 3.6 fusion.15.hb_ref
  159.9 11.9 %attend_back.1 = (bf16[512,512]{1,0:T(8,128)(2,1)}, f32[512,128]{1,0:T(8,128)}, bf16[1,512,128]{2,1,0:T(8,128)(2,1)}) custom-call(bf16[512,512]{1,0:T(8,128)(2,1)} %get-tuple-element.52.q_ref, bf16[512,512]{1,0:T(8,128)(2,1)} %fusion.15.hb_ref, bf16[2,512,128]{2,1,0:T(8,128)(2,1)} %pad_maximum_fusion.13.kv_ref, f32[8,512]{1,0:T(8,128)} %get-tuple-element.77.lse_ref, ...), custom_call_target="tpu_custom_call" | custom-call | flops 1 | bytes 1 | tf_op jit(solution)/shard_map/attend_back/pallas_call | solution.py:315
  172.3 1.1 constant_dynamic-slice_fusion.17
  174.3 8.5 %collective-permute-done.19.refs_1_ = bf16[512,128]{1,0:T(8,128)(2,1)S(1)} collective-permute-done((bf16[512,128]{1,0:T(8,128)(2,1)}, bf16[512,128]{1,0:T(8,128)(2,1)S(1)}, u32[]{:S(2)}, u32[]{:S(2)}) %collective-permute-start.19) | collective-permute-done | bytes 131104 | tf_op jit(solution)/shard_map/ppermute | solution.py:30
  183.5 2.0 join_keys.1
  185.5 1.2 fusion.37
  187.4 1.5 fusion.45
  190.5 2.5 add_convert_fusion.refs_32_
  193.0 1.4 fusion.39
  194.4 2.1 fusion.23
  198.6 2.4 fusion.16
  201.9 1.8 fusion.4.refs_31_
  205.2 70.6 %far_rows.1 = (f32[256,1408]{1,0:T(8,128)}, f32[256,1408]{1,0:T(8,128)}, f32[1408,256]{1,0:T(8,128)}, bf16[256,2048]{1,0:T(8,128)(2,1)}, bf16[256,2048]{1,0:T(8,...) custom-call(bf16[512,2048]{1,0:T(8,128)(2,1)} %pad_maximum_fusion.2., ...), custom_call_target="tpu_custom_call" | custom-call | flops 1 | bytes 1 | tf_op jit(solution)/shard_map/far_rows/pallas_call | solution.py:678
  276.4 2.6 fusion.10
  279.7 1.1 copy-done.3
  281.3 4.2 %constant_dynamic-update-slice_fusion.1 = (f32[512,2048]{1,0:T(8,128)S(1)}, f32[256,2048]{1,0:T(8,128)}) fusion(f32[512,2048]{1,0:T(8,128)S(1)} %broadcast.63.clone.1, s32[]{:T(128)S(6)} %select_n.20, f32[256]{0:T(256)S(1)} %broadcast_multiply_fusion, bf16[512,2048]{1,0:T(8,128)(2,1)S(1)} %copy-done.11, f32[2048]{0:T(1024)S(1)} %copy-done.51, ...), kind=kLoop, calls=%fused_computation.117 | loop fusion | flops 10485760 | bytes 12603396 | tf_op jit(solution)/shard_map/dynamic_update_slice | solution.py:813
  286.4 1.1 copy-done.18
  288.5 1.9 constant_dynamic-update-slice_fusion.3
  292.6 1.4 collective-permute-start.31
  295.1 1.1 collective-permute-start.28
  296.2 1.0 collective-permute-start.25
  297.3 24.1 %collective-permute-done.25 = f32[2,2048]{1,0:T(2,128)S(1)} collective-permute-done((f32[2,2048]{1,0:T(2,128)S(1)}, f32[2,2048]{1,0:T(2,128)S(1)}, u32[]{:S(2)}, u32[]{:S(2)}) %collective-permute-start.25) | collective-permute-done | bytes 16416 | tf_op jit(solution)/shard_map/ppermute | solution.py:30
  321.3 1.5 collective-permute-start.26
  322.9 3.2 collective-permute-done.26
  326.3 1.5 collective-permute-start.32
  328.0 1.5 collective-permute-start.29
  330.2 15.9 %collective-permute-done.32 = bf16[512,256]{1,0:T(8,128)(2,1)S(1)} collective-permute-done((bf16[512,256]{1,0:T(8,128)(2,1)S(1)}, bf16[512,256]{1,0:T(8,128)(2,1)S(1)}, u32[]{:S(2)}, u32[]{:S(2)}) %collective-permute-start.32) | collective-permute-done | bytes 262176 | tf_op jit(solution)/shard_map/ppermute | solution.py:30
  346.9 6.0 %collective-permute-done.29 = bf16[256,640]{0,1:T(8,128)(2,1)S(1)} collective-permute-done((bf16[256,640]{0,1:T(8,128)(2,1)S(1)}, bf16[256,640]{0,1:T(8,128)(2,1)S(1)}, u32[]{:S(2)}, u32[]{:S(2)}) %collective-permute-start.29) | collective-permute-done | bytes 327712 | tf_op jit(solution)/shard_map/ppermute | solution.py:30
  353.1 1.0 copy.30
  354.8 3.3 constant_dynamic-update-slice_fusion
  358.1 1.9 constant_dynamic-update-slice_fusion.2
  360.1 1.1 copy.38
  361.2 1.2 copy-done.30
  362.4 1.1 copy.39
  364.3 1.1 copy.40
  (189 shorter events, 26.3 us)
Async XLA Ops:
  0.6 34.1 %copy-start = (bf16[512,2048]{1,0:T(8,128)(2,1)S(1)}, bf16[512,2048]{1,0:T(8,128)(2,1)}, u32[]{:S(2)}) copy-start(bf16[512,2048]{1,0:T(8,128)(2,1)} %param.18) | copy-start | bytes 6291460
  0.7 9.8 %copy-start.47 = (bf16[2048,64]{0,1:T(8,128)(2,1)S(1)}, bf16[2048,64]{0,1:T(8,128)(2,1)}, u32[]{:S(2)}) copy-start(bf16[2048,64]{0,1:T(8,128)(2,1)} %param.16) | copy-start | bytes 786436
  0.7 10.1 %copy-start.48 = (bf16[2048,64]{0,1:T(8,128)(2,1)S(1)}, bf16[2048,64]{0,1:T(8,128)(2,1)}, u32[]{:S(2)}) copy-start(bf16[2048,64]{0,1:T(8,128)(2,1)} %param.17) | copy-start | bytes 786436
  3.1 22.3 %collective-permute-start.1 = (bf16[128,2048]{1,0:T(8,128)(2,1)}, bf16[128,2048]{1,0:T(8,128)(2,1)}, u32[]{:S(2)}, u32[]{:S(2)}) collective-permute-start(bf16[128,2048]{1,0:T(8,128)(2,1)} %get-tuple-element.141), channel_id=1, source_target_pairs={{0,24},{8,16},{16,8},{24,0},{1,25},{9,17},{17,9},{25,1},{2,26},{10... | collective-permute-start | bytes 1572872 | tf_op jit(solution)/shard_map/ppermute | solution.py:30
  12.2 7.9 %copy-start.52 = (s32[1,1024]{1,0:T(1,128)S(1)}, s32[1,1024]{1,0:T(1,128)}, u32[]{:S(2)}) copy-start(s32[1,1024]{1,0:T(1,128)} %segr_ref.3) | copy-start | bytes 12292
  18.6 5.2 %collective-permute-start = (bf16[512,128]{1,0:T(8,128)(2,1)}, bf16[512,128]{1,0:T(8,128)(2,1)S(1)}, u32[]{:S(2)}, u32[]{:S(2)}) collective-permute-start(bf16[512,128]{1,0:T(8,128)(2,1)} %get-tuple-element.53), channel_id=1, source_target_pairs={{0,4},{4,0},{1,5},{5,1},{2,6},{6,2},{3,7},{7,3},{8,12},{12,8},{9,1... | collective-permute-start | bytes 393224 | tf_op jit(solution)/shard_map/ppermute | solution.py:30
  34.7 2.3 copy-start.24
  35.5 2.7 collective-permute-start.2
  39.9 26.6 %copy-start.12 = (bf16[256,2048]{1,0:T(8,128)(2,1)S(1)}, bf16[256,2048]{1,0:T(8,128)(2,1)}, u32[]{:S(2)}) copy-start(bf16[256,2048]{1,0:T(8,128)(2,1)} %add_convert_fusion.2.refs_0_) | copy-start | bytes 3145732
  66.4 2.3 copy-start.49
  68.7 78.6 %copy-start.2 = (f32[256,2048]{1,0:T(8,128)}, f32[256,2048]{1,0:T(8,128)S(1)}, u32[]{:S(2)}) copy-start(f32[256,2048]{1,0:T(8,128)S(1)} %get-tuple-element.124) | copy-start | bytes 6291460
  68.7 2.7 copy-start.22
  69.0 5.1 %copy-start.10 = (bf16[256,2048]{1,0:T(8,128)(2,1)}, bf16[256,2048]{1,0:T(8,128)(2,1)S(1)}, u32[]{:S(2)}) copy-start(bf16[256,2048]{1,0:T(8,128)(2,1)S(1)} %multiply_convert_fusion.sources_0_) | copy-start | bytes 3145732
  69.0 5.0 %collective-permute-start.3 = (bf16[256,2048]{1,0:T(8,128)(2,1)S(1)}, bf16[256,2048]{1,0:T(8,128)(2,1)S(1)}, u32[]{:S(2)}, u32[]{:S(2)}) collective-permute-start(bf16[256,2048]{1,0:T(8,128)(2,1)S(1)} %multiply_convert_fusion.sources_0_), channel_id=1, source_target_pairs={{0,1},{1,0},{2,3},{3,2},{4,5},{5,4},{6,7},{7,6},{8,9},{9,8},{10,11... | collective-permute-start | bytes 3145736 | tf_op jit(solution)/shard_map/ppermute | solution.py:30
  107.5 2.9 collective-permute-start.6
  107.6 5.7 %collective-permute-start.5 = (bf16[256,2048]{1,0:T(8,128)(2,1)}, bf16[256,2048]{1,0:T(8,128)(2,1)}, u32[]{:S(2)}, u32[]{:S(2)}) collective-permute-start(bf16[256,2048]{1,0:T(8,128)(2,1)} %get-tuple-element.58.refs_2_.refs_12_), channel_id=1, source_target_pairs={{0,1},{1,0},{2,3},{3,2},{4,5},{5,4},{6,7},{7,6},{8,9},{9,8},{10,11... | collective-permute-start | bytes 3145736 | tf_op jit(solution)/shard_map/ppermute | solution.py:30
  108.1 5.5 %collective-permute-start.4 = (bf16[256,2048]{1,0:T(8,128)(2,1)}, bf16[256,2048]{1,0:T(8,128)(2,1)}, u32[]{:S(2)}, u32[]{:S(2)}) collective-permute-start(bf16[256,2048]{1,0:T(8,128)(2,1)} %get-tuple-element.57.refs_0_.refs_1_), channel_id=1, source_target_pairs={{0,1},{1,0},{2,3},{3,2},{4,5},{5,4},{6,7},{7,6},{8,9},{9,8},{10,11... | collective-permute-start | bytes 3145736 | tf_op jit(solution)/shard_map/ppermute | solution.py:30
  144.8 2.5 copy-start.5
  144.8 2.5 copy-start.14
  149.1 7.2 %collective-permute-start.18 = (bf16[256,2048]{1,0:T(8,128)(2,1)}, bf16[256,2048]{1,0:T(8,128)(2,1)}, u32[]{:S(2)}, u32[]{:S(2)}) collective-permute-start(bf16[256,2048]{1,0:T(8,128)(2,1)} %fusion.56), channel_id=1, source_target_pairs={{0,1},{1,0},{2,3},{3,2},{4,5},{5,4},{6,7},{7,6},{8,9},{9,8},{10,11... | collective-permute-start | bytes 3145736 | tf_op jit(solution)/shard_map/ppermute | solution.py:30
  152.9 44.1 %collective-permute-start.14 = (bf16[128,2048]{1,0:T(8,128)(2,1)}, bf16[128,2048]{1,0:T(8,128)(2,1)}, u32[]{:S(2)}, u32[]{:S(2)}) collective-permute-start(bf16[128,2048]{1,0:T(8,128)(2,1)} %collective-permute-done.1.refs_9_.refs_14_), channel_id=1, source_target_pairs={{0,1},{1,0},{2,3},{3,2},{4,5},{5,4},{6,7},{7,6},{8,9},{9,8},{10,11... | collective-permute-start | bytes 1572872 | tf_op jit(solution)/shard_map/ppermute | solution.py:30
  154.2 35.4 %collective-permute-start.7 = (bf16[256,2048]{1,0:T(8,128)(2,1)}, bf16[256,2048]{1,0:T(8,128)(2,1)}, u32[]{:S(2)}, u32[]{:S(2)}) collective-permute-start(bf16[256,2048]{1,0:T(8,128)(2,1)} %get-tuple-element.64), channel_id=1, source_target_pairs={{0,1},{1,0},{2,3},{3,2},{4,5},{5,4},{6,7},{7,6},{8,9},{9,8},{10,11... | collective-permute-start | bytes 3145736 | tf_op jit(solution)/shard_map/ppermute | solution.py:30
  154.3 32.5 %collective-permute-start.12 = (bf16[128,2048]{1,0:T(8,128)(2,1)}, bf16[128,2048]{1,0:T(8,128)(2,1)}, u32[]{:S(2)}, u32[]{:S(2)}) collective-permute-start(bf16[128,2048]{1,0:T(8,128)(2,1)} %get-tuple-element.69.refs_5_), channel_id=1, source_target_pairs={{0,4},{4,0},{1,5},{5,1},{2,6},{6,2},{3,7},{7,3},{8,12},{12,8},{9,1... | collective-permute-start | bytes 1572872 | tf_op jit(solution)/shard_map/ppermute | solution.py:30
  154.8 32.1 %collective-permute-start.10 = (bf16[128,2048]{1,0:T(8,128)(2,1)}, bf16[128,2048]{1,0:T(8,128)(2,1)}, u32[]{:S(2)}, u32[]{:S(2)}) collective-permute-start(bf16[128,2048]{1,0:T(8,128)(2,1)} %get-tuple-element.68.refs_3_), channel_id=1, source_target_pairs={{0,4},{4,0},{1,5},{5,1},{2,6},{6,2},{3,7},{7,3},{8,12},{12,8},{9,1... | collective-permute-start | bytes 1572872 | tf_op jit(solution)/shard_map/ppermute | solution.py:30
  171.8 11.1 %collective-permute-start.19 = (bf16[512,128]{1,0:T(8,128)(2,1)}, bf16[512,128]{1,0:T(8,128)(2,1)S(1)}, u32[]{:S(2)}, u32[]{:S(2)}) collective-permute-start(bf16[512,128]{1,0:T(8,128)(2,1)} %bitcast.32), channel_id=1, source_target_pairs={{0,4},{4,0},{1,5},{5,1},{2,6},{6,2},{3,7},{7,3},{8,12},{12,8},{9,1... | collective-permute-start | bytes 393224 | tf_op jit(solution)/shard_map/ppermute | solution.py:30
  182.8 14.8 %collective-permute-start.15 = (bf16[128,2048]{1,0:T(8,128)(2,1)}, bf16[128,2048]{1,0:T(8,128)(2,1)}, u32[]{:S(2)}, u32[]{:S(2)}) collective-permute-start(bf16[128,2048]{1,0:T(8,128)(2,1)} %get-tuple-element.62.refs_10_.refs_16_), channel_id=1, source_target_pairs={{0,1},{1,0},{2,3},{3,2},{4,5},{5,4},{6,7},{7,6},{8,9},{9,8},{10,11... | collective-permute-start | bytes 1572872 | tf_op jit(solution)/shard_map/ppermute | solution.py:30
  185.5 3.3 copy-start.7
  186.8 11.3 %collective-permute-start.8 = (bf16[128,2048]{1,0:T(8,128)(2,1)}, bf16[128,2048]{1,0:T(8,128)(2,1)S(1)}, u32[]{:S(2)}, u32[]{:S(2)}) collective-permute-start(bf16[128,2048]{1,0:T(8,128)(2,1)} %get-tuple-element.68.refs_3_), channel_id=1, source_target_pairs={{0,1},{1,0},{2,3},{3,2},{4,5},{5,4},{6,7},{7,6},{8,9},{9,8},{10,11... | collective-permute-start | bytes 1572872 | tf_op jit(solution)/shard_map/ppermute | solution.py:30
  186.9 16.8 %collective-permute-start.9 = (bf16[128,2048]{1,0:T(8,128)(2,1)}, bf16[128,2048]{1,0:T(8,128)(2,1)S(1)}, u32[]{:S(2)}, u32[]{:S(2)}) collective-permute-start(bf16[128,2048]{1,0:T(8,128)(2,1)} %get-tuple-element.69.refs_5_), channel_id=1, source_target_pairs={{0,1},{1,0},{2,3},{3,2},{4,5},{5,4},{6,7},{7,6},{8,9},{9,8},{10,11... | collective-permute-start | bytes 1572872 | tf_op jit(solution)/shard_map/ppermute | solution.py:30
  189.7 8.6 %collective-permute-start.20 = (bf16[256,2048]{1,0:T(8,128)(2,1)S(1)}, bf16[256,2048]{1,0:T(8,128)(2,1)S(1)}, u32[]{:S(2)}, u32[]{:S(2)}) collective-permute-start(bf16[256,2048]{1,0:T(8,128)(2,1)S(1)} %fusion.5), channel_id=1, source_target_pairs={{0,1},{1,0},{2,3},{3,2},{4,5},{5,4},{6,7},{7,6},{8,9},{9,8},{10,11... | collective-permute-start | bytes 3145736 | tf_op jit(solution)/shard_map/ppermute | solution.py:30
  194.4 2.2 copy-start.16
  197.6 6.1 %collective-permute-start.16 = (bf16[128,2048]{1,0:T(8,128)(2,1)S(1)}, bf16[128,2048]{1,0:T(8,128)(2,1)S(1)}, u32[]{:S(2)}, u32[]{:S(2)}) collective-permute-start(bf16[128,2048]{1,0:T(8,128)(2,1)S(1)} %copy-done.34), channel_id=1, source_target_pairs={{0,1},{1,0},{2,3},{3,2},{4,5},{5,4},{6,7},{7,6},{8,9},{9,8},{10,11... | collective-permute-start | bytes 1572872 | tf_op jit(solution)/shard_map/ppermute | solution.py:30
  197.7 5.9 %collective-permute-start.17 = (bf16[128,2048]{1,0:T(8,128)(2,1)S(1)}, bf16[128,2048]{1,0:T(8,128)(2,1)S(1)}, u32[]{:S(2)}, u32[]{:S(2)}) collective-permute-start(bf16[128,2048]{1,0:T(8,128)(2,1)S(1)} %copy-done.35), channel_id=1, source_target_pairs={{0,1},{1,0},{2,3},{3,2},{4,5},{5,4},{6,7},{7,6},{8,9},{9,8},{10,11... | collective-permute-start | bytes 1572872 | tf_op jit(solution)/shard_map/ppermute | solution.py:30
  198.1 2.9 copy-start.36
  198.1 5.6 %collective-permute-start.13 = (bf16[128,2048]{1,0:T(8,128)(2,1)}, bf16[128,2048]{1,0:T(8,128)(2,1)S(1)}, u32[]{:S(2)}, u32[]{:S(2)}) collective-permute-start(bf16[128,2048]{1,0:T(8,128)(2,1)} %collective-permute-done.12.refs_9_), channel_id=1, source_target_pairs={{0,1},{1,0},{2,3},{3,2},{4,5},{5,4},{6,7},{7,6},{8,9},{9,8},{10,11... | collective-permute-start | bytes 1572872 | tf_op jit(solution)/shard_map/ppermute | solution.py:30
  198.2 5.5 %collective-permute-start.11 = (bf16[128,2048]{1,0:T(8,128)(2,1)}, bf16[128,2048]{1,0:T(8,128)(2,1)S(1)}, u32[]{:S(2)}, u32[]{:S(2)}) collective-permute-start(bf16[128,2048]{1,0:T(8,128)(2,1)} %collective-permute-done.10.refs_7_), channel_id=1, source_target_pairs={{0,1},{1,0},{2,3},{3,2},{4,5},{5,4},{6,7},{7,6},{8,9},{9,8},{10,11... | collective-permute-start | bytes 1572872 | tf_op jit(solution)/shard_map/ppermute | solution.py:30
  205.2 71.2 %copy-start.8 = (bf16[256,2048]{1,0:T(8,128)(2,1)S(1)}, bf16[256,2048]{1,0:T(8,128)(2,1)}, u32[]{:S(2)}) copy-start(bf16[256,2048]{1,0:T(8,128)(2,1)} %fusion.4.refs_31_) | copy-start | bytes 3145732
  205.2 71.2 %copy-start.51 = (f32[2048]{0:T(1024)S(1)}, f32[2048]{0:T(1024)}, u32[]{:S(2)}) copy-start(f32[2048]{0:T(1024)} %param.14) | copy-start | bytes 24580
  275.8 15.7 %collective-permute-start.30 = (bf16[256,1024]{1,0:T(8,128)(2,1)}, bf16[256,1024]{1,0:T(8,128)(2,1)S(1)}, u32[]{:S(2)}, u32[]{:S(2)}) collective-permute-start(bf16[256,1024]{1,0:T(8,128)(2,1)} %get-tuple-element.89), channel_id=1, source_target_pairs={{0,1},{1,0},{2,3},{3,2},{4,5},{5,4},{6,7},{7,6},{8,9},{9,8},{10,11... | collective-permute-start | bytes 1572872 | tf_op jit(solution)/shard_map/ppermute | solution.py:30
  275.9 18.1 %collective-permute-start.27 = (bf16[256,1024]{1,0:T(8,128)(2,1)}, bf16[256,1024]{1,0:T(8,128)(2,1)S(1)}, u32[]{:S(2)}, u32[]{:S(2)}) collective-permute-start(bf16[256,1024]{1,0:T(8,128)(2,1)} %get-tuple-element.86), channel_id=1, source_target_pairs={{0,1},{1,0},{2,3},{3,2},{4,5},{5,4},{6,7},{7,6},{8,9},{9,8},{10,11... | collective-permute-start | bytes 1572872 | tf_op jit(solution)/shard_map/ppermute | solution.py:30
  276.4 3.3 copy-start.11
  276.4 3.3 copy-start.15
  279.0 11.9 %collective-permute-start.23 = (f32[2,2048]{1,0:T(2,128)S(1)}, f32[2,2048]{1,0:T(2,128)S(1)}, u32[]{:S(2)}, u32[]{:S(2)}) collective-permute-start(f32[2,2048]{1,0:T(2,128)S(1)} %pad_maximum_fusion.14), channel_id=1, source_target_pairs={{0,1},{1,0},{2,3},{3,2},{4,5},{5,4},{6,7},{7,6},{8,9},{9,8},{10,11... | collective-permute-start | bytes 49160 | tf_op jit(solution)/shard_map/ppermute | solution.py:30
  279.1 2.2 copy-start.9
  285.5 69.3 %collective-permute-start.22 = (f32[256,2048]{1,0:T(8,128)}, f32[256,2048]{1,0:T(8,128)}, u32[]{:S(2)}, u32[]{:S(2)}) collective-permute-start(f32[256,2048]{1,0:T(8,128)} %get-tuple-element.120), channel_id=1, source_target_pairs={{0,1},{1,0},{2,3},{3,2},{4,5},{5,4},{6,7},{7,6},{8,9},{9,8},{10,11... | collective-permute-start | bytes 6291464 | tf_op jit(solution)/shard_map/ppermute | solution.py:30
  285.9 2.6 copy-start.32
  288.5 3.0 copy-start.28
  288.5 3.0 copy-start.45
  288.5 3.0 copy-start.46
  290.5 67.6 %collective-permute-start.21 = (f32[256,2048]{1,0:T(8,128)}, f32[256,2048]{1,0:T(8,128)}, u32[]{:S(2)}, u32[]{:S(2)}) collective-permute-start(f32[256,2048]{1,0:T(8,128)} %get-tuple-element.122), channel_id=1, source_target_pairs={{0,1},{1,0},{2,3},{3,2},{4,5},{5,4},{6,7},{7,6},{8,9},{9,8},{10,11... | collective-permute-start | bytes 6291464 | tf_op jit(solution)/shard_map/ppermute | solution.py:30
  291.0 5.2 %collective-permute-start.24 = (f32[2,2048]{1,0:T(2,128)S(1)}, f32[2,2048]{1,0:T(2,128)S(1)}, u32[]{:S(2)}, u32[]{:S(2)}) collective-permute-start(f32[2,2048]{1,0:T(2,128)S(1)} %fusion.55), channel_id=1, source_target_pairs={{0,4},{4,0},{1,5},{5,1},{2,6},{6,2},{3,7},{7,3},{8,12},{12,8},{9,1... | collective-permute-start | bytes 49160 | tf_op jit(solution)/shard_map/ppermute | solution.py:30
  291.6 2.4 copy-start.23
  291.6 2.4 copy-start.33
  291.6 2.4 copy-start.44
  292.6 33.5 %collective-permute-start.31 = (bf16[512,512]{1,0:T(8,128)(2,1)S(1)}, bf16[512,512]{1,0:T(8,128)(2,1)S(1)}, u32[]{:S(2)}, u32[]{:S(2)}) collective-permute-start(bf16[512,512]{1,0:T(8,128)(2,1)S(1)} %slice.120), channel_id=1, source_target_pairs={{0,8},{8,0},{16,24},{24,16},{1,9},{9,1},{17,25},{25,17},{2,10},{10... | collective-permute-start | bytes 1572872 | tf_op jit(solution)/shard_map/ppermute | solution.py:30
  295.1 32.7 %collective-permute-start.28 = (bf16[512,640]{0,1:T(8,128)(2,1)S(1)}, bf16[512,640]{0,1:T(8,128)(2,1)S(1)}, u32[]{:S(2)}, u32[]{:S(2)}) collective-permute-start(bf16[512,640]{0,1:T(8,128)(2,1)S(1)} %slice.119), channel_id=1, source_target_pairs={{0,8},{8,0},{16,24},{24,16},{1,9},{9,1},{17,25},{25,17},{2,10},{10... | collective-permute-start | bytes 1966088 | tf_op jit(solution)/shard_map/ppermute | solution.py:30
  296.2 25.1 %collective-permute-start.25 = (f32[2,2048]{1,0:T(2,128)S(1)}, f32[2,2048]{1,0:T(2,128)S(1)}, u32[]{:S(2)}, u32[]{:S(2)}) collective-permute-start(f32[2,2048]{1,0:T(2,128)S(1)} %fusion.72), channel_id=1, source_target_pairs={{0,8},{8,0},{16,24},{24,16},{1,9},{9,1},{17,25},{25,17},{2,10},{10... | collective-permute-start | bytes 49160 | tf_op jit(solution)/shard_map/ppermute | solution.py:30
  321.3 4.7 %collective-permute-start.26 = (f32[2,2048]{1,0:T(2,128)S(1)}, f32[2,2048]{1,0:T(2,128)S(1)}, u32[]{:S(2)}, u32[]{:S(2)}) collective-permute-start(f32[2,2048]{1,0:T(2,128)S(1)} %add.212), channel_id=1, source_target_pairs={{0,16},{8,24},{16,0},{24,8},{1,17},{9,25},{17,1},{25,9},{2,18},{10... | collective-permute-start | bytes 49160 | tf_op jit(solution)/shard_map/ppermute | solution.py:30
  326.3 19.7 %collective-permute-start.32 = (bf16[512,256]{1,0:T(8,128)(2,1)S(1)}, bf16[512,256]{1,0:T(8,128)(2,1)S(1)}, u32[]{:S(2)}, u32[]{:S(2)}) collective-permute-start(bf16[512,256]{1,0:T(8,128)(2,1)S(1)} %slice.122), channel_id=1, source_target_pairs={{0,16},{8,24},{16,0},{24,8},{1,17},{9,25},{17,1},{25,9},{2,18},{10... | collective-permute-start | bytes 786440 | tf_op jit(solution)/shard_map/ppermute | solution.py:30
  328.0 24.9 %collective-permute-start.29 = (bf16[256,640]{0,1:T(8,128)(2,1)S(1)}, bf16[256,640]{0,1:T(8,128)(2,1)S(1)}, u32[]{:S(2)}, u32[]{:S(2)}) collective-permute-start(bf16[256,640]{0,1:T(8,128)(2,1)S(1)} %slice.121), channel_id=1, source_target_pairs={{0,16},{8,24},{16,0},{24,8},{1,17},{9,25},{17,1},{25,9},{2,18},{10... | collective-permute-start | bytes 983048 | tf_op jit(solution)/shard_map/ppermute | solution.py:30
  354.8 3.3 copy-start.20
  360.0 3.5 copy-start.21
  360.0 2.4 copy-start.30
  362.4 3.0 copy-start.1
  (22 other events, 34.8 us)

commit v2 on v1

--- a/solution.py
+++ b/solution.py
@@ -245,17 +245,22 @@
     segr_ref,
     cos_ref,
     sin_ref,
+    sources,
     qb_ref,
     own_ref,
     far_ref,
+    landings,
     k0,
     k1,
     v0,
     v1,
     dk,
     dv,
+    sent,
+    got,
     *,
     window,
+    routes,
 ):
     rows = q_ref.shape[0]
     pairs = q_ref.shape[1] // 128
@@ -263,6 +268,10 @@
     ctx = lax.axis_index("ctx")
     core = lax.rem(lax.axis_index("tp"), 2)
     k_refs, v_refs = (k0, k1), (v0, v1)
+    greet(routes)
+    carried = links(sources, landings, sent, got, routes)
+    for copy in carried:
+        copy.start()
     lay_keys(ctx, kv_ref, k_refs, v_refs)
     dk[...] = jnp.zeros_like(dk)
     dv[...] = jnp.zeros_like(dv)
@@ -307,25 +316,34 @@
             own_ref[...] = both
         else:
             far_ref[j - 1] = both.astype(BF)
-
-
-def attend_back(q, hb, kv, lse, seg_col, seg_row, cos, sin, window):
+    for copy in carried:
+        copy.wait()
+
+
+def attend_back(q, hb, kv, lse, seg_col, seg_row, cos, sin, window, carried):
     rows, width = q.shape
     count = kv.shape[0]
+    arrays = [value for value, _ in carried]
+    anywhere = pl.BlockSpec(memory_space=pl.ANY)
     return pl.pallas_call(
-        functools.partial(backward_kernel, window=window),
+        functools.partial(
+            backward_kernel, window=window, routes=tuple(route for _, route in carried)
+        ),
         out_shape=[
             jax.ShapeDtypeStruct((rows, width), BF),
             jax.ShapeDtypeStruct((rows, 128), F32),
             jax.ShapeDtypeStruct((count - 1, rows, 128), BF),
+            [jax.ShapeDtypeStruct(a.shape, a.dtype) for a in arrays],
         ],
-        in_specs=[pl.BlockSpec(memory_space=pltpu.VMEM)] * 8,
-        out_specs=[pl.BlockSpec(memory_space=pltpu.VMEM)] * 3,
+        in_specs=[pl.BlockSpec(memory_space=pltpu.VMEM)] * 8 + [[anywhere] * len(arrays)],
+        out_specs=[pl.BlockSpec(memory_space=pltpu.VMEM)] * 3 + [[anywhere] * len(arrays)],
         scratch_shapes=[pltpu.VMEM((count * rows, 128), BF)] * 4
-        + [pltpu.VMEM((count * rows, 128), F32)] * 2,
+        + [pltpu.VMEM((count * rows, 128), F32)] * 2
+        + [pltpu.SemaphoreType.DMA((len(arrays),))] * 2,
+        compiler_params=pltpu.CompilerParams(collective_id=4, has_side_effects=True),
         cost_estimate=BRIEF,
         name="attend_back",
-    )(q, hb, kv, lse, seg_col, seg_row, cos, sin)
+    )(q, hb, kv, lse, seg_col, seg_row, cos, sin, arrays)
 
 
 def join_kernel(*refs):
@@ -364,8 +382,8 @@
 
 
 def own_kernel(
-    m_ref,
-    c_ref,
+    m_refs,
+    c_refs,
     wg_hbm,
     wu_hbm,
     wd_hbm,
@@ -386,8 +404,8 @@
     tile,
     routes,
 ):
-    rows, d = m_ref.shape
-    half = rows // 2
+    half, d = m_refs[0].shape
+    rows = 2 * half
     width = wg_ref.shape[1]
     full, tail = divmod(width, STEP)
 
@@ -402,13 +420,13 @@
             pltpu.make_async_copy(wd_hbm.at[at, :], wd_ref.at[at, :], sems.at[2, c]),
         ]
 
+    carried = links(sources, landings, sent, got, routes)
+    greet(routes)
+    for copy in carried:
+        copy.start()
     for c in range(full + (1 if tail else 0)):
         for copy in copies(c, STEP if c < full else tail):
             copy.start()
-    greet(routes)
-    carried = links(sources, landings, sent, got, routes)
-    for copy in carried:
-        copy.start()
 
     def chunk(c, w):
         for copy in copies(c, w):
@@ -417,7 +435,9 @@
         wg, wu, wd = wg_ref[:, at], wu_ref[:, at], wd_ref[at, :]
         for t in range(rows // tile):
             r = slice(t * tile, (t + 1) * tile)
-            h, gb, ub = gated(m_ref[r, :], c_ref[r, :], wg, wu, wd)
+            piece, at_row = divmod(t * tile, half)
+            local = slice(at_row, at_row + tile)
+            h, gb, ub = gated(m_refs[piece][local, :], c_refs[piece][local, :], wg, wu, wd)
             h_ref[r, at] = h
             gb_ref[r, at] = gb
             ub_ref[r, at] = ub
@@ -447,17 +467,17 @@
         copy.wait()
 
 
-def own_rows(m, cot, wg, wu, wd, carried):
+def own_rows(ms, cots, wg, wu, wd, carried):
     arrays = [value for value, _ in carried]
     routes = tuple(route for _, route in carried)
-    rows, d = m.shape
+    rows, d = 2 * ms[0].shape[0], ms[0].shape[1]
     width = wg.shape[1]
     out = jax.ShapeDtypeStruct((rows, width), BF)
     vmem = pl.BlockSpec(memory_space=pltpu.VMEM)
     hbm = pl.BlockSpec(memory_space=pl.ANY)
     return pl.pallas_call(
         functools.partial(own_kernel, tile=256, routes=routes),
-        in_specs=[vmem, vmem, hbm, hbm, hbm, [hbm] * len(arrays)],
+        in_specs=[[vmem] * 2, [vmem] * 2, hbm, hbm, hbm, [hbm] * len(arrays)],
         out_specs=[vmem] * 5 + [[hbm] * len(arrays)],
         out_shape=[out] * 3
         + [jax.ShapeDtypeStruct((rows // 2, d), BF), jax.ShapeDtypeStruct((rows // 2, d), F32)]
@@ -470,20 +490,21 @@
         ),
         cost_estimate=BRIEF,
         name="own_rows",
-    )(m, cot, wg, wu, wd, arrays)
+    )(ms, cots, wg, wu, wd, arrays)
 
 
 def more_kernel(*refs, count, width, routes):
     m, cot, refs = refs[:count], refs[count : 2 * count], refs[2 * count :]
-    wg_ref, wu_ref, wd_ref, hidden_ref = refs[:4]
+    wg_ref, wu_ref, wd_ref, hidden_ref, down_hbm = refs[:5]
     n = len(routes)
-    sources, refs = refs[4 : 4 + n], refs[4 + n :]
+    sources, refs = refs[5 : 5 + n], refs[5 + n :]
     h_ref, gb_ref, ub_ref, send_ref, keep_ref = refs[:5]
-    landings, (total, sent, got) = refs[5 : 5 + n], refs[5 + n :]
+    landings, (down_all, down_sem, sent, got) = refs[5 : 5 + n], refs[5 + n :]
+    down_copy = pltpu.make_async_copy(down_hbm, down_all, down_sem)
     step = pl.program_id(0)
     full, tail = divmod(width, STEP)
     steps = full + (1 if tail else 0)
-    half = total.shape[0] // 2
+    half = hidden_ref.shape[0] // 2
     lanes = 512
 
     @pl.when(step == 0)
@@ -491,7 +512,7 @@
         greet(routes)
         for copy in links(sources, landings, sent, got, routes):
             copy.start()
-        total[...] = jnp.zeros_like(total)
+        down_copy.start()
 
     def body(w):
         wg, wu, wd = wg_ref[:, :w], wu_ref[:, :w], wd_ref[:w, :]
@@ -504,9 +525,6 @@
             gb_ref[dst, :w] = gb
             ub_ref[dst, :w] = ub
             at += long
-        for c in range(total.shape[1] // lanes):
-            cols = slice(c * lanes, (c + 1) * lanes)
-            total[:, cols] += contract(hidden_ref[:, :w], wd[:, cols], 1, 0)
 
     if tail:
         pl.when(step < full)(lambda: body(STEP))
@@ -516,8 +534,16 @@
 
     @pl.when(step == steps - 1)
     def _():
-        keep_ref[...] = total[:half]
-        send_ref[...] = total[half:].astype(BF)
+        down_copy.wait()
+
+        def product(c, carry):
+            cols = pl.ds(pl.multiple_of(c * lanes, lanes), lanes)
+            total = contract(hidden_ref[...], down_all[:, cols], 1, 0)
+            keep_ref[:, cols] = total[:half]
+            send_ref[:, cols] = total[half:].astype(BF)
+            return carry
+
+        lax.fori_loop(0, keep_ref.shape[1] // lanes, product, 0)
         for copy in links(sources, landings, sent, got, routes):
             copy.wait()
 
@@ -542,7 +568,7 @@
         grid=(pl.cdiv(width, STEP),),
         in_specs=[whole(a) for a in list(ms) + list(cots)]
         + [pl.BlockSpec((d, STEP), col)] * 2
-        + [pl.BlockSpec((STEP, d), row), pl.BlockSpec((own, STEP), col)]
+        + [pl.BlockSpec((STEP, d), row), whole(hidden), anywhere]
         + [anywhere] * len(arrays),
         out_specs=[pl.BlockSpec((rows, STEP), col)] * 3
         + [pl.BlockSpec((own // 2, d), fixed)] * 2
@@ -550,17 +576,18 @@
         out_shape=[shape((rows, width), BF)] * 3
         + [shape((own // 2, d), BF), shape((own // 2, d), F32)]
         + [shape(a.shape, a.dtype) for a in arrays],
-        scratch_shapes=[pltpu.VMEM((own, d), F32)]
+        scratch_shapes=[pltpu.VMEM(wd.shape, BF), pltpu.SemaphoreType.DMA]
         + [pltpu.SemaphoreType.DMA((len(arrays),))] * 2,
         compiler_params=pltpu.CompilerParams(
             vmem_limit_bytes=58 << 20, collective_id=3, has_side_effects=True
         ),
         cost_estimate=BRIEF,
         name="more_rows",
-    )(*ms, *cots, wg, wu, wd, hidden, *arrays)
-
-
-def far_kernel(*refs, count, ready, width, tile, block, offsets, sliced, routes, cross):
+    )(*ms, *cots, wg, wu, wd, hidden, wd, *arrays)
+
+
+def far_kernel(*refs, longs, ready, width, tile, block, offsets, sliced, routes, cross, part_route):
+    count = len(longs)
     m, cot = refs[:count], refs[count : 2 * count]
     refs = refs[2 * count :]
     m_src, c_src = m, cot
@@ -571,40 +598,68 @@
     known = [refs[3:6], refs[6:9]]
     refs = refs[9:]
     n = len(routes)
+    summed = part_route is not None
+    if summed:
+        (part_send, part_keep), refs = refs[:2], refs[2:]
     sources, refs = refs[:n], refs[n:]
-    gk, uk, dk = refs[:3]
-    landings, refs = refs[3 : 3 + n], refs[3 + n :]
-    m_turned, c_turned, h_all, gb_all, ub_all, sends, gets, sent, got = refs
+    (gk, uk, dk), refs = refs[:3], refs[3:]
+    if summed:
+        part_out, refs = refs[0], refs[1:]
+    landings, refs = refs[:n], refs[n:]
+    m_far, c_far, m_cols, c_cols, m_turned, c_turned = refs[:6]
+    h_all, gb_all, ub_all, sends, gets, sent, got, row_sems, col_sems = refs[6:15]
+    part_got = refs[15] if summed else None
     step = pl.program_id(0)
     first = gk.shape[0]
     full, tail = divmod(width, STEP)
     steps = full + (1 if tail else 0)
+    begins = [sum(longs[:i]) for i in range(count)]
+    near = begins[ready]
+    total = sum(longs)
 
     def carried():
         return links(sources, landings, sent, got, routes, steps)
 
-    @pl.when(step == 0)
-    def _():
-        greet(list(routes) + [cross])
-        for copy in carried():
-            copy.start()
+    def part_copy():
+        return link(part_send, part_got, sent, got, steps + n, part_route)
+
+    def row_copies():
+        return [
+            pltpu.make_async_copy(
+                src[i], dst.at[pl.ds(begins[i] - near, longs[i]), :], row_sems.at[k, i]
+            )
+            for i in range(ready, count)
+            for k, (src, dst) in enumerate(((m, m_far), (cot, c_far)))
+        ]
+
+    def column_copies():
+        spans = [(0, None)]
         if not sliced:
             dp, ctx = lax.axis_index("dp"), lax.axis_index("ctx")
             n_ctx = lax.axis_size("ctx")
-            starts = [
-                pl.multiple_of(((dp ^ a) * n_ctx + (ctx ^ b)) * block, 128) for a, b in offsets
+            spans = [
+                (j * block, pl.multiple_of(((dp ^ a) * n_ctx + (ctx ^ b)) * block, 128))
+                for j, (a, b) in enumerate(offsets)
             ]
-        for src, dst in ((m_src, m_turned), (c_src, c_turned)):
-            at = 0
-            for ref in src:
-                long = ref.shape[0]
-                if sliced:
-                    dst[:, at : at + long] = ref[...].T
-                else:
-                    for j, start in enumerate(starts):
-                        piece = ref[:, pl.ds(start, block)]
-                        dst[j * block : (j + 1) * block, at : at + long] = piece.T
-                at += long
+        made = []
+        for i in range(count):
+            for k, (src, dst) in enumerate(((m_src, m_cols), (c_src, c_cols))):
+                for j, (at, start) in enumerate(spans):
+                    rows_at = pl.ds(begins[i], longs[i])
+                    if start is None:
+                        pair = src[i], dst.at[rows_at, :]
+                    else:
+                        pair = src[i].at[:, pl.ds(start, block)], dst.at[rows_at, pl.ds(at, block)]
+                    made.append(pltpu.make_async_copy(*pair, col_sems.at[k, i, j]))
+        return made
+
+    @pl.when(step == 0)
+    def _():
+        greet(list(routes) + [cross] + [part_route] * summed)
+        for copy in ([part_copy()] if summed else []) + carried() + row_copies() + column_copies():
+            copy.start()
+        for copy in row_copies():
+            copy.wait()
 
     def crossing(c, w):
         return link(sends.at[c, :, :, :w], gets.at[c, :, :, :w], sent, got, c, cross)
@@ -617,17 +672,22 @@
             for src, dst in zip(some, (h_all, gb_all, ub_all)):
                 dst[at : at + long, :w] = src[:, :w]
             at += long
-        for i in range(ready, count):
-            long = m[i].shape[0]
-            size = min(tile, long)
-            for t in range(long // size):
-                src = slice(t * size, (t + 1) * size)
-                dst = slice(at + t * size, at + (t + 1) * size)
-                h, gb, ub = gated(m[i][src, :], cot[i][src, :], wg, wu, wd)
-                h_all[dst, :w] = h
-                gb_all[dst, :w] = gb
-                ub_all[dst, :w] = ub
-            at += long
+        for t in range((total - near) // tile):
+            src = slice(t * tile, (t + 1) * tile)
+            dst = slice(near + t * tile, near + (t + 1) * tile)
+            h, gb, ub = gated(m_far[src, :], c_far[src, :], wg, wu, wd)
+            h_all[dst, :w] = h
+            gb_all[dst, :w] = gb
+            ub_all[dst, :w] = ub
+
+        @pl.when(step == 0)
+        def _():
+            for copy in column_copies():
+                copy.wait()
+            for src, dst in ((m_cols, m_turned), (c_cols, c_turned)):
+                for t in range(total // tile):
+                    dst[:, t * tile : (t + 1) * tile] = src[t * tile : (t + 1) * tile, :].T
+
         lanes = pl.ds(pl.multiple_of(step * STEP, STEP), w)
         for i, (src, keep) in enumerate(((gb_all, gk), (ub_all, uk))):
             grad = contract(m_turned[...], src[:, :w], 1, 0)
@@ -646,6 +706,9 @@
 
     @pl.when(step == steps - 1)
     def _():
+        if summed:
+            part_copy().wait()
+            part_out[...] = part_keep[...] + part_got[...].astype(F32)
         for c in range(steps):
             w = STEP if c < full else tail
             crossing(c, w).wait()
@@ -657,59 +720,226 @@
             copy.wait()
 
 
-def far_rows(ms, cots, m_cols, cot_cols, wg, wu, wd, known, ready, block, offsets, cross, carried):
-    count = len(ms)
-    d = ms[0].shape[1]
-    width = wg.shape[1]
-    total = sum(m.shape[0] for m in ms)
+def far_rows(
+    ms,
+    cots,
+    m_cols,
+    cot_cols,
+    weights,
+    known,
+    span,
+    ready,
+    block,
+    offsets,
+    cross,
+    part,
+    carried,
+    collective_id,
+    name,
+):
+    base, steps, width = span
+    longs = tuple(m.shape[0] for m in ms)
+    total, later = sum(longs), sum(longs[ready:])
+    d = weights[0].shape[0]
     wide = block * len(offsets)
     first = wide // 2
-    steps = pl.cdiv(width, STEP)
     fixed = lambda i: (0, 0)
-    col = lambda i: (0, i)
-    row = lambda i: (i, 0)
-    whole = lambda a: pl.BlockSpec(a.shape, fixed, pipeline_mode=pl.Buffered(1))
+    col = lambda i: (0, i + base)
+    row = lambda i: (i + base, 0)
     anywhere = pl.BlockSpec(memory_space=pl.ANY)
     shape = jax.ShapeDtypeStruct
     extra = [] if m_cols is None else list(m_cols) + list(cot_cols)
     arrays = [value for value, _ in carried]
-    routes = tuple(route for _, route in carried)
-    sems = pltpu.SemaphoreType.DMA((steps + len(carried),))
+    parts = [] if part is None else list(part[:2])
+    part_specs = [] if part is None else [
+        anywhere,
+        pl.BlockSpec(part[1].shape, fixed, pipeline_mode=pl.Buffered(1)),
+    ]
+    part_shapes = [] if part is None else [part[1].shape]
+    sems = pltpu.SemaphoreType.DMA((steps + len(carried) + 1,))
     return pl.pallas_call(
         functools.partial(
             far_kernel,
-            count=count,
+            longs=longs,
             ready=ready,
             width=width,
             tile=512,
             block=block,
             offsets=offsets,
             sliced=m_cols is not None,
-            routes=routes,
+            routes=tuple(route for _, route in carried),
             cross=cross,
+            part_route=None if part is None else part[2],
         ),
         grid=(steps,),
-        in_specs=[whole(a) for a in list(ms) + list(cots) + extra]
+        in_specs=[anywhere] * (2 * len(ms) + len(extra))
         + [pl.BlockSpec((d, STEP), col)] * 2
         + [pl.BlockSpec((STEP, d), row)]
         + [pl.BlockSpec((a.shape[0], STEP), col) for a in known]
+        + part_specs
         + [anywhere] * len(carried),
         out_specs=[pl.BlockSpec((first, width), fixed)] * 2
         + [pl.BlockSpec((width, first), fixed)]
+        + [pl.BlockSpec(a, fixed) for a in part_shapes]
         + [anywhere] * len(carried),
         out_shape=[shape((first, width), F32)] * 2
         + [shape((width, first), F32)]
+        + [shape(a, F32) for a in part_shapes]
         + [shape(a.shape, a.dtype) for a in arrays],
-        scratch_shapes=[pltpu.VMEM((wide, total), BF)] * 2
+        scratch_shapes=[pltpu.VMEM((later, d), BF)] * 2
+        + [pltpu.VMEM((total, wide), BF)] * 2
+        + [pltpu.VMEM((wide, total), BF)] * 2
         + [pltpu.VMEM((total, STEP), BF)] * 3
         + [pltpu.VMEM((steps, 3, first, STEP), BF)] * 2
-        + [sems] * 2,
+        + [sems] * 2
+        + [
+            pltpu.SemaphoreType.DMA((2, len(ms))),
+            pltpu.SemaphoreType.DMA((2, len(ms), len(offsets))),
+        ]
+        + [pltpu.VMEM(a, BF) for a in part_shapes],
         compiler_params=pltpu.CompilerParams(
-            vmem_limit_bytes=60 << 20, collective_id=0, has_side_effects=True
+            vmem_limit_bytes=60 << 20, collective_id=collective_id, has_side_effects=True
         ),
         cost_estimate=BRIEF,
-        name="far_rows",
-    )(*ms, *cots, *extra, wg, wu, wd, *known, *arrays)
+        name=name,
+    )(*ms, *cots, *extra, *weights, *known, *parts, *arrays)
+
+
+TILE = 32
+
+
+def finish_kernel(
+    low_two,
+    far_two,
+    middle,
+    low_four,
+    far_four,
+    middle_back,
+    x_ref,
+    gain_ref,
+    mlp_part,
+    sources,
+    layer_ref,
+    tokens_ref,
+    gains_ref,
+    landings,
+    parts,
+    other_parts,
+    blocks,
+    landed,
+    sent,
+    got,
+    peer_sent,
+    peer_got,
+    *,
+    routes,
+):
+    dp, ctx = lax.axis_index("dp"), lax.axis_index("ctx")
+    n_dp, n_ctx = lax.axis_size("dp"), lax.axis_size("ctx")
+    core = lax.rem(lax.axis_index("tp"), 2)
+    half, d = middle.shape
+    owners, _, block = blocks.shape
+    mesh = pl.DeviceIdType.MESH
+    near = ("tp", 1)
+    codes = [(a, b) for a in range(n_dp) for b in range(n_ctx)][1:]
+    ids = [{"dp": dp ^ a, "ctx": ctx ^ b} for a, b in codes]
+    barrier = pltpu.get_barrier_semaphore()
+    for peer in ids + [mate(*near)]:
+        pl.semaphore_signal(barrier, inc=1, device_id=peer, device_id_type=mesh)
+    pl.semaphore_wait(barrier, len(ids) + 1)
+    n = len(routes)
+    carried = links(sources, landings, sent, got, routes)
+    for copy in carried:
+        copy.start()
+
+    own = pl.ds(pl.multiple_of(core * half, half), half)
+    parts[0:1, :] = jnp.zeros((1, d), F32)
+    parts[1:2, :] = mlp_part[...]
+
+    def tokens_step(t, carry):
+        at = pl.ds(pl.multiple_of(t * TILE, TILE), TILE)
+        out_at = pl.ds(pl.multiple_of(core * half + t * TILE, TILE), TILE)
+        x = x_ref[at, :].astype(F32)
+        inverse = lax.rsqrt(jnp.mean(x * x, axis=-1, keepdims=True) + EPSILON)
+        normed = x * inverse
+        back = low_four[at, :].astype(F32) + far_four[at, :].astype(F32)
+        parts[0:1, :] += jnp.sum(back * normed, axis=0, keepdims=True)
+        scaled = back * gain_ref[...]
+        mean = jnp.mean(scaled * normed, axis=-1, keepdims=True)
+        tokens_ref[out_at, :] = middle_back[at, :] + inverse * (scaled - normed * mean)
+        return carry
+
+    lax.fori_loop(0, half // TILE, tokens_step, 0)
+    to_core = [
+        link(parts, other_parts, sent, got, n, near),
+        link(tokens_ref.at[own, :], tokens_ref.at[own, :], sent, got, n + 1, near),
+        link(layer_ref.at[own, :], layer_ref.at[own, :], sent, got, n + 2, near),
+    ]
+    to_core[0].start()
+    to_core[1].start()
+
+    def layer_step(t, carry):
+        at = pl.ds(pl.multiple_of(t * TILE, TILE), TILE)
+        out_at = pl.ds(pl.multiple_of(core * half + t * TILE, TILE), TILE)
+        layer_ref[out_at, :] = middle[at, :] + (
+            low_two[at, :].astype(F32) + far_two[at, :].astype(F32)
+        )
+        return carry
+
+    lax.fori_loop(0, half // TILE, layer_step, 0)
+    to_core[2].start()
+    to_core[0].wait()
+    for k in range(owners):
+        at = slice(k * block, (k + 1) * block)
+        blocks[k] = parts[:, at] + other_parts[:, at]
+    copies = [
+        pltpu.make_async_remote_copy(
+            src_ref=blocks.at[peer["dp"] * n_ctx + peer["ctx"]],
+            dst_ref=landed.at[k],
+            send_sem=peer_sent.at[k],
+            recv_sem=peer_got.at[k],
+            device_id=peer,
+            device_id_type=mesh,
+        )
+        for k, peer in enumerate(ids)
+    ]
+    for copy in copies:
+        copy.start()
+    for copy in copies:
+        copy.wait()
+    total = blocks[dp * n_ctx + ctx]
+    for k in range(len(ids)):
+        total = total + landed[k]
+    gains_ref[...] = total
+    for copy in to_core[1:] + carried:
+        copy.wait()
+
+
+def finish(values, gain, mlp_part, rows, carried):
+    d = values[2].shape[1]
+    owners = lax.axis_size("dp") * lax.axis_size("ctx")
+    block = d // owners
+    arrays = [value for value, _ in carried]
+    vmem = pl.BlockSpec(memory_space=pltpu.VMEM)
+    anywhere = pl.BlockSpec(memory_space=pl.ANY)
+    shape = jax.ShapeDtypeStruct
+    layer_out, tokens_grad, gains, landed = pl.pallas_call(
+        functools.partial(finish_kernel, routes=tuple(route for _, route in carried)),
+        in_specs=[vmem] * 9 + [[anywhere] * len(arrays)],
+        out_specs=[vmem] * 3 + [[anywhere] * len(arrays)],
+        out_shape=[shape((rows, d), F32)] * 2
+        + [shape((2, block), F32), [shape(a.shape, a.dtype) for a in arrays]],
+        scratch_shapes=[pltpu.VMEM((2, d), F32)] * 2
+        + [pltpu.VMEM((owners, 2, block), F32), pltpu.VMEM((owners - 1, 2, block), F32)]
+        + [pltpu.SemaphoreType.DMA((len(arrays) + 3,))] * 2
+        + [pltpu.SemaphoreType.DMA((owners - 1,))] * 2,
+        compiler_params=pltpu.CompilerParams(
+            vmem_limit_bytes=58 << 20, collective_id=5, has_side_effects=True
+        ),
+        cost_estimate=BRIEF,
+        name="finish",
+    )(*values, gain, mlp_part, arrays)
+    return layer_out, tokens_grad, gains, *landed
 
 
 def shards(
@@ -794,24 +1024,16 @@
     def after(value, *others):
         return lax.optimization_barrier((value,) + others)[0]
 
+    def halves(value, dim):
+        middle = value.shape[dim] // 2
+        keep = lax.slice_in_dim(value, 0, middle, axis=dim)
+        return keep, lax.slice_in_dim(value, middle, 2 * middle, axis=dim).astype(BF)
+
     def reduce_blocks(value, reduce_bits, dim):
         for axis, mask in reduce_bits:
-            middle = value.shape[dim] // 2
-            keep = lax.slice_in_dim(value, 0, middle, axis=dim)
-            send = lax.slice_in_dim(value, middle, 2 * middle, axis=dim).astype(BF)
+            keep, send = halves(value, dim)
             value = keep + swap(send, axis, mask).astype(F32)
         return value
-
-    def sum_gains(value):
-        value = value + swap(value, "tp", 1)
-        for axis, mask in every_bit:
-            value = value + swap(value, axis, mask)
-        return lax.dynamic_slice_in_dim(value, owner_start(()), block_width, 1)
-
-    def whole_rows(value):
-        out = jnp.zeros((rows, value.shape[1]), F32)
-        out = lax.dynamic_update_slice_in_dim(out, value, core * half, 0)
-        return lax.dynamic_update_slice_in_dim(out, swap(value, "tp", 1), (1 - core) * half, 0)
 
     seg_row = segments
     seg_col = jnp.swapaxes(segments, 0, 1)
@@ -819,7 +1041,7 @@
     cos_table, sin_table = rope_tables(query_pos, HEAD)
     kv_weight = jnp.concatenate([key_weight, value_weight], 1)
     cot_half = own_half(cotangent)
-    cot_own = jnp.concatenate([cot_half, other_half(cotangent)], 0)
+    cot_own = [cot_half, other_half(cotangent)]
     x_half = own_half(tokens).astype(F32)
 
     attn_in, q_rot, kv_own = enter(
@@ -830,31 +1052,50 @@
         kv_parts = kv_parts + [swap(piece, axis, mask) for piece in kv_parts]
     kv_all = jnp.stack(kv_parts, 0)
     quarter = half // 2
-    cot_dp_a = mirror(cot_half[:quarter])
-    kv_all = after(kv_all, cot_dp_a)
+    last, side, across = tp_rest[-1], ("ctx", 1), ("dp", n_dp - 1)
+
+    def own_quarter(value):
+        which = lax.rem(lax.div(lax.axis_index("tp"), last[1]), 2)
+        return lax.dynamic_slice_in_dim(value, which * quarter, quarter, 0)
+
+    cot_dp_q = mirror(own_quarter(cot_half))
+    cot_ctx_a = swap(cot_half[:quarter], *side)
+    attn_cols_half = own_half(all_columns(attn_in, attn_reduce, attn_share))
+    kv_all, attn_cols_half, *_ = lax.optimization_barrier(
+        (kv_all, attn_cols_half, cot_dp_q, cot_ctx_a)
+    )
+    attn_cols_far = swap(attn_cols_half, *side)
+    cot_dp_r = swap(cot_dp_q, *last)
     heads_out, lse = attend(q_rot, kv_all, seg_col, seg_row, window)
+    heads_out = after(heads_out, attn_cols_far, cot_dp_r)
     heads_mine, heads_other = own_half(heads_out), other_half(heads_out)
     low_one = tp_low(
         contract(heads_other, output_weight, 1, 0), contract(heads_mine, output_weight, 1, 0)
     )
-    last, side, across = tp_rest[-1], ("ctx", 1), ("dp", n_dp - 1)
-    far_one, cot_ctx, cot_dp_b = exchange(
-        [(low_one, last), (cot_half, side), (cot_half[quarter:], across)], 2, "exchange_one"
-    )
+    far_one, cot_ctx_b, cot_both_q = exchange(
+        [(low_one, last), (cot_half[quarter:], side), (cot_dp_q, side)], 2, "exchange_one"
+    )
+    cot_ctx = jnp.concatenate([cot_ctx_a, cot_ctx_b], 0)
     middle = x_half + tp_end(low_one, far_one)
     inverse_two = lax.rsqrt(jnp.mean(middle * middle, axis=-1, keepdims=True) + EPSILON)
     normed_two = middle * inverse_two
     mlp_half = (normed_two * mlp_gain).astype(BF)
-    mlp_own = join_cores(mlp_half)
-    hidden_own, gate_own, up_own, back_send, back_keep, (mlp_ctx, mlp_dp_a) = own_rows(
+    mlp_own = [mlp_half, swap(mlp_half, "tp", 1)]
+    hidden_own, gate_own, up_own, back_send, back_keep, arrived = own_rows(
         mlp_own,
         cot_own,
         gate_weight,
         up_weight,
         down_weight,
-        [(mlp_half, side), (mlp_half[:quarter], across)],
-    )
+        [
+            (mlp_half, side),
+            (own_quarter(mlp_half), across),
+            (cot_both_q, last),
+        ],
+    )
+    mlp_ctx, mlp_dp_q, cot_both_r = arrived
     low_three = tp_low(back_send, back_keep)
+    heads_rel = jnp.concatenate([heads_mine, heads_other], 0)
     mlp_near, cot_near = with_core([mlp_ctx]), with_core([cot_ctx])
     more = more_rows(
         mlp_near,
@@ -865,13 +1106,11 @@
         hidden_own,
         [
             (low_three, last),
-            (cot_dp_a, side),
-            (cot_dp_b, side),
-            (mlp_half[quarter:], across),
+            (mlp_dp_q, side),
+            (heads_rel, side),
         ],
     )
-    down_send, down_keep, far_three, cot_both_a, cot_both_b, mlp_dp_b = more[3:]
-    mlp_both = [swap(after(piece, far_three), "ctx", 1) for piece in (mlp_dp_a, mlp_dp_b)]
+    down_send, down_keep, far_three, mlp_both_q, heads_far = more[3:]
     low_two = tp_low(down_send, down_keep)
     mlp_in_back = tp_end(low_three, far_three)
     scaled = mlp_in_back * mlp_gain
@@ -883,38 +1122,31 @@
     branch_own = join_cores(branch_half)
     heads_back = contract(branch_own, output_weight, 1, 1).astype(BF)
 
-    query_back, kv_part, kv_far = attend_back(
-        q_rot, heads_back, kv_all, lse, seg_col, seg_row, cos_table, sin_table, window
-    )
-    kv_back = join_keys(
-        kv_part,
-        [swap(kv_far[j - 1], "ctx", j) for j in range(1, n_ctx)],
+    flip = attn_share
+    branch_cols = all_columns(branch_own, attn_reduce)
+    branch_cols_half = all_columns(branch_half, attn_reduce, flip)
+    query_back, kv_part, kv_far, (branch_cols_far, mlp_dp_r) = attend_back(
+        q_rot,
+        heads_back,
+        kv_all,
+        lse,
+        seg_col,
+        seg_row,
         cos_table,
         sin_table,
-    )
-    qkv_back = jnp.concatenate([query_back, kv_back], 1)
-    back_mine, back_other = own_half(qkv_back), other_half(qkv_back)
-    q_width = query_back.shape[1]
-
-    def attn_back(part):
-        return contract(part[:, :q_width], query_weight, 1, 1) + contract(
-            part[:, q_width:], kv_weight, 1, 1
-        )
-
-    low_four = tp_low(
-        attn_back(after(back_other, *mlp_both)), attn_back(after(back_mine, *mlp_both))
-    )
-
-    flip = attn_share
-    attn_cols = both_halves(all_columns(attn_in, attn_reduce))
-    attn_cols_half = own_half(all_columns(attn_in, attn_reduce, flip))
-    heads_rel = jnp.concatenate([heads_mine, heads_other], 0)
-    branch_cols = all_columns(branch_own, attn_reduce)
-    branch_cols_half = all_columns(branch_half, attn_reduce, flip)
-    back_rel = jnp.concatenate([back_mine, back_other], 0)
-
-    mlp_group = [mlp_own] + mlp_near + with_core([mlp_dp_a, mlp_dp_b] + mlp_both)
-    cot_group = [cot_own] + cot_near + with_core([cot_dp_a, cot_dp_b, cot_both_a, cot_both_b])
+        window,
+        [(branch_cols_half, side), (mlp_dp_q, last)],
+    )
+    mlp_both_r = swap(after(mlp_both_q, far_three), *last)
+    kv_far, query_back, *_ = lax.optimization_barrier((kv_far, query_back, mlp_both_r))
+    output_part = contract(heads_rel, branch_cols, 0, 0) + contract(
+        heads_far, join_cores(branch_cols_far), 0, 0
+    )
+    output_keep, output_send = halves(reduce_blocks(output_part, attn_reduce[:-2], 1), 1)
+    query_rel = jnp.concatenate([own_half(query_back), other_half(query_back)], 0)
+
+    mlp_group = mlp_own + mlp_near + with_core([mlp_dp_q, mlp_dp_r, mlp_both_q, mlp_both_r])
+    cot_group = cot_own + cot_near + with_core([cot_dp_q, cot_dp_r, cot_both_q, cot_both_r])
     offsets = tuple(
         (
             sum(mask for axis, mask in chosen if axis == "dp"),
@@ -925,57 +1157,92 @@
     aligned = block_width % 128 == 0
     m_cols = None if aligned else [all_columns(m, mlp_reduce) for m in mlp_group]
     c_cols = None if aligned else [all_columns(c, mlp_reduce) for c in cot_group]
-    far = far_rows(
-        mlp_group,
-        cot_group,
-        m_cols,
-        c_cols,
-        gate_weight,
-        up_weight,
-        down_weight,
-        [hidden_own, gate_own, up_own, *more[:3]],
-        3,
-        block_width,
-        offsets,
-        mlp_reduce[0],
-        [
-            (low_four, last),
-            (low_two, last),
-            (branch_cols_half, side),
-            (heads_rel, side),
-            (attn_cols_half, side),
-            (back_rel, side),
-        ],
-    )
-    gate_part, up_part, down_part, far_four, far_two = far[:5]
-    branch_cols_far, heads_far, attn_cols_far, back_far_rel = far[5:]
-    branch_cols_far, attn_cols_far = join_cores(branch_cols_far), join_cores(attn_cols_far)
-
-
-    layer_out = whole_rows(middle + tp_end(low_two, far_two))
-    attn_in_back = tp_end(low_four, far_four)
-    inverse_one = lax.rsqrt(jnp.mean(x_half * x_half, axis=-1, keepdims=True) + EPSILON)
-    normed_one = x_half * inverse_one
-    scaled_one = attn_in_back * attn_gain
-    tokens_half = middle_back + inverse_one * (
-        scaled_one - normed_one * jnp.mean(scaled_one * normed_one, axis=-1, keepdims=True)
-    )
-    tokens_grad = whole_rows(tokens_half)
+    hidden_width = gate_weight.shape[1]
+    early_steps = pl.cdiv(hidden_width, STEP) // 2
+    early_width = early_steps * STEP
+
+    def far_span(base, steps, width, part, carried, collective_id, name):
+        return far_rows(
+            mlp_group,
+            cot_group,
+            m_cols,
+            c_cols,
+            [gate_weight, up_weight, down_weight],
+            [hidden_own, gate_own, up_own, *more[:3]],
+            (base, steps, width),
+            4,
+            block_width,
+            offsets,
+            mlp_reduce[0],
+            part,
+            carried,
+            collective_id,
+            name,
+        )
+
+    early = far_span(
+        0,
+        early_steps,
+        early_width,
+        None,
+        [(kv_far[j - 1], ("ctx", j)) for j in range(1, n_ctx)]
+        + [(query_rel, side), (output_send, attn_reduce[-2]), (low_two, last)],
+        0,
+        "far_early",
+    )
+    output_near, far_two = early[-2:]
+    query_far = early[-3]
+    output_keep, output_send = halves(output_keep + output_near.astype(F32), 1)
+    kv_back = join_keys(kv_part, early[3 : 2 + n_ctx], cos_table, sin_table)
+    qkv_back = jnp.concatenate([query_back, kv_back], 1)
+    back_mine, back_other = own_half(qkv_back), other_half(qkv_back)
+    q_width = query_back.shape[1]
+
+    def attn_back(part):
+        return contract(part[:, :q_width], query_weight, 1, 1) + contract(
+            part[:, q_width:], kv_weight, 1, 1
+        )
+
+    low_four = tp_low(attn_back(back_other), attn_back(back_mine))
+
+    attn_cols = both_halves(all_columns(attn_in, attn_reduce))
+    back_rel = jnp.concatenate([back_mine, back_other], 0)
+    back_far_rel = jnp.concatenate([query_far, swap(back_rel[:, q_width:], *side)], 1)
+    qkv_keep, qkv_send = halves(
+        reduce_blocks(
+            contract(attn_cols, back_rel, 0, 0)
+            + contract(join_cores(attn_cols_far), back_far_rel, 0, 0),
+            attn_reduce[:-2],
+            0,
+        ),
+        0,
+    )
+    late = far_span(
+        early_steps,
+        pl.cdiv(hidden_width, STEP) - early_steps,
+        hidden_width - early_width,
+        (qkv_send, qkv_keep, attn_reduce[-2]),
+        [(low_four, last), (output_send, attn_reduce[-1])],
+        6,
+        "far_late",
+    )
+    qkv_part, far_four, output_far = late[3:]
+    gate_part = jnp.concatenate([early[0], late[0]], 1)
+    up_part = jnp.concatenate([early[1], late[1]], 1)
+    down_part = jnp.concatenate([early[2], late[2]], 0)
+    output_grad = output_keep + output_far.astype(F32)
+    qkv_keep, qkv_send = halves(qkv_part, 0)
+    layer_out, tokens_grad, gains, qkv_far = finish(
+        (low_two, far_two, middle, low_four, far_four, middle_back, own_half(tokens)),
+        attn_gain[None],
+        mlp_gain_part[None],
+        rows,
+        [(qkv_send, attn_reduce[-1])],
+    )
+    qkv_grad = qkv_keep + qkv_far.astype(F32)
     gate_grad = reduce_blocks(gate_part, mlp_reduce[1:], 0)
     up_grad = reduce_blocks(up_part, mlp_reduce[1:], 0)
     down_grad = reduce_blocks(down_part, mlp_reduce[1:], 1)
-    gains = sum_gains(jnp.stack([jnp.sum(attn_in_back * normed_one, axis=0), mlp_gain_part]))
-
-    output_grad = reduce_blocks(
-        contract(heads_rel, branch_cols, 0, 0) + contract(heads_far, branch_cols_far, 0, 0),
-        attn_reduce,
-        1,
-    )
-    qkv_grad = reduce_blocks(
-        contract(attn_cols, back_rel, 0, 0) + contract(attn_cols_far, back_far_rel, 0, 0),
-        attn_reduce,
-        0,
-    )
     return (
         layer_out,
         tokens_grad,

time: 369 us -> 363 us (0.984)
  Pallas kernels: 189 us -> 251 us
  waiting for transfers between devices: 64.1 us -> 8.23 us
  starting transfers between devices: 22.5 us -> 14.8 us
  other arithmetic: 36.7 us -> 29.9 us
  local copies, waits for them, and re-layouts: 35.4 us -> 41.2 us
  matrix products: 16.7 us -> 12.7 us
    pallas_call x2 -> x4, Pallas kernels: 82.5 us -> 146 us  [the longest x2 97.2 us: far_rows(): pl.pallas_call(functools.partial(far_kernel, longs=longs, ready=ready, wi...]
    ppermute x33 -> x25, waiting for transfers between devices: 64.1 us -> 8.23 us  [swap(): return lax.ppermute(value, axis, [(i, i ^ mask) for i in range(size)])]
    ppermute x33 -> x25, starting transfers between devices: 22.5 us -> 14.8 us  [swap(): return lax.ppermute(value, axis, [(i, i ^ mask) for i in range(size)])]
    dynamic_update_slice x2 -> x0, other arithmetic: 6.11 us -> none  [whole_rows(): out = lax.dynamic_update_slice_in_dim(out, value, core * half, 0)]
    dynamic_update_slice x2 -> x0, local copies, waits for them, and re-layouts: 5.18 us -> none  [whole_rows(): lax.dynamic_update_slice_in_dim(out, swap(value, 'tp', 1), (1 - core) * h...]
    unnamed x112 -> x133, local copies, waits for them, and re-layouts: 16.6 us -> 21 us
    slice x5, local copies, waits for them, and re-layouts: 1.32 us -> 5.63 us  [the longest x4 4.49 us: halves(): lax.slice_in_dim(value, middle, 2 * middle, axis=dim).astype(BF)]
    dot_general x11, matrix products: 16.7 us -> 12.7 us  [contract(): lax.dot_general(left_side, right_side, (((left_dim,), (right_dim,)), ((),...]
  transfers between devices with their start and end apart: 33 -> 25, of which waited for: 9 -> 5; matrix products, arithmetic and copies ran while one was open for 16% -> 11% of each run, Pallas kernels for 6% -> 24%
where the time goes in v2:
time: 363 us; the launch traced here: 359 us
  Pallas kernels  251 us (69%)
  local copies, waits for them, and re-layouts  41.2 us (11%)
  other arithmetic  29.9 us (8%)
  starting transfers between devices  14.8 us (4%)
  matrix products  12.7 us (3%)
  waiting for transfers between devices  8.23 us (2%)
    pallas_call x2, Pallas kernels, far_rows(): pl.pallas_call(functools.partial(far_kernel, longs=longs, ready=ready, wi...  97.2 us
    pallas_call x1, Pallas kernels, more_rows(): pl.pallas_call(functools.partial(more_kernel, count=count, width=width, r...  31.8 us
    pallas_call x1, Pallas kernels, own_rows(): pl.pallas_call(functools.partial(own_kernel, tile=256, routes=routes), in...  30.1 us
    pallas_call x1, Pallas kernels, exchange(): pl.pallas_call(functools.partial(exchange_kernel, routes=tuple((route for...  26.5 us
    pallas_call x1, Pallas kernels, finish(): pl.pallas_call(functools.partial(finish_kernel, routes=tuple((route for _...  25.9 us
    pallas_call x1, Pallas kernels, attend_back(): pl.pallas_call(functools.partial(backward_kernel, window=window, routes=t...  22.7 us
    unnamed x133, local copies, waits for them, and re-layouts  21 us
    ppermute x25, starting transfers between devices, swap(): return lax.ppermute(value, axis, [(i, i ^ mask) for i in range(size)])  14.8 us
  transfers between devices with their start and end apart: 25, of which 5 were waited for; matrix products, arithmetic and copies ran while one was open for 11% of the time, Pallas kernels for 24%

profile of v2, /device:TPU:0, one launch (start us, length us, event | category | flops | bytes accessed | tf_op | source)
XLA Modules:
  0.0 359.4 jit_solution(13298105130151780910)
XLA Ops:
  0.7 2.7 constant_dynamic-slice_fusion.7
  3.4 5.1 %collective-permute-start.1 = (bf16[128,2048]{1,0:T(8,128)(2,1)}, bf16[128,2048]{1,0:T(8,128)(2,1)S(1)}, u32[]{:S(2)}, u32[]{:S(2)}) collective-permute-start(bf16[128,2048]{1,0:T(8,128)(2,1)} %get-tuple-element.160), channel_id=1, source_target_pairs={{0,24},{8,16},{16,8},{24,0},{1,25},{9,17},{17,9},{25,1},{2,26},{10... | collective-permute-start | bytes 1572872 | tf_op jit(solution)/shard_map/ppermute | solution.py:30
  8.5 1.5 collective-permute-start.2
  10.3 2.0 copy.28
  12.3 1.0 multiply_sine_fusion
  13.3 2.1 pad_maximum_fusion.8.wkv_ref
  15.4 1.3 pad_maximum_fusion.12
  16.7 6.4 %enter.1 = (bf16[512,2048]{1,0:T(8,128)(2,1)}, bf16[512,512]{1,0:T(8,128)(2,1)}, bf16[512,128]{1,0:T(8,128)(2,1)}) custom-call(bf16[512,2048]{1,0:T(8,128)(2,1)} %x_ref.1, f32[1,2048]{1,0:T(1,128)} %bitcast.22, bf16[2048,512]{1,0:T(8,128)(2,1)} %wq_ref.1, bf16[2048,128]{1,0:T(8,128)(2,1)} %pad_maximum_fusion.8.wkv_ref, ...), custom_call_target="tpu_custom_call" | custom-call | flops 1 | bytes 1 | tf_op jit(solution)/shard_map/enter/pallas_call | solution.py:138
  23.7 2.6 constant_dynamic-slice_fusion.5
  26.4 1.9 collective-permute-done
  29.7 1.5 collective-permute-start.4
  31.2 1.0 copy.29.segc_ref
  32.2 8.1 %attend.1 = (bf16[512,512]{1,0:T(8,128)(2,1)}, f32[8,512]{1,0:T(8,128)}) custom-call(bf16[512,512]{1,0:T(8,128)(2,1)} %get-tuple-element.63.q_ref, bf16[2,512,128]{2,1,0:T(8,128)(2,1)} %pad_maximum_fusion.14.kv_ref, s32[1024,1]{1,0:T(8,128)} %copy.29.segc_ref, s32[1,1024]{1,0:T(1,128)} %segr_ref.3), custom_call_target="tpu_custom_call" | custom-call | flops 1 | bytes 1 | tf_op jit(solution)/shard_map/attend/pallas_call | solution.py:225
  40.3 0.9 collective-permute-done.3
  41.5 1.1 constant_dynamic-slice_fusion.16
  43.4 2.6 collective-permute-done.5
  46.0 1.7 fusion.refs_0_
  47.7 26.5 %exchange_one.1 = (bf16[256,2048]{1,0:T(8,128)(2,1)}, bf16[128,2048]{1,0:T(8,128)(2,1)}, bf16[128,2048]{1,0:T(8,128)(2,1)}) custom-call(bf16[256,2048]{1,0:T(8,128)(2,1)} %fusion.refs_0_, bf16[128,2048]{1,0:T(8,128)(2,1)} %get-tuple-element.158.refs_1_, bf16[128,2048]{1,0:T(8,128)(2,1)} %copy-done.19), custom_call_target="tpu_custom_call" | custom-call | flops 1 | bytes 1 | tf_op jit(solution)/shard_map/exchange_one/pallas_call | solution.py:104
  74.3 3.1 multiply_reduce_fusion.2
  77.7 2.4 copy-done.17
  80.1 1.5 constant_dynamic-slice_fusion.15
  81.6 0.8 constant_dynamic-slice_fusion.14.sources_1_
  82.4 1.0 copy-done.8
  83.4 30.1 %own_rows.1 = (bf16[512,1408]{1,0:T(8,128)(2,1)}, bf16[512,1408]{1,0:T(8,128)(2,1)}, bf16[512,1408]{1,0:T(8,128)(2,1)}, bf16[256,2048]{1,0:T(8,128)(2,1)}, f32[2...) custom-call(bf16[256,2048]{1,0:T(8,128)(2,1)} %copy-done.3, ...), custom_call_target="tpu_custom_call" | custom-call | flops 1 | bytes 1 | tf_op jit(solution)/shard_map/own_rows/pallas_call | solution.py:478
  113.6 1.2 constant_dynamic-update-slice_fusion.1
  114.7 1.1 constant_dynamic-update-slice_fusion.refs_2_.refs_14_
  116.4 0.8 pad_maximum_fusion.9.refs_11_
  117.2 2.8 add_convert_fusion.2.refs_9_
  120.1 1.0 copy-done.11
  121.4 31.8 %more_rows.1 = (bf16[512,1408]{1,0:T(8,128)(2,1)}, bf16[512,1408]{1,0:T(8,128)(2,1)}, bf16[512,1408]{1,0:T(8,128)(2,1)}, bf16[256,2048]{1,0:T(8,128)(2,1)}, f32[...) custom-call(bf16[256,2048]{1,0:T(8,128)(2,1)} %get-tuple-element.72.refs_0_.r, ...), custom_call_target="tpu_custom_call" | custom-call | flops 1 | bytes 1 | tf_op jit(solution)/shard_map/more_rows/pallas_call | solution.py:564
  153.2 2.7 multiply_reduce_fusion
  156.0 2.2 fusion.55
  158.9 1.0 constant_dynamic-slice_fusion.1
  161.1 0.9 pad_maximum_fusion.10.sources_0_
  162.1 2.1 fusion.4.hb_ref
  164.2 22.7 %attend_back.1 = (bf16[512,512]{1,0:T(8,128)(2,1)}, f32[512,128]{1,0:T(8,128)}, bf16[1,512,128]{2,1,0:T(8,128)(2,1)}, bf16[256,1024]{1,0:T(8,128)(2,1)}, bf16[128,2048]{1,0:T(8,128)(2,1)}) custom-call(bf16[512,512]{1,0:T(8,128)(2,1)} %get-tuple-element.63.q_ref, bf16[512,512]{1,0:T(8,128)(2,1)} %fusion.4.hb_ref, ...), custom_call_target="tpu_custom_call" | custom-call | flops 1 | bytes 1 | tf_op jit(solution)/shard_map/attend_back/pallas_call | solution.py:328
  187.0 1.1 constant_dynamic-slice_fusion.9
  188.1 0.8 pad_maximum_fusion.11.refs_34_
  190.1 2.6 add_convert_fusion.1.refs_36_.low_two
  195.5 1.0 slice.116.refs_35_
  197.7 0.8 copy-done.35
  198.6 48.6 %far_early.1 = (f32[256,768]{1,0:T(8,128)}, f32[256,768]{1,0:T(8,128)}, f32[768,256]{1,0:T(8,128)}, bf16[512,128]{1,0:T(8,128)(2,1)}, bf16[512,512]{1,0:T(8,128)...) custom-call(bf16[256,2048]{1,0:T(8,128)(2,1)} %copy-done.3, bf16[256,2048]{1,0:T(8,128)(2,1)} %copy-done.8, ...), custom_call_target="tpu_custom_call" | custom-call | flops 1 | bytes 1 | tf_op jit(solution)/shard_map/far_early/pallas_call | solution.py:760
  247.2 2.1 join_keys.1
  249.3 1.2 fusion.37
  253.7 1.1 collective-permute-start.24
  255.3 1.0 fusion.20
  256.3 2.4 collective-permute-done.24
  258.8 2.2 convolution_add_fusion.3
  261.0 1.1 slice.90.refs_34_
  262.2 0.9 slice.115.refs_33_
  263.1 1.8 add_convert_fusion.refs_35_.low_four
  264.9 48.6 %far_late.1 = (f32[256,640]{1,0:T(8,128)}, f32[256,640]{1,0:T(8,128)}, f32[640,256]{1,0:T(8,128)}, f32[512,640]{1,0:T(8,128)}, bf16[256,2048]{1,0:T(8,128)(2,1)}, /*index=5*/bf16[512,256]{1,0:T(8,128)(2,1)}) custom-call(bf16[256,2048]{1,0:T(8,128)(2,1)} %copy-done.3, bf16[256,2048]{1,0:T(8,128)(2,1)} %copy-done.8, ...), custom_call_target="tpu_custom_call" | custom-call | flops 1 | bytes 1 | tf_op jit(solution)/shard_map/far_late/pallas_call | solution.py:760
  313.5 1.8 slice.117.sources_0_
  315.3 25.9 %finish.1 = (f32[512,2048]{1,0:T(8,128)}, f32[512,2048]{1,0:T(8,128)}, f32[2,256]{1,0:T(2,128)}, bf16[256,640]{1,0:T(8,128)(2,1)}) custom-call(bf16[256,2048]{1,0:T(8,128)(2,1)} %add_convert_fusion.1.refs_36_.low_two, bf16[256,2048]{1,0:T(8,128)(2,1)} %get-tuple-element.97.far_two, f32[256,2048]{1,0:T(8,128)} %copy-done.2, ...), custom_call_target="tpu_custom_call" | custom-call | flops 1 | bytes 1 | tf_op jit(solution)/shard_map/finish/pallas_call | solution.py:926
  341.3 1.2 convert_add_fusion.1
  342.5 0.9 slice.94
  343.5 0.9 slice_add_fusion.1
  346.4 2.3 pad_maximum_fusion.4
  348.7 1.2 pad_maximum_fusion.3
  350.5 1.2 pad_maximum_fusion.2
  352.3 2.1 copy.36
  354.5 1.6 copy-done.21
  356.0 2.1 copy.37
  358.2 1.0 copy-done.1
  (186 shorter events, 18.6 us)
Async XLA Ops:
  0.6 41.9 %copy-start = (bf16[512,2048]{1,0:T(8,128)(2,1)S(1)}, bf16[512,2048]{1,0:T(8,128)(2,1)}, u32[]{:S(2)}) copy-start(bf16[512,2048]{1,0:T(8,128)(2,1)} %param.18) | copy-start | bytes 6291460
  0.7 9.4 %copy-start.57 = (bf16[2048,64]{0,1:T(8,128)(2,1)S(1)}, bf16[2048,64]{0,1:T(8,128)(2,1)}, u32[]{:S(2)}) copy-start(bf16[2048,64]{0,1:T(8,128)(2,1)} %param.16) | copy-start | bytes 786436
  3.4 25.6 %collective-permute-start.1 = (bf16[128,2048]{1,0:T(8,128)(2,1)}, bf16[128,2048]{1,0:T(8,128)(2,1)S(1)}, u32[]{:S(2)}, u32[]{:S(2)}) collective-permute-start(bf16[128,2048]{1,0:T(8,128)(2,1)} %get-tuple-element.160), channel_id=1, source_target_pairs={{0,24},{8,16},{16,8},{24,0},{1,25},{9,17},{17,9},{25,1},{2,26},{10... | collective-permute-start | bytes 1572872 | tf_op jit(solution)/shard_map/ppermute | solution.py:30
  8.5 20.6 %collective-permute-start.2 = (bf16[128,2048]{1,0:T(8,128)(2,1)}, bf16[128,2048]{1,0:T(8,128)(2,1)}, u32[]{:S(2)}, u32[]{:S(2)}) collective-permute-start(bf16[128,2048]{1,0:T(8,128)(2,1)} %get-tuple-element.159), channel_id=1, source_target_pairs={{0,4},{4,0},{1,5},{5,1},{2,6},{6,2},{3,7},{7,3},{8,12},{12,8},{9,1... | collective-permute-start | bytes 1572872 | tf_op jit(solution)/shard_map/ppermute | solution.py:30
  23.1 5.2 %collective-permute-start = (bf16[512,128]{1,0:T(8,128)(2,1)}, bf16[512,128]{1,0:T(8,128)(2,1)S(1)}, u32[]{:S(2)}, u32[]{:S(2)}) collective-permute-start(bf16[512,128]{1,0:T(8,128)(2,1)} %get-tuple-element.64), channel_id=1, source_target_pairs={{0,4},{4,0},{1,5},{5,1},{2,6},{6,2},{3,7},{7,3},{8,12},{12,8},{9,1... | collective-permute-start | bytes 393224 | tf_op jit(solution)/shard_map/ppermute | solution.py:30
  23.7 4.6 %copy-start.59 = (bf16[512,128]{1,0:T(8,128)(2,1)S(1)}, bf16[512,128]{1,0:T(8,128)(2,1)}, u32[]{:S(2)}) copy-start(bf16[512,128]{1,0:T(8,128)(2,1)} %get-tuple-element.64) | copy-start | bytes 393220
  26.3 4.9 %copy-start.61 = (s32[1,1024]{1,0:T(1,128)S(1)}, s32[1,1024]{1,0:T(1,128)}, u32[]{:S(2)}) copy-start(s32[1,1024]{1,0:T(1,128)} %segr_ref.3) | copy-start | bytes 12292
  29.1 14.2 %copy-start.19 = (bf16[128,2048]{1,0:T(8,128)(2,1)}, bf16[128,2048]{1,0:T(8,128)(2,1)S(1)}, u32[]{:S(2)}) copy-start(bf16[128,2048]{1,0:T(8,128)(2,1)S(1)} %collective-permute-done.1.refs_2_.refs_16_) | copy-start | bytes 1572868
  29.1 12.1 %collective-permute-start.3 = (bf16[256,1024]{1,0:T(8,128)(2,1)S(1)}, bf16[256,1024]{1,0:T(8,128)(2,1)}, u32[]{:S(2)}, u32[]{:S(2)}) collective-permute-start(bf16[256,1024]{1,0:T(8,128)(2,1)S(1)} %fusion.35), channel_id=1, source_target_pairs={{0,4},{4,0},{1,5},{5,1},{2,6},{6,2},{3,7},{7,3},{8,12},{12,8},{9,1... | collective-permute-start | bytes 1572872 | tf_op jit(solution)/shard_map/ppermute | solution.py:30
  29.7 11.8 %collective-permute-start.4 = (bf16[128,2048]{1,0:T(8,128)(2,1)S(1)}, bf16[128,2048]{1,0:T(8,128)(2,1)}, u32[]{:S(2)}, u32[]{:S(2)}) collective-permute-start(bf16[128,2048]{1,0:T(8,128)(2,1)S(1)} %collective-permute-done.1.refs_2_.refs_16_), channel_id=1, source_target_pairs={{0,2},{1,3},{2,0},{3,1},{4,6},{5,7},{6,4},{7,5},{8,10},{9,11},{10,... | collective-permute-start | bytes 1572872 | tf_op jit(solution)/shard_map/ppermute | solution.py:30
  42.5 3.5 copy-start.26
  43.3 2.7 collective-permute-start.5
  47.7 26.6 %copy-start.9 = (bf16[256,2048]{1,0:T(8,128)(2,1)S(1)}, bf16[256,2048]{1,0:T(8,128)(2,1)}, u32[]{:S(2)}) copy-start(bf16[256,2048]{1,0:T(8,128)(2,1)} %fusion.refs_0_) | copy-start | bytes 3145732
  74.3 3.1 copy-start.60
  77.4 78.5 %copy-start.2 = (f32[256,2048]{1,0:T(8,128)}, f32[256,2048]{1,0:T(8,128)S(1)}, u32[]{:S(2)}) copy-start(f32[256,2048]{1,0:T(8,128)S(1)} %get-tuple-element.142.middle) | copy-start | bytes 6291460
  77.4 2.7 copy-start.17
  77.7 3.9 %copy-start.3 = (bf16[256,2048]{1,0:T(8,128)(2,1)}, bf16[256,2048]{1,0:T(8,128)(2,1)S(1)}, u32[]{:S(2)}) copy-start(bf16[256,2048]{1,0:T(8,128)(2,1)S(1)} %multiply_convert_fusion.m_refs_0_.sources_0_.refs_0_) | copy-start | bytes 3145732
  77.7 4.7 %collective-permute-start.6 = (bf16[256,2048]{1,0:T(8,128)(2,1)S(1)}, bf16[256,2048]{1,0:T(8,128)(2,1)S(1)}, u32[]{:S(2)}, u32[]{:S(2)}) collective-permute-start(bf16[256,2048]{1,0:T(8,128)(2,1)S(1)} %multiply_convert_fusion.m_refs_0_.sources_0_.refs_0_), channel_id=1, source_target_pairs={{0,1},{1,0},{2,3},{3,2},{4,5},{5,4},{6,7},{7,6},{8,9},{9,8},{10,11... | collective-permute-start | bytes 3145736 | tf_op jit(solution)/shard_map/ppermute | solution.py:30
  113.5 2.8 copy-start.10
  113.5 2.9 copy-start.27
  113.5 3.7 %collective-permute-start.9 = (bf16[256,2048]{1,0:T(8,128)(2,1)}, bf16[256,2048]{1,0:T(8,128)(2,1)S(1)}, u32[]{:S(2)}, u32[]{:S(2)}) collective-permute-start(bf16[256,2048]{1,0:T(8,128)(2,1)} %get-tuple-element.76), channel_id=1, source_target_pairs={{0,1},{1,0},{2,3},{3,2},{4,5},{5,4},{6,7},{7,6},{8,9},{9,8},{10,11... | collective-permute-start | bytes 3145736 | tf_op jit(solution)/shard_map/ppermute | solution.py:30
  115.8 4.3 %copy-start.7 = (bf16[256,2048]{1,0:T(8,128)(2,1)}, bf16[256,2048]{1,0:T(8,128)(2,1)S(1)}, u32[]{:S(2)}) copy-start(bf16[256,2048]{1,0:T(8,128)(2,1)S(1)} %constant_dynamic-update-slice_fusion.refs_2_.refs_14_) | copy-start | bytes 3145732
  115.8 4.3 %collective-permute-start.8 = (bf16[256,2048]{1,0:T(8,128)(2,1)S(1)}, bf16[256,2048]{1,0:T(8,128)(2,1)S(1)}, u32[]{:S(2)}, u32[]{:S(2)}) collective-permute-start(bf16[256,2048]{1,0:T(8,128)(2,1)S(1)} %constant_dynamic-update-slice_fusion.refs_2_.refs_14_), channel_id=1, source_target_pairs={{0,1},{1,0},{2,3},{3,2},{4,5},{5,4},{6,7},{7,6},{8,9},{9,8},{10,11... | collective-permute-start | bytes 3145736 | tf_op jit(solution)/shard_map/ppermute | solution.py:30
  116.3 3.8 %collective-permute-start.7 = (bf16[256,2048]{1,0:T(8,128)(2,1)S(1)}, bf16[256,2048]{1,0:T(8,128)(2,1)S(1)}, u32[]{:S(2)}, u32[]{:S(2)}) collective-permute-start(bf16[256,2048]{1,0:T(8,128)(2,1)S(1)} %copy-done.10), channel_id=1, source_target_pairs={{0,1},{1,0},{2,3},{3,2},{4,5},{5,4},{6,7},{7,6},{8,9},{9,8},{10,11... | collective-permute-start | bytes 3145736 | tf_op jit(solution)/shard_map/ppermute | solution.py:30
  121.4 31.8 %copy-start.6 = (bf16[256,2048]{1,0:T(8,128)(2,1)S(1)}, bf16[256,2048]{1,0:T(8,128)(2,1)}, u32[]{:S(2)}) copy-start(bf16[256,2048]{1,0:T(8,128)(2,1)} %add_convert_fusion.2.refs_9_) | copy-start | bytes 3145732
  153.2 2.7 copy-start.4
  153.2 2.7 copy-start.23
  155.9 2.3 copy-start.42
  158.2 3.9 %copy-start.15 = (bf16[256,2048]{1,0:T(8,128)(2,1)}, bf16[256,2048]{1,0:T(8,128)(2,1)S(1)}, u32[]{:S(2)}) copy-start(bf16[256,2048]{1,0:T(8,128)(2,1)S(1)} %get-tuple-element.139) | copy-start | bytes 3145732
  158.2 3.8 %collective-permute-start.12 = (bf16[256,2048]{1,0:T(8,128)(2,1)S(1)}, bf16[256,2048]{1,0:T(8,128)(2,1)S(1)}, u32[]{:S(2)}, u32[]{:S(2)}) collective-permute-start(bf16[256,2048]{1,0:T(8,128)(2,1)S(1)} %get-tuple-element.139), channel_id=1, source_target_pairs={{0,1},{1,0},{2,3},{3,2},{4,5},{5,4},{6,7},{7,6},{8,9},{9,8},{10,11... | collective-permute-start | bytes 3145736 | tf_op jit(solution)/shard_map/ppermute | solution.py:30
  158.4 3.6 %copy-start.18 = (bf16[128,2048]{1,0:T(8,128)(2,1)S(1)}, bf16[128,2048]{1,0:T(8,128)(2,1)}, u32[]{:S(2)}) copy-start(bf16[128,2048]{1,0:T(8,128)(2,1)} %get-tuple-element.71.sources_2_.refs_20_) | copy-start | bytes 1572868
  158.4 30.8 %collective-permute-start.10 = (bf16[256,2048]{1,0:T(8,128)(2,1)}, bf16[256,2048]{1,0:T(8,128)(2,1)}, u32[]{:S(2)}, u32[]{:S(2)}) collective-permute-start(bf16[256,2048]{1,0:T(8,128)(2,1)} %get-tuple-element.79), channel_id=1, source_target_pairs={{0,1},{1,0},{2,3},{3,2},{4,5},{5,4},{6,7},{7,6},{8,9},{9,8},{10,11... | collective-permute-start | bytes 3145736 | tf_op jit(solution)/shard_map/ppermute | solution.py:30
  160.0 32.8 %collective-permute-start.17 = (bf16[128,2048]{1,0:T(8,128)(2,1)S(1)}, bf16[128,2048]{1,0:T(8,128)(2,1)}, u32[]{:S(2)}, u32[]{:S(2)}) collective-permute-start(bf16[128,2048]{1,0:T(8,128)(2,1)S(1)} %copy-done.20), channel_id=1, source_target_pairs={{0,1},{1,0},{2,3},{3,2},{4,5},{5,4},{6,7},{7,6},{8,9},{9,8},{10,11... | collective-permute-start | bytes 1572872 | tf_op jit(solution)/shard_map/ppermute | solution.py:30
  160.0 33.2 %collective-permute-start.18 = (bf16[128,2048]{1,0:T(8,128)(2,1)}, bf16[128,2048]{1,0:T(8,128)(2,1)}, u32[]{:S(2)}, u32[]{:S(2)}) collective-permute-start(bf16[128,2048]{1,0:T(8,128)(2,1)} %collective-permute-done.4.refs_18_), channel_id=1, source_target_pairs={{0,1},{1,0},{2,3},{3,2},{4,5},{5,4},{6,7},{7,6},{8,9},{9,8},{10,11... | collective-permute-start | bytes 1572872 | tf_op jit(solution)/shard_map/ppermute | solution.py:30
  160.5 26.4 %collective-permute-start.15 = (bf16[128,2048]{1,0:T(8,128)(2,1)}, bf16[128,2048]{1,0:T(8,128)(2,1)}, u32[]{:S(2)}, u32[]{:S(2)}) collective-permute-start(bf16[128,2048]{1,0:T(8,128)(2,1)} %get-tuple-element.84.refs_8_), channel_id=1, source_target_pairs={{0,2},{1,3},{2,0},{3,1},{4,6},{5,7},{6,4},{7,5},{8,10},{9,11},{10,... | collective-permute-start | bytes 1572872 | tf_op jit(solution)/shard_map/ppermute | solution.py:30
  162.0 31.3 %collective-permute-start.19 = (bf16[128,2048]{1,0:T(8,128)(2,1)S(1)}, bf16[128,2048]{1,0:T(8,128)(2,1)}, u32[]{:S(2)}, u32[]{:S(2)}) collective-permute-start(bf16[128,2048]{1,0:T(8,128)(2,1)S(1)} %copy-done.18), channel_id=1, source_target_pairs={{0,1},{1,0},{2,3},{3,2},{4,5},{5,4},{6,7},{7,6},{8,9},{9,8},{10,11... | collective-permute-start | bytes 1572872 | tf_op jit(solution)/shard_map/ppermute | solution.py:30
  164.2 22.7 %copy-start.13 = (bf16[128,2048]{1,0:T(8,128)(2,1)S(1)}, bf16[128,2048]{1,0:T(8,128)(2,1)}, u32[]{:S(2)}) copy-start(bf16[128,2048]{1,0:T(8,128)(2,1)} %get-tuple-element.77.refs_10_.sources_1_.refs_4_) | copy-start | bytes 1572868
  164.2 24.8 %copy-start.16 = (bf16[256,2048]{1,0:T(8,128)(2,1)S(1)}, bf16[256,2048]{1,0:T(8,128)(2,1)}, u32[]{:S(2)}) copy-start(bf16[256,2048]{1,0:T(8,128)(2,1)} %copy-done.15) | copy-start | bytes 3145732
  186.9 9.6 %collective-permute-start.11 = (bf16[128,2048]{1,0:T(8,128)(2,1)S(1)}, bf16[128,2048]{1,0:T(8,128)(2,1)S(1)}, u32[]{:S(2)}, u32[]{:S(2)}) collective-permute-start(bf16[128,2048]{1,0:T(8,128)(2,1)S(1)} %copy-done.13), channel_id=1, source_target_pairs={{0,1},{1,0},{2,3},{3,2},{4,5},{5,4},{6,7},{7,6},{8,9},{9,8},{10,11... | collective-permute-start | bytes 1572872 | tf_op jit(solution)/shard_map/ppermute | solution.py:30
  189.4 4.3 %collective-permute-start.21 = (bf16[256,1024]{1,0:T(8,128)(2,1)S(1)}, bf16[256,1024]{1,0:T(8,128)(2,1)S(1)}, u32[]{:S(2)}, u32[]{:S(2)}) collective-permute-start(bf16[256,1024]{1,0:T(8,128)(2,1)S(1)} %copy-done.52), channel_id=1, source_target_pairs={{0,1},{1,0},{2,3},{3,2},{4,5},{5,4},{6,7},{7,6},{8,9},{9,8},{10,11... | collective-permute-start | bytes 1572872 | tf_op jit(solution)/shard_map/ppermute | solution.py:30
  190.1 2.7 copy-start.29
  190.1 3.6 copy-start.30
  190.1 3.7 %copy-start.37 = (bf16[512,512]{1,0:T(8,128)(2,1)S(1)}, bf16[512,512]{1,0:T(8,128)(2,1)}, u32[]{:S(2)}) copy-start(bf16[512,512]{1,0:T(8,128)(2,1)} %get-tuple-element.95) | copy-start | bytes 1572868
  192.8 4.1 %collective-permute-start.20 = (bf16[128,2048]{1,0:T(8,128)(2,1)S(1)}, bf16[128,2048]{1,0:T(8,128)(2,1)S(1)}, u32[]{:S(2)}, u32[]{:S(2)}) collective-permute-start(bf16[128,2048]{1,0:T(8,128)(2,1)S(1)} %copy-done.29), channel_id=1, source_target_pairs={{0,1},{1,0},{2,3},{3,2},{4,5},{5,4},{6,7},{7,6},{8,9},{9,8},{10,11... | collective-permute-start | bytes 1572872 | tf_op jit(solution)/shard_map/ppermute | solution.py:30
  193.2 3.7 %collective-permute-start.14 = (bf16[128,2048]{1,0:T(8,128)(2,1)}, bf16[128,2048]{1,0:T(8,128)(2,1)S(1)}, u32[]{:S(2)}, u32[]{:S(2)}) collective-permute-start(bf16[128,2048]{1,0:T(8,128)(2,1)} %get-tuple-element.84.refs_8_), channel_id=1, source_target_pairs={{0,1},{1,0},{2,3},{3,2},{4,5},{5,4},{6,7},{7,6},{8,9},{9,8},{10,11... | collective-permute-start | bytes 1572872 | tf_op jit(solution)/shard_map/ppermute | solution.py:30
  193.3 3.6 %collective-permute-start.16 = (bf16[128,2048]{1,0:T(8,128)(2,1)}, bf16[128,2048]{1,0:T(8,128)(2,1)S(1)}, u32[]{:S(2)}, u32[]{:S(2)}) collective-permute-start(bf16[128,2048]{1,0:T(8,128)(2,1)} %collective-permute-done.15.refs_10_), channel_id=1, source_target_pairs={{0,1},{1,0},{2,3},{3,2},{4,5},{5,4},{6,7},{7,6},{8,9},{9,8},{10,11... | collective-permute-start | bytes 1572872 | tf_op jit(solution)/shard_map/ppermute | solution.py:30
  193.7 3.3 collective-permute-start.13
  195.5 3.1 copy-start.38
  196.5 59.8 %collective-permute-start.23 = (bf16[256,1024]{1,0:T(8,128)(2,1)}, bf16[256,1024]{1,0:T(8,128)(2,1)}, u32[]{:S(2)}, u32[]{:S(2)}) collective-permute-start(bf16[256,1024]{1,0:T(8,128)(2,1)} %collective-permute-done.3), channel_id=1, source_target_pairs={{0,1},{1,0},{2,3},{3,2},{4,5},{5,4},{6,7},{7,6},{8,9},{9,8},{10,11... | collective-permute-start | bytes 1572872 | tf_op jit(solution)/shard_map/ppermute | solution.py:30
  247.1 3.4 copy-start.14
  251.8 11.3 %collective-permute-start.22 = (bf16[256,2048]{1,0:T(8,128)(2,1)S(1)}, bf16[256,2048]{1,0:T(8,128)(2,1)S(1)}, u32[]{:S(2)}, u32[]{:S(2)}) collective-permute-start(bf16[256,2048]{1,0:T(8,128)(2,1)S(1)} %fusion.1), channel_id=1, source_target_pairs={{0,1},{1,0},{2,3},{3,2},{4,5},{5,4},{6,7},{7,6},{8,9},{9,8},{10,11... | collective-permute-start | bytes 3145736 | tf_op jit(solution)/shard_map/ppermute | solution.py:30
  252.9 2.4 copy-start.24
  252.9 2.4 copy-start.54
  252.9 2.4 copy-start.55
  253.7 5.1 %collective-permute-start.24 = (bf16[512,128]{1,0:T(8,128)(2,1)S(1)}, bf16[512,128]{1,0:T(8,128)(2,1)S(1)}, u32[]{:S(2)}, u32[]{:S(2)}) collective-permute-start(bf16[512,128]{1,0:T(8,128)(2,1)S(1)} %pad_maximum_fusion.15), channel_id=1, source_target_pairs={{0,4},{4,0},{1,5},{5,1},{2,6},{6,2},{3,7},{7,3},{8,12},{12,8},{9,1... | collective-permute-start | bytes 393224 | tf_op jit(solution)/shard_map/ppermute | solution.py:30
  255.3 3.5 copy-start.56
  315.3 26.0 %copy-start.49 = (f32[512,640]{1,0:T(8,128)S(1)}, f32[512,640]{1,0:T(8,128)}, u32[]{:S(2)}) copy-start(f32[512,640]{1,0:T(8,128)} %get-tuple-element.103) | copy-start | bytes 3932164
  341.3 4.5 %copy-start.62 = (f32[2,256]{1,0:T(2,128)S(1)}, f32[2,256]{1,0:T(2,128)}, u32[]{:S(2)}) copy-start(f32[2,256]{1,0:T(2,128)} %get-tuple-element.106) | copy-start | bytes 6148
  341.3 5.0 %copy-start.48 = (f32[768,256]{1,0:T(8,128)S(1)}, f32[768,256]{1,0:T(8,128)}, u32[]{:S(2)}) copy-start(f32[768,256]{1,0:T(8,128)} %get-tuple-element.113) | copy-start | bytes 2359300
  343.5 5.2 %copy-start.47 = (f32[256,768]{1,0:T(8,128)S(1)}, f32[256,768]{1,0:T(8,128)}, u32[]{:S(2)}) copy-start(f32[256,768]{1,0:T(8,128)} %get-tuple-element.111) | copy-start | bytes 2359300
  343.5 5.2 %copy-start.51 = (f32[256,640]{1,0:T(8,128)S(1)}, f32[256,640]{1,0:T(8,128)}, u32[]{:S(2)}) copy-start(f32[256,640]{1,0:T(8,128)} %get-tuple-element.112) | copy-start | bytes 1966084
  348.7 3.7 %copy-start.22 = (f32[512,2048]{1,0:T(8,128)S(1)}, f32[512,2048]{1,0:T(8,128)}, u32[]{:S(2)}) copy-start(f32[512,2048]{1,0:T(8,128)} %get-tuple-element.192) | copy-start | bytes 12582916
  352.3 3.7 %copy-start.21 = (f32[512,2048]{1,0:T(8,128)S(1)}, f32[512,2048]{1,0:T(8,128)}, u32[]{:S(2)}) copy-start(f32[512,2048]{1,0:T(8,128)} %get-tuple-element.193) | copy-start | bytes 12582916
  356.0 3.1 copy-start.1
  (24 other events, 40.0 us)

commit v3 on v2

--- a/solution.py
+++ b/solution.py
@@ -424,8 +424,9 @@
     greet(routes)
     for copy in carried:
         copy.start()
-    for c in range(full + (1 if tail else 0)):
-        for copy in copies(c, STEP if c < full else tail):
+    ahead = min(3, full)
+    for c in range(ahead):
+        for copy in copies(c, STEP):
             copy.start()
 
     def chunk(c, w):
@@ -443,6 +444,18 @@
             ub_ref[r, at] = ub
 
     def chunk_step(c, carry):
+        @pl.when(c + ahead < full)
+        def _():
+            for copy in copies(c + ahead, STEP):
+                copy.start()
+
+        if tail:
+
+            @pl.when(c + ahead == full)
+            def _():
+                for copy in copies(full, tail):
+                    copy.start()
+
         chunk(c, STEP)
         return carry
 
@@ -512,7 +525,6 @@
         greet(routes)
         for copy in links(sources, landings, sent, got, routes):
             copy.start()
-        down_copy.start()
 
     def body(w):
         wg, wu, wd = wg_ref[:, :w], wu_ref[:, :w], wd_ref[:w, :]
@@ -525,6 +537,10 @@
             gb_ref[dst, :w] = gb
             ub_ref[dst, :w] = ub
             at += long
+
+    @pl.when(step == steps // 2)
+    def _():
+        down_copy.start()
 
     if tail:
         pl.when(step < full)(lambda: body(STEP))

time: 363 us -> 363 us (level)
  no operation moved by 1% of the time
where the time goes in v3:
time: 363 us; the launch traced here: 359 us
  Pallas kernels  251 us (69%)
  local copies, waits for them, and re-layouts  41.2 us (11%)
  other arithmetic  29.9 us (8%)
  starting transfers between devices  14.8 us (4%)
  matrix products  12.7 us (3%)
  waiting for transfers between devices  8.23 us (2%)
    pallas_call x2, Pallas kernels, far_rows(): pl.pallas_call(functools.partial(far_kernel, longs=longs, ready=ready, wi...  97.2 us
    pallas_call x1, Pallas kernels, more_rows(): pl.pallas_call(functools.partial(more_kernel, count=count, width=width, r...  31.8 us
    pallas_call x1, Pallas kernels, own_rows(): pl.pallas_call(functools.partial(own_kernel, tile=256, routes=routes), in...  30.1 us
    pallas_call x1, Pallas kernels, exchange(): pl.pallas_call(functools.partial(exchange_kernel, routes=tuple((route for...  26.5 us
    pallas_call x1, Pallas kernels, finish(): pl.pallas_call(functools.partial(finish_kernel, routes=tuple((route for _...  25.9 us
    pallas_call x1, Pallas kernels, attend_back(): pl.pallas_call(functools.partial(backward_kernel, window=window, routes=t...  22.7 us
    unnamed x133, local copies, waits for them, and re-layouts  21 us
    ppermute x25, starting transfers between devices, swap(): return lax.ppermute(value, axis, [(i, i ^ mask) for i in range(size)])  14.8 us
  transfers between devices with their start and end apart: 25, of which 5 were waited for; matrix products, arithmetic and copies ran while one was open for 11% of the time, Pallas kernels for 24%

profile of v3, /device:TPU:0, one launch (start us, length us, event | category | flops | bytes accessed | tf_op | source)
XLA Modules:
  0.0 359.4 jit_solution(12715737122053061368)
XLA Ops:
  0.7 2.7 constant_dynamic-slice_fusion.7
  3.4 5.1 %collective-permute-start.1 = (bf16[128,2048]{1,0:T(8,128)(2,1)}, bf16[128,2048]{1,0:T(8,128)(2,1)S(1)}, u32[]{:S(2)}, u32[]{:S(2)}) collective-permute-start(bf16[128,2048]{1,0:T(8,128)(2,1)} %get-tuple-element.160), channel_id=1, source_target_pairs={{0,24},{8,16},{16,8},{24,0},{1,25},{9,17},{17,9},{25,1},{2,26},{10... | collective-permute-start | bytes 1572872 | tf_op jit(solution)/shard_map/ppermute | solution.py:30
  8.5 1.5 collective-permute-start.2
  10.3 2.0 copy.28
  12.3 1.0 multiply_sine_fusion
  13.3 2.1 pad_maximum_fusion.8.wkv_ref
  15.4 1.3 pad_maximum_fusion.12
  16.7 6.4 %enter.1 = (bf16[512,2048]{1,0:T(8,128)(2,1)}, bf16[512,512]{1,0:T(8,128)(2,1)}, bf16[512,128]{1,0:T(8,128)(2,1)}) custom-call(bf16[512,2048]{1,0:T(8,128)(2,1)} %x_ref.1, f32[1,2048]{1,0:T(1,128)} %bitcast.22, bf16[2048,512]{1,0:T(8,128)(2,1)} %wq_ref.1, bf16[2048,128]{1,0:T(8,128)(2,1)} %pad_maximum_fusion.8.wkv_ref, ...), custom_call_target="tpu_custom_call" | custom-call | flops 1 | bytes 1 | tf_op jit(solution)/shard_map/enter/pallas_call | solution.py:138
  23.7 2.6 constant_dynamic-slice_fusion.5
  26.4 1.9 collective-permute-done
  29.7 1.5 collective-permute-start.4
  31.2 1.0 copy.29.segc_ref
  32.2 8.1 %attend.1 = (bf16[512,512]{1,0:T(8,128)(2,1)}, f32[8,512]{1,0:T(8,128)}) custom-call(bf16[512,512]{1,0:T(8,128)(2,1)} %get-tuple-element.63.q_ref, bf16[2,512,128]{2,1,0:T(8,128)(2,1)} %pad_maximum_fusion.14.kv_ref, s32[1024,1]{1,0:T(8,128)} %copy.29.segc_ref, s32[1,1024]{1,0:T(1,128)} %segr_ref.3), custom_call_target="tpu_custom_call" | custom-call | flops 1 | bytes 1 | tf_op jit(solution)/shard_map/attend/pallas_call | solution.py:225
  40.3 0.9 collective-permute-done.3
  41.5 1.1 constant_dynamic-slice_fusion.16
  43.4 2.6 collective-permute-done.5
  46.0 1.7 fusion.refs_0_
  47.7 26.5 %exchange_one.1 = (bf16[256,2048]{1,0:T(8,128)(2,1)}, bf16[128,2048]{1,0:T(8,128)(2,1)}, bf16[128,2048]{1,0:T(8,128)(2,1)}) custom-call(bf16[256,2048]{1,0:T(8,128)(2,1)} %fusion.refs_0_, bf16[128,2048]{1,0:T(8,128)(2,1)} %get-tuple-element.158.refs_1_, bf16[128,2048]{1,0:T(8,128)(2,1)} %copy-done.19), custom_call_target="tpu_custom_call" | custom-call | flops 1 | bytes 1 | tf_op jit(solution)/shard_map/exchange_one/pallas_call | solution.py:104
  74.3 3.1 multiply_reduce_fusion.2
  77.7 2.4 copy-done.17
  80.1 1.5 constant_dynamic-slice_fusion.15
  81.6 0.8 constant_dynamic-slice_fusion.14.sources_1_
  82.4 1.0 copy-done.8
  83.4 30.1 %own_rows.1 = (bf16[512,1408]{1,0:T(8,128)(2,1)}, bf16[512,1408]{1,0:T(8,128)(2,1)}, bf16[512,1408]{1,0:T(8,128)(2,1)}, bf16[256,2048]{1,0:T(8,128)(2,1)}, f32[2...) custom-call(bf16[256,2048]{1,0:T(8,128)(2,1)} %copy-done.3, ...), custom_call_target="tpu_custom_call" | custom-call | flops 1 | bytes 1 | tf_op jit(solution)/shard_map/own_rows/pallas_call | solution.py:491
  113.6 1.2 constant_dynamic-update-slice_fusion.1
  114.7 1.1 constant_dynamic-update-slice_fusion.refs_2_.refs_14_
  116.4 0.8 pad_maximum_fusion.9.refs_11_
  117.2 2.8 add_convert_fusion.2.refs_9_
  120.1 1.0 copy-done.11
  121.4 31.8 %more_rows.1 = (bf16[512,1408]{1,0:T(8,128)(2,1)}, bf16[512,1408]{1,0:T(8,128)(2,1)}, bf16[512,1408]{1,0:T(8,128)(2,1)}, bf16[256,2048]{1,0:T(8,128)(2,1)}, f32[...) custom-call(bf16[256,2048]{1,0:T(8,128)(2,1)} %get-tuple-element.72.refs_0_.r, ...), custom_call_target="tpu_custom_call" | custom-call | flops 1 | bytes 1 | tf_op jit(solution)/shard_map/more_rows/pallas_call | solution.py:580
  153.2 2.7 multiply_reduce_fusion
  156.0 2.2 fusion.55
  158.9 1.0 constant_dynamic-slice_fusion.1
  161.1 0.9 pad_maximum_fusion.10.sources_0_
  162.1 2.1 fusion.4.hb_ref
  164.2 22.7 %attend_back.1 = (bf16[512,512]{1,0:T(8,128)(2,1)}, f32[512,128]{1,0:T(8,128)}, bf16[1,512,128]{2,1,0:T(8,128)(2,1)}, bf16[256,1024]{1,0:T(8,128)(2,1)}, bf16[128,2048]{1,0:T(8,128)(2,1)}) custom-call(bf16[512,512]{1,0:T(8,128)(2,1)} %get-tuple-element.63.q_ref, bf16[512,512]{1,0:T(8,128)(2,1)} %fusion.4.hb_ref, ...), custom_call_target="tpu_custom_call" | custom-call | flops 1 | bytes 1 | tf_op jit(solution)/shard_map/attend_back/pallas_call | solution.py:328
  187.0 1.1 constant_dynamic-slice_fusion.9
  188.1 0.8 pad_maximum_fusion.11.refs_34_
  190.1 2.6 add_convert_fusion.1.refs_36_.low_two
  195.5 1.0 slice.116.refs_35_
  197.7 0.8 copy-done.35
  198.6 48.6 %far_early.1 = (f32[256,768]{1,0:T(8,128)}, f32[256,768]{1,0:T(8,128)}, f32[768,256]{1,0:T(8,128)}, bf16[512,128]{1,0:T(8,128)(2,1)}, bf16[512,512]{1,0:T(8,128)...) custom-call(bf16[256,2048]{1,0:T(8,128)(2,1)} %copy-done.3, bf16[256,2048]{1,0:T(8,128)(2,1)} %copy-done.8, ...), custom_call_target="tpu_custom_call" | custom-call | flops 1 | bytes 1 | tf_op jit(solution)/shard_map/far_early/pallas_call | solution.py:776
  247.2 2.1 join_keys.1
  249.3 1.2 fusion.37
  253.7 1.1 collective-permute-start.24
  255.3 1.0 fusion.20
  256.3 2.4 collective-permute-done.24
  258.8 2.2 convolution_add_fusion.3
  261.0 1.1 slice.90.refs_34_
  262.2 0.9 slice.115.refs_33_
  263.1 1.8 add_convert_fusion.refs_35_.low_four
  264.9 48.6 %far_late.1 = (f32[256,640]{1,0:T(8,128)}, f32[256,640]{1,0:T(8,128)}, f32[640,256]{1,0:T(8,128)}, f32[512,640]{1,0:T(8,128)}, bf16[256,2048]{1,0:T(8,128)(2,1)}, /*index=5*/bf16[512,256]{1,0:T(8,128)(2,1)}) custom-call(bf16[256,2048]{1,0:T(8,128)(2,1)} %copy-done.3, bf16[256,2048]{1,0:T(8,128)(2,1)} %copy-done.8, ...), custom_call_target="tpu_custom_call" | custom-call | flops 1 | bytes 1 | tf_op jit(solution)/shard_map/far_late/pallas_call | solution.py:776
  313.5 1.8 slice.117.sources_0_
  315.3 25.9 %finish.1 = (f32[512,2048]{1,0:T(8,128)}, f32[512,2048]{1,0:T(8,128)}, f32[2,256]{1,0:T(2,128)}, bf16[256,640]{1,0:T(8,128)(2,1)}) custom-call(bf16[256,2048]{1,0:T(8,128)(2,1)} %add_convert_fusion.1.refs_36_.low_two, bf16[256,2048]{1,0:T(8,128)(2,1)} %get-tuple-element.97.far_two, f32[256,2048]{1,0:T(8,128)} %copy-done.2, ...), custom_call_target="tpu_custom_call" | custom-call | flops 1 | bytes 1 | tf_op jit(solution)/shard_map/finish/pallas_call | solution.py:942
  341.3 1.2 convert_add_fusion.1
  342.5 0.9 slice.94
  343.5 0.9 slice_add_fusion.1
  346.4 2.3 pad_maximum_fusion.4
  348.7 1.2 pad_maximum_fusion.3
  350.5 1.2 pad_maximum_fusion.2
  352.3 2.1 copy.36
  354.5 1.6 copy-done.21
  356.0 2.1 copy.37
  358.2 1.0 copy-done.1
  (186 shorter events, 18.6 us)
Async XLA Ops:
  0.6 41.9 %copy-start = (bf16[512,2048]{1,0:T(8,128)(2,1)S(1)}, bf16[512,2048]{1,0:T(8,128)(2,1)}, u32[]{:S(2)}) copy-start(bf16[512,2048]{1,0:T(8,128)(2,1)} %param.18) | copy-start | bytes 6291460
  0.7 9.4 %copy-start.57 = (bf16[2048,64]{0,1:T(8,128)(2,1)S(1)}, bf16[2048,64]{0,1:T(8,128)(2,1)}, u32[]{:S(2)}) copy-start(bf16[2048,64]{0,1:T(8,128)(2,1)} %param.16) | copy-start | bytes 786436
  3.4 25.6 %collective-permute-start.1 = (bf16[128,2048]{1,0:T(8,128)(2,1)}, bf16[128,2048]{1,0:T(8,128)(2,1)S(1)}, u32[]{:S(2)}, u32[]{:S(2)}) collective-permute-start(bf16[128,2048]{1,0:T(8,128)(2,1)} %get-tuple-element.160), channel_id=1, source_target_pairs={{0,24},{8,16},{16,8},{24,0},{1,25},{9,17},{17,9},{25,1},{2,26},{10... | collective-permute-start | bytes 1572872 | tf_op jit(solution)/shard_map/ppermute | solution.py:30
  8.5 20.6 %collective-permute-start.2 = (bf16[128,2048]{1,0:T(8,128)(2,1)}, bf16[128,2048]{1,0:T(8,128)(2,1)}, u32[]{:S(2)}, u32[]{:S(2)}) collective-permute-start(bf16[128,2048]{1,0:T(8,128)(2,1)} %get-tuple-element.159), channel_id=1, source_target_pairs={{0,4},{4,0},{1,5},{5,1},{2,6},{6,2},{3,7},{7,3},{8,12},{12,8},{9,1... | collective-permute-start | bytes 1572872 | tf_op jit(solution)/shard_map/ppermute | solution.py:30
  23.1 5.2 %collective-permute-start = (bf16[512,128]{1,0:T(8,128)(2,1)}, bf16[512,128]{1,0:T(8,128)(2,1)S(1)}, u32[]{:S(2)}, u32[]{:S(2)}) collective-permute-start(bf16[512,128]{1,0:T(8,128)(2,1)} %get-tuple-element.64), channel_id=1, source_target_pairs={{0,4},{4,0},{1,5},{5,1},{2,6},{6,2},{3,7},{7,3},{8,12},{12,8},{9,1... | collective-permute-start | bytes 393224 | tf_op jit(solution)/shard_map/ppermute | solution.py:30
  23.7 4.6 %copy-start.59 = (bf16[512,128]{1,0:T(8,128)(2,1)S(1)}, bf16[512,128]{1,0:T(8,128)(2,1)}, u32[]{:S(2)}) copy-start(bf16[512,128]{1,0:T(8,128)(2,1)} %get-tuple-element.64) | copy-start | bytes 393220
  26.3 4.9 %copy-start.61 = (s32[1,1024]{1,0:T(1,128)S(1)}, s32[1,1024]{1,0:T(1,128)}, u32[]{:S(2)}) copy-start(s32[1,1024]{1,0:T(1,128)} %segr_ref.3) | copy-start | bytes 12292
  29.1 14.2 %copy-start.19 = (bf16[128,2048]{1,0:T(8,128)(2,1)}, bf16[128,2048]{1,0:T(8,128)(2,1)S(1)}, u32[]{:S(2)}) copy-start(bf16[128,2048]{1,0:T(8,128)(2,1)S(1)} %collective-permute-done.1.refs_2_.refs_16_) | copy-start | bytes 1572868
  29.1 12.1 %collective-permute-start.3 = (bf16[256,1024]{1,0:T(8,128)(2,1)S(1)}, bf16[256,1024]{1,0:T(8,128)(2,1)}, u32[]{:S(2)}, u32[]{:S(2)}) collective-permute-start(bf16[256,1024]{1,0:T(8,128)(2,1)S(1)} %fusion.35), channel_id=1, source_target_pairs={{0,4},{4,0},{1,5},{5,1},{2,6},{6,2},{3,7},{7,3},{8,12},{12,8},{9,1... | collective-permute-start | bytes 1572872 | tf_op jit(solution)/shard_map/ppermute | solution.py:30
  29.7 11.8 %collective-permute-start.4 = (bf16[128,2048]{1,0:T(8,128)(2,1)S(1)}, bf16[128,2048]{1,0:T(8,128)(2,1)}, u32[]{:S(2)}, u32[]{:S(2)}) collective-permute-start(bf16[128,2048]{1,0:T(8,128)(2,1)S(1)} %collective-permute-done.1.refs_2_.refs_16_), channel_id=1, source_target_pairs={{0,2},{1,3},{2,0},{3,1},{4,6},{5,7},{6,4},{7,5},{8,10},{9,11},{10,... | collective-permute-start | bytes 1572872 | tf_op jit(solution)/shard_map/ppermute | solution.py:30
  42.5 3.5 copy-start.26
  43.3 2.7 collective-permute-start.5
  47.7 26.6 %copy-start.9 = (bf16[256,2048]{1,0:T(8,128)(2,1)S(1)}, bf16[256,2048]{1,0:T(8,128)(2,1)}, u32[]{:S(2)}) copy-start(bf16[256,2048]{1,0:T(8,128)(2,1)} %fusion.refs_0_) | copy-start | bytes 3145732
  74.3 3.1 copy-start.60
  77.4 78.5 %copy-start.2 = (f32[256,2048]{1,0:T(8,128)}, f32[256,2048]{1,0:T(8,128)S(1)}, u32[]{:S(2)}) copy-start(f32[256,2048]{1,0:T(8,128)S(1)} %get-tuple-element.142.middle) | copy-start | bytes 6291460
  77.4 2.7 copy-start.17
  77.7 3.9 %copy-start.3 = (bf16[256,2048]{1,0:T(8,128)(2,1)}, bf16[256,2048]{1,0:T(8,128)(2,1)S(1)}, u32[]{:S(2)}) copy-start(bf16[256,2048]{1,0:T(8,128)(2,1)S(1)} %multiply_convert_fusion.m_refs_0_.sources_0_.refs_0_) | copy-start | bytes 3145732
  77.7 4.7 %collective-permute-start.6 = (bf16[256,2048]{1,0:T(8,128)(2,1)S(1)}, bf16[256,2048]{1,0:T(8,128)(2,1)S(1)}, u32[]{:S(2)}, u32[]{:S(2)}) collective-permute-start(bf16[256,2048]{1,0:T(8,128)(2,1)S(1)} %multiply_convert_fusion.m_refs_0_.sources_0_.refs_0_), channel_id=1, source_target_pairs={{0,1},{1,0},{2,3},{3,2},{4,5},{5,4},{6,7},{7,6},{8,9},{9,8},{10,11... | collective-permute-start | bytes 3145736 | tf_op jit(solution)/shard_map/ppermute | solution.py:30
  113.5 2.8 copy-start.10
  113.5 2.9 copy-start.27
  113.5 3.7 %collective-permute-start.9 = (bf16[256,2048]{1,0:T(8,128)(2,1)}, bf16[256,2048]{1,0:T(8,128)(2,1)S(1)}, u32[]{:S(2)}, u32[]{:S(2)}) collective-permute-start(bf16[256,2048]{1,0:T(8,128)(2,1)} %get-tuple-element.76), channel_id=1, source_target_pairs={{0,1},{1,0},{2,3},{3,2},{4,5},{5,4},{6,7},{7,6},{8,9},{9,8},{10,11... | collective-permute-start | bytes 3145736 | tf_op jit(solution)/shard_map/ppermute | solution.py:30
  115.8 4.3 %copy-start.7 = (bf16[256,2048]{1,0:T(8,128)(2,1)}, bf16[256,2048]{1,0:T(8,128)(2,1)S(1)}, u32[]{:S(2)}) copy-start(bf16[256,2048]{1,0:T(8,128)(2,1)S(1)} %constant_dynamic-update-slice_fusion.refs_2_.refs_14_) | copy-start | bytes 3145732
  115.8 4.3 %collective-permute-start.8 = (bf16[256,2048]{1,0:T(8,128)(2,1)S(1)}, bf16[256,2048]{1,0:T(8,128)(2,1)S(1)}, u32[]{:S(2)}, u32[]{:S(2)}) collective-permute-start(bf16[256,2048]{1,0:T(8,128)(2,1)S(1)} %constant_dynamic-update-slice_fusion.refs_2_.refs_14_), channel_id=1, source_target_pairs={{0,1},{1,0},{2,3},{3,2},{4,5},{5,4},{6,7},{7,6},{8,9},{9,8},{10,11... | collective-permute-start | bytes 3145736 | tf_op jit(solution)/shard_map/ppermute | solution.py:30
  116.3 3.8 %collective-permute-start.7 = (bf16[256,2048]{1,0:T(8,128)(2,1)S(1)}, bf16[256,2048]{1,0:T(8,128)(2,1)S(1)}, u32[]{:S(2)}, u32[]{:S(2)}) collective-permute-start(bf16[256,2048]{1,0:T(8,128)(2,1)S(1)} %copy-done.10), channel_id=1, source_target_pairs={{0,1},{1,0},{2,3},{3,2},{4,5},{5,4},{6,7},{7,6},{8,9},{9,8},{10,11... | collective-permute-start | bytes 3145736 | tf_op jit(solution)/shard_map/ppermute | solution.py:30
  121.4 31.8 %copy-start.6 = (bf16[256,2048]{1,0:T(8,128)(2,1)S(1)}, bf16[256,2048]{1,0:T(8,128)(2,1)}, u32[]{:S(2)}) copy-start(bf16[256,2048]{1,0:T(8,128)(2,1)} %add_convert_fusion.2.refs_9_) | copy-start | bytes 3145732
  153.2 2.7 copy-start.4
  153.2 2.7 copy-start.23
  155.9 2.3 copy-start.42
  158.2 3.9 %copy-start.15 = (bf16[256,2048]{1,0:T(8,128)(2,1)}, bf16[256,2048]{1,0:T(8,128)(2,1)S(1)}, u32[]{:S(2)}) copy-start(bf16[256,2048]{1,0:T(8,128)(2,1)S(1)} %get-tuple-element.139) | copy-start | bytes 3145732
  158.2 3.8 %collective-permute-start.12 = (bf16[256,2048]{1,0:T(8,128)(2,1)S(1)}, bf16[256,2048]{1,0:T(8,128)(2,1)S(1)}, u32[]{:S(2)}, u32[]{:S(2)}) collective-permute-start(bf16[256,2048]{1,0:T(8,128)(2,1)S(1)} %get-tuple-element.139), channel_id=1, source_target_pairs={{0,1},{1,0},{2,3},{3,2},{4,5},{5,4},{6,7},{7,6},{8,9},{9,8},{10,11... | collective-permute-start | bytes 3145736 | tf_op jit(solution)/shard_map/ppermute | solution.py:30
  158.4 3.6 %copy-start.18 = (bf16[128,2048]{1,0:T(8,128)(2,1)S(1)}, bf16[128,2048]{1,0:T(8,128)(2,1)}, u32[]{:S(2)}) copy-start(bf16[128,2048]{1,0:T(8,128)(2,1)} %get-tuple-element.71.sources_2_.refs_20_) | copy-start | bytes 1572868
  158.4 30.8 %collective-permute-start.10 = (bf16[256,2048]{1,0:T(8,128)(2,1)}, bf16[256,2048]{1,0:T(8,128)(2,1)}, u32[]{:S(2)}, u32[]{:S(2)}) collective-permute-start(bf16[256,2048]{1,0:T(8,128)(2,1)} %get-tuple-element.79), channel_id=1, source_target_pairs={{0,1},{1,0},{2,3},{3,2},{4,5},{5,4},{6,7},{7,6},{8,9},{9,8},{10,11... | collective-permute-start | bytes 3145736 | tf_op jit(solution)/shard_map/ppermute | solution.py:30
  160.0 32.8 %collective-permute-start.17 = (bf16[128,2048]{1,0:T(8,128)(2,1)S(1)}, bf16[128,2048]{1,0:T(8,128)(2,1)}, u32[]{:S(2)}, u32[]{:S(2)}) collective-permute-start(bf16[128,2048]{1,0:T(8,128)(2,1)S(1)} %copy-done.20), channel_id=1, source_target_pairs={{0,1},{1,0},{2,3},{3,2},{4,5},{5,4},{6,7},{7,6},{8,9},{9,8},{10,11... | collective-permute-start | bytes 1572872 | tf_op jit(solution)/shard_map/ppermute | solution.py:30
  160.0 33.2 %collective-permute-start.18 = (bf16[128,2048]{1,0:T(8,128)(2,1)}, bf16[128,2048]{1,0:T(8,128)(2,1)}, u32[]{:S(2)}, u32[]{:S(2)}) collective-permute-start(bf16[128,2048]{1,0:T(8,128)(2,1)} %collective-permute-done.4.refs_18_), channel_id=1, source_target_pairs={{0,1},{1,0},{2,3},{3,2},{4,5},{5,4},{6,7},{7,6},{8,9},{9,8},{10,11... | collective-permute-start | bytes 1572872 | tf_op jit(solution)/shard_map/ppermute | solution.py:30
  160.5 26.4 %collective-permute-start.15 = (bf16[128,2048]{1,0:T(8,128)(2,1)}, bf16[128,2048]{1,0:T(8,128)(2,1)}, u32[]{:S(2)}, u32[]{:S(2)}) collective-permute-start(bf16[128,2048]{1,0:T(8,128)(2,1)} %get-tuple-element.84.refs_8_), channel_id=1, source_target_pairs={{0,2},{1,3},{2,0},{3,1},{4,6},{5,7},{6,4},{7,5},{8,10},{9,11},{10,... | collective-permute-start | bytes 1572872 | tf_op jit(solution)/shard_map/ppermute | solution.py:30
  162.0 31.3 %collective-permute-start.19 = (bf16[128,2048]{1,0:T(8,128)(2,1)S(1)}, bf16[128,2048]{1,0:T(8,128)(2,1)}, u32[]{:S(2)}, u32[]{:S(2)}) collective-permute-start(bf16[128,2048]{1,0:T(8,128)(2,1)S(1)} %copy-done.18), channel_id=1, source_target_pairs={{0,1},{1,0},{2,3},{3,2},{4,5},{5,4},{6,7},{7,6},{8,9},{9,8},{10,11... | collective-permute-start | bytes 1572872 | tf_op jit(solution)/shard_map/ppermute | solution.py:30
  164.2 22.7 %copy-start.13 = (bf16[128,2048]{1,0:T(8,128)(2,1)S(1)}, bf16[128,2048]{1,0:T(8,128)(2,1)}, u32[]{:S(2)}) copy-start(bf16[128,2048]{1,0:T(8,128)(2,1)} %get-tuple-element.77.refs_10_.sources_1_.refs_4_) | copy-start | bytes 1572868
  164.2 24.8 %copy-start.16 = (bf16[256,2048]{1,0:T(8,128)(2,1)S(1)}, bf16[256,2048]{1,0:T(8,128)(2,1)}, u32[]{:S(2)}) copy-start(bf16[256,2048]{1,0:T(8,128)(2,1)} %copy-done.15) | copy-start | bytes 3145732
  186.9 9.6 %collective-permute-start.11 = (bf16[128,2048]{1,0:T(8,128)(2,1)S(1)}, bf16[128,2048]{1,0:T(8,128)(2,1)S(1)}, u32[]{:S(2)}, u32[]{:S(2)}) collective-permute-start(bf16[128,2048]{1,0:T(8,128)(2,1)S(1)} %copy-done.13), channel_id=1, source_target_pairs={{0,1},{1,0},{2,3},{3,2},{4,5},{5,4},{6,7},{7,6},{8,9},{9,8},{10,11... | collective-permute-start | bytes 1572872 | tf_op jit(solution)/shard_map/ppermute | solution.py:30
  189.4 4.3 %collective-permute-start.21 = (bf16[256,1024]{1,0:T(8,128)(2,1)S(1)}, bf16[256,1024]{1,0:T(8,128)(2,1)S(1)}, u32[]{:S(2)}, u32[]{:S(2)}) collective-permute-start(bf16[256,1024]{1,0:T(8,128)(2,1)S(1)} %copy-done.52), channel_id=1, source_target_pairs={{0,1},{1,0},{2,3},{3,2},{4,5},{5,4},{6,7},{7,6},{8,9},{9,8},{10,11... | collective-permute-start | bytes 1572872 | tf_op jit(solution)/shard_map/ppermute | solution.py:30
  190.1 2.7 copy-start.29
  190.1 3.6 copy-start.30
  190.1 3.7 %copy-start.37 = (bf16[512,512]{1,0:T(8,128)(2,1)S(1)}, bf16[512,512]{1,0:T(8,128)(2,1)}, u32[]{:S(2)}) copy-start(bf16[512,512]{1,0:T(8,128)(2,1)} %get-tuple-element.95) | copy-start | bytes 1572868
  192.8 4.1 %collective-permute-start.20 = (bf16[128,2048]{1,0:T(8,128)(2,1)S(1)}, bf16[128,2048]{1,0:T(8,128)(2,1)S(1)}, u32[]{:S(2)}, u32[]{:S(2)}) collective-permute-start(bf16[128,2048]{1,0:T(8,128)(2,1)S(1)} %copy-done.29), channel_id=1, source_target_pairs={{0,1},{1,0},{2,3},{3,2},{4,5},{5,4},{6,7},{7,6},{8,9},{9,8},{10,11... | collective-permute-start | bytes 1572872 | tf_op jit(solution)/shard_map/ppermute | solution.py:30
  193.2 3.7 %collective-permute-start.14 = (bf16[128,2048]{1,0:T(8,128)(2,1)}, bf16[128,2048]{1,0:T(8,128)(2,1)S(1)}, u32[]{:S(2)}, u32[]{:S(2)}) collective-permute-start(bf16[128,2048]{1,0:T(8,128)(2,1)} %get-tuple-element.84.refs_8_), channel_id=1, source_target_pairs={{0,1},{1,0},{2,3},{3,2},{4,5},{5,4},{6,7},{7,6},{8,9},{9,8},{10,11... | collective-permute-start | bytes 1572872 | tf_op jit(solution)/shard_map/ppermute | solution.py:30
  193.3 3.6 %collective-permute-start.16 = (bf16[128,2048]{1,0:T(8,128)(2,1)}, bf16[128,2048]{1,0:T(8,128)(2,1)S(1)}, u32[]{:S(2)}, u32[]{:S(2)}) collective-permute-start(bf16[128,2048]{1,0:T(8,128)(2,1)} %collective-permute-done.15.refs_10_), channel_id=1, source_target_pairs={{0,1},{1,0},{2,3},{3,2},{4,5},{5,4},{6,7},{7,6},{8,9},{9,8},{10,11... | collective-permute-start | bytes 1572872 | tf_op jit(solution)/shard_map/ppermute | solution.py:30
  193.7 3.3 collective-permute-start.13
  195.5 3.1 copy-start.38
  196.5 59.8 %collective-permute-start.23 = (bf16[256,1024]{1,0:T(8,128)(2,1)}, bf16[256,1024]{1,0:T(8,128)(2,1)}, u32[]{:S(2)}, u32[]{:S(2)}) collective-permute-start(bf16[256,1024]{1,0:T(8,128)(2,1)} %collective-permute-done.3), channel_id=1, source_target_pairs={{0,1},{1,0},{2,3},{3,2},{4,5},{5,4},{6,7},{7,6},{8,9},{9,8},{10,11... | collective-permute-start | bytes 1572872 | tf_op jit(solution)/shard_map/ppermute | solution.py:30
  247.1 3.4 copy-start.14
  251.8 11.3 %collective-permute-start.22 = (bf16[256,2048]{1,0:T(8,128)(2,1)S(1)}, bf16[256,2048]{1,0:T(8,128)(2,1)S(1)}, u32[]{:S(2)}, u32[]{:S(2)}) collective-permute-start(bf16[256,2048]{1,0:T(8,128)(2,1)S(1)} %fusion.1), channel_id=1, source_target_pairs={{0,1},{1,0},{2,3},{3,2},{4,5},{5,4},{6,7},{7,6},{8,9},{9,8},{10,11... | collective-permute-start | bytes 3145736 | tf_op jit(solution)/shard_map/ppermute | solution.py:30
  252.9 2.4 copy-start.24
  252.9 2.4 copy-start.54
  252.9 2.4 copy-start.55
  253.7 5.1 %collective-permute-start.24 = (bf16[512,128]{1,0:T(8,128)(2,1)S(1)}, bf16[512,128]{1,0:T(8,128)(2,1)S(1)}, u32[]{:S(2)}, u32[]{:S(2)}) collective-permute-start(bf16[512,128]{1,0:T(8,128)(2,1)S(1)} %pad_maximum_fusion.15), channel_id=1, source_target_pairs={{0,4},{4,0},{1,5},{5,1},{2,6},{6,2},{3,7},{7,3},{8,12},{12,8},{9,1... | collective-permute-start | bytes 393224 | tf_op jit(solution)/shard_map/ppermute | solution.py:30
  255.3 3.5 copy-start.56
  315.3 26.0 %copy-start.49 = (f32[512,640]{1,0:T(8,128)S(1)}, f32[512,640]{1,0:T(8,128)}, u32[]{:S(2)}) copy-start(f32[512,640]{1,0:T(8,128)} %get-tuple-element.103) | copy-start | bytes 3932164
  341.3 4.5 %copy-start.62 = (f32[2,256]{1,0:T(2,128)S(1)}, f32[2,256]{1,0:T(2,128)}, u32[]{:S(2)}) copy-start(f32[2,256]{1,0:T(2,128)} %get-tuple-element.106) | copy-start | bytes 6148
  341.3 5.0 %copy-start.48 = (f32[768,256]{1,0:T(8,128)S(1)}, f32[768,256]{1,0:T(8,128)}, u32[]{:S(2)}) copy-start(f32[768,256]{1,0:T(8,128)} %get-tuple-element.113) | copy-start | bytes 2359300
  343.5 5.2 %copy-start.47 = (f32[256,768]{1,0:T(8,128)S(1)}, f32[256,768]{1,0:T(8,128)}, u32[]{:S(2)}) copy-start(f32[256,768]{1,0:T(8,128)} %get-tuple-element.111) | copy-start | bytes 2359300
  343.5 5.2 %copy-start.51 = (f32[256,640]{1,0:T(8,128)S(1)}, f32[256,640]{1,0:T(8,128)}, u32[]{:S(2)}) copy-start(f32[256,640]{1,0:T(8,128)} %get-tuple-element.112) | copy-start | bytes 1966084
  348.7 3.7 %copy-start.22 = (f32[512,2048]{1,0:T(8,128)S(1)}, f32[512,2048]{1,0:T(8,128)}, u32[]{:S(2)}) copy-start(f32[512,2048]{1,0:T(8,128)} %get-tuple-element.192) | copy-start | bytes 12582916
  352.3 3.7 %copy-start.21 = (f32[512,2048]{1,0:T(8,128)S(1)}, f32[512,2048]{1,0:T(8,128)}, u32[]{:S(2)}) copy-start(f32[512,2048]{1,0:T(8,128)} %get-tuple-element.193) | copy-start | bytes 12582916
  356.0 3.1 copy-start.1
  (24 other events, 40.0 us)
